TPU v7x, 256 devices: a whole 4x4x8 slice. The times are simulated.
256 devices in a mesh: gx: 4 (over x), gy: 8 (over z_hi, core), gz: 8 (over z_lo, y).
Axes of the slice: x: 4, y: 4, z: 8 (z_hi: 4, z_lo: 2; z = z_hi * 2 + z_lo), core: 2. Of those that a mesh axis runs over, the one named last changes fastest.
Arguments:
- velocity: float32 [3, 20971520], P(None, ('gx', 'gy', 'gz')), may hold values from -6 to 6
- particle_place: int32 [20971520], P(('gx', 'gy', 'gz')), may hold values from 0 to 8191
- grid_shift: int32 [3], replicated, may hold values from 1 to 3
- rotation_axis: int32 [256, 128, 128], P('gy', 'gx', 'gz'), may hold values from 0 to 1023
Outputs:
- new_velocity: float32 [3, 20971520], P(None, ('gx', 'gy', 'gz'))
- modes: float32 [2, 3, 128, 256, 128], P(None, None, ('gy', 'gz'), 'gx')
- spectrum: float32 [64], replicated
Inputs may be any that keep to these rules, and one draw needn't show every extreme that they name: `particle_place`: A device's particle slots come in tiles of 640 slots; tile j holds particles of the device's local cells j * 128 to j * 128 + 127, and a value is (cell within the tile) * 4**3 + (sub-cell code).
All inputs are finite; a program needn't handle non-finite values.
Results may differ from a plain program's by a relative error of at most 0.0005.
Values sent between devices are 32-bit elements; how exact they have to be, the bound alone decides.
No kernel may reach another device: no remote copies, remote signals or barrier semaphores. Data moves between devices by JAX's collectives and lax.ppermute only.
A program may use at most 128 MiB of HBM per device.

v0:
```python
import math

import jax
import jax.numpy as jnp
import numpy as np
from jax import lax
from jax.experimental import pallas as pl
from jax.experimental.pallas import tpu as pltpu
from jax.sharding import Mesh
from jax.sharding import PartitionSpec as P

PPC = 5
TILE = 128
SUB = 4
NAXES = 1024
NSHELL = 64
NX, NY, NZ = 128, 256, 128
GX_GY_GZ = ("gx", "gy_0", "gy_1", "gz_0", "gz_1")
GY = ("gy_0", "gy_1")
GZ = ("gz_0", "gz_1")
GY_GZ = ("gy_0", "gy_1", "gz_0", "gz_1")
ROT_COS = math.cos(130.0 * math.pi / 180.0)
ROT_SIN = math.sin(130.0 * math.pi / 180.0)
F32 = jnp.float32
BF16 = jnp.bfloat16
TILES = 128
ROWS = 160
SROW = 36
LROW = 68
BLOCKS = 4
GROUPS = TILES // 8 // BLOCKS


def axis_vectors(axis_index):
    level = 1.0 - (2.0 * axis_index.astype(F32) + 1.0) / NAXES
    radius = jnp.sqrt(1.0 - level * level)
    whole_turns = (axis_index * 1597).astype(F32) * (1.0 / 2584.0)
    turn = (axis_index * 1597 - 2584 * jnp.floor(whole_turns).astype(jnp.int32)).astype(F32)
    turn = turn * (2.0 * math.pi / 2584.0)
    return radius * jnp.cos(turn), radius * jnp.sin(turn), level


def iota(shape, dim):
    return lax.broadcasted_iota(jnp.int32, shape, dim)


def lroll(x, amount):
    amount %= 128
    return pltpu.roll(x, amount, 1) if amount else x


def sroll(x, amount):
    return pltpu.roll(x, amount % x.shape[0], 0)


def split(x):
    high = x.astype(BF16)
    return high, (x - high.astype(F32)).astype(BF16)


def dot(a, b):
    return jnp.dot(a, b, preferred_element_type=F32)


def octants(place, shift_ref):
    bit_x = (((place >> 4) & 3) + shift_ref[0] >= SUB).astype(jnp.int32)
    bit_y = (((place >> 2) & 3) + shift_ref[1] >= SUB).astype(jnp.int32)
    bit_z = ((place & 3) + shift_ref[2] >= SUB).astype(jnp.int32)
    return bit_x * 4 + bit_y * 2 + bit_z


def tile_row(rows, t):
    return jnp.concatenate([rows[PPC * t + r : PPC * t + r + 1, :] for r in range(PPC)], axis=1)


def onehot_of(member, t, cells):
    return jnp.concatenate(
        [
            (cells == member[PPC * t + r : PPC * t + r + 1, :]).astype(F32).astype(BF16)
            for r in range(PPC)
        ],
        axis=1,
    )


def scatter_body(shift_ref, v_ref, p_ref, axis_ref, s_ref, m_ref, n_ref, xlo_ref, xhi_ref, ylo_ref,
                 yhi_ref, zlo_ref, zhi_ref, turn_ref, edge_ref, zed_ref):
    step = pl.program_id(0)
    cells = iota((TILE, TILE), 0)
    upper = iota((8, TILE), 0) < 4

    def group(g, carry):
        place = p_ref[pl.ds(pl.multiple_of(g * 40, 8), 40), :]
        member = place >> 6
        octant = octants(place, shift_ref)
        speed = v_ref[:, pl.ds(pl.multiple_of(g * 5120, 128), 5120)]
        high = speed.astype(BF16).astype(F32)
        low = speed - high
        one = jnp.ones((1, 640), F32)
        zero = jnp.zeros((1, 640), F32)
        for t in range(8):
            here = slice(t * 640, (t + 1) * 640)
            onehot = onehot_of(member, t, cells)
            code = jnp.broadcast_to(tile_row(octant, t), (8, 640))
            values = jnp.concatenate([high[:, here], one, low[:, here], zero], axis=0)
            weighted = jnp.concatenate(
                [jnp.where(code == o, values, 0.0) for o in range(8)], axis=0
            ).astype(BF16)
            sums = lax.dot_general(
                weighted, onehot, (((1,), (1,)), ((), ())), preferred_element_type=F32
            )
            for pair in range(4):
                even = sums[16 * pair : 16 * pair + 8]
                odd = sums[16 * pair + 8 : 16 * pair + 16]
                both = jnp.where(upper, even + sroll(even, 4), odd + sroll(odd, 4))
                turn_ref[SROW * t + 8 * pair : SROW * t + 8 * pair + 8, :] = both
        first = pl.multiple_of((step * GROUPS + g) * 8, 8)
        for r in range(32):
            s_ref[r, pl.ds(first, 8), :] = turn_ref[pl.ds(r, 8, stride=SROW), :]
        return carry

    lax.fori_loop(0, GROUPS, group, 0)

    @pl.when(step == BLOCKS - 1)
    def _():
        for c, part in enumerate(axis_vectors(axis_ref[...])):
            n_ref[c] = part
        lane = iota((TILES, 128), 1)
        row = iota((TILES, 128), 0)
        z = lane & 15
        x_in = lane >> 4
        x_out = row & 3
        last = (x_in == 7) & (x_out == 3)

        def x_shift(plane):
            rolled = lroll(plane, 16)
            return jnp.where(
                x_in > 0, rolled, jnp.where(x_out > 0, sroll(rolled, 1), 0.0)
            )

        for q in range(5):
            for by in range(2):
                parts = []
                for bx in range(2):
                    base = bx * 4 + by * 2
                    if q < 4:
                        above = s_ref[(base + 1) * 4 + q]
                        parts.append(
                            s_ref[base * 4 + q] + jnp.where(z > 0, lroll(above, 1), 0.0)
                        )
                    else:
                        rim = jnp.zeros((TILES, 128), F32)
                        for k in range(4):
                            rim = jnp.where(z == k, lroll(s_ref[(base + 1) * 4 + k], k - 15), rim)
                        parts.append(rim)
                main = parts[0] + x_shift(parts[1])
                edge = jnp.where(last, parts[1], 0.0)
                dst = m_ref if q < 4 else zed_ref
                at = q if q < 4 else 0
                if by == 0:
                    dst[at, 0:TILES, :] = main
                    dst[at, TILES:ROWS, :] = jnp.zeros((ROWS - TILES, 128), F32)
                    edge_ref[q, 0:TILES, :] = edge
                    edge_ref[q, TILES:ROWS, :] = jnp.zeros((ROWS - TILES, 128), F32)
                else:
                    dst[at, 4:132, :] = dst[at, 4:132, :] + main
                    edge_ref[q, 4:132, :] = edge_ref[q, 4:132, :] + edge
        lane40 = iota((40, 128), 1)
        low_face = jnp.zeros((40, 128), F32)
        high_face = jnp.zeros((40, 128), F32)
        for q in range(4):
            inside = (lane40 >> 4) == q
            low_face = jnp.where(inside, lroll(m_ref[q, pl.ds(0, 40, stride=4), :], 16 * q), low_face)
            high_face = jnp.where(
                inside, lroll(edge_ref[q, pl.ds(3, 40, stride=4), :], 16 * q - 112), high_face
            )
        inside = (lane40 >> 2) == 16
        low_face = jnp.where(inside, lroll(zed_ref[0, pl.ds(0, 40, stride=4), :], 64), low_face)
        high_face = jnp.where(inside, lroll(edge_ref[4, pl.ds(3, 40, stride=4), :], 64 - 112), high_face)
        for c in range(3):
            inside = ((lane40 >> 4) == 5 + c) & (iota((40, 128), 0) < 32)
            face = jnp.concatenate(
                [n_ref[c, pl.ds(0, 32, stride=4), :], jnp.zeros((8, 128), F32)], axis=0
            )
            low_face = jnp.where(inside, lroll(face, 80 + 16 * c), low_face)
        xlo_ref[...] = low_face
        xhi_ref[...] = high_face
        ylo_ref[...] = jnp.zeros((40, 128), F32)
        yhi_ref[...] = jnp.zeros((40, 128), F32)
        for q in range(5):
            src = m_ref if q < 4 else zed_ref
            at = q if q < 4 else 0
            ylo_ref[4 * q : 4 * q + 4, :] = src[at, 0:4, :]
            yhi_ref[4 * q : 4 * q + 4, :] = src[at, 128:132, :]
        for c in range(3):
            ylo_ref[20 + 4 * c : 24 + 4 * c, :] = n_ref[c, 0:4, :]
        big = iota((ROWS, 128), 1)
        slot = big & 15
        low_z = jnp.zeros((ROWS, 128), F32)
        for q in range(4):
            low_z = jnp.where(slot == q, lroll(m_ref[q], q), low_z)
        for c in range(3):
            face = jnp.concatenate([n_ref[c], jnp.zeros((ROWS - TILES, 128), F32)], axis=0)
            low_z = jnp.where(slot == 4 + c, lroll(face, 4 + c), low_z)
        zlo_ref[...] = low_z
        zhi_ref[...] = zed_ref[0]


def fold_x_body(xlo_ref, xhi_ref, from_low, from_high, ylo_ref, yhi_ref,
                xlo_out, xhi_out, ylo_out, yhi_out):
    low = xlo_ref[...] + from_low[...]
    high = xhi_ref[...] + from_high[...]
    xlo_out[...] = low
    xhi_out[...] = high
    lane = iota((1, 128), 1)
    for src, dst, y in ((ylo_ref, ylo_out, 0), (yhi_ref, yhi_out, 32)):
        dst[...] = src[...]
        for q in range(4):
            dst[4 * q : 4 * q + 1, :] = jnp.where(
                lane < 16, lroll(low[y : y + 1], -16 * q), src[4 * q : 4 * q + 1, :]
            )
        dst[16:17, :] = jnp.where(lane < 4, lroll(low[y : y + 1], -64), src[16:17, :])
        dst[32:33, :] = high[y : y + 1]


def fold_y_body(ylo_ref, yhi_ref, from_low, from_high, xlo_ref, xhi_ref, zlo_ref, zhi_ref,
                ylo_out, yhi_out, zlo_out, zhi_out):
    low = ylo_ref[...] + from_low[...]
    high = yhi_ref[...] + from_high[...]
    ylo_out[...] = low
    yhi_out[...] = high
    zlo_out[...] = zlo_ref[...]
    zhi_out[...] = zhi_ref[...]
    x_low = xlo_ref[...]
    x_high = xhi_ref[...]
    lane = iota((40, 128), 1)
    lo0 = zlo_out[pl.ds(0, 40, stride=4), :]
    hi0 = zhi_out[pl.ds(0, 40, stride=4), :]
    lo3 = zlo_out[pl.ds(3, 40, stride=4), :]
    hi3 = zhi_out[pl.ds(3, 40, stride=4), :]
    for q in range(4):
        lo0 = jnp.where(lane == q, lroll(x_low, q - 16 * q), lo0)
        lo3 = jnp.where(lane == 120 + q, lroll(x_high, 120 + q - 16 * q), lo3)
    for c in range(3):
        lo3 = jnp.where(lane == 124 + c, lroll(x_high, 124 + c - 80 - 16 * c), lo3)
    hi0 = jnp.where(lane < 4, lroll(x_low, -64), hi0)
    hi3 = jnp.where((lane >= 120) & (lane < 124), lroll(x_high, 120 - 64), hi3)
    zlo_out[pl.ds(0, 40, stride=4), :] = lo0
    zhi_out[pl.ds(0, 40, stride=4), :] = hi0
    zlo_out[pl.ds(3, 40, stride=4), :] = lo3
    zhi_out[pl.ds(3, 40, stride=4), :] = hi3
    lane4 = iota((4, 128), 1)
    slot = lane4 & 15
    corner = (iota((4, 128), 0) == 3) & (lane4 >= 120)
    for face, first in ((low, 0), (high, 128)):
        lo = jnp.zeros((4, 128), F32)
        for q in range(4):
            lo = jnp.where(slot == q, lroll(face[4 * q : 4 * q + 4], q), lo)
        for c in range(3):
            lo = jnp.where(slot == 4 + c, lroll(face[20 + 4 * c : 24 + 4 * c], 4 + c), lo)
        end = face[32:33]
        tail = jnp.zeros((1, 128), F32)
        lane1 = iota((1, 128), 1)
        for q in range(4):
            tail = jnp.where(lane1 == 120 + q, lroll(end, 120 + q - 16 * q), tail)
        for c in range(3):
            tail = jnp.where(lane1 == 124 + c, lroll(end, 124 + c - 80 - 16 * c), tail)
        zlo_out[first : first + 4, :] = jnp.where(corner, tail, lo)
        hi = jnp.where(slot < 4, face[16:20], 0.0)
        zhi_out[first : first + 4, :] = jnp.where(
            corner, jnp.where(lane1 < 124, lroll(end, 120 - 64), 0.0), hi
        )


VROWS = 136


def cell_body(s_ref, m_ref, n_ref, xlo_ref, xhi_ref, ylo_ref, yhi_ref, zlo_ref, zhi_ref,
              from_low, from_high, view_ref, send_ref, ext_ref, end_ref, vel_ref):
    z_low = zlo_ref[0:VROWS, :] + from_low[0:VROWS, :]
    z_high = zhi_ref[0:VROWS, :] + from_high[0:VROWS, :]
    x_low = xlo_ref[...]
    x_high = xhi_ref[...]
    y_low = ylo_ref[...]
    y_high = yhi_ref[...]
    lane40 = iota((40, 128), 1)
    lane = iota((VROWS, 128), 1)
    row = iota((VROWS, 128), 0)
    z = lane & 15
    x_in = lane >> 4
    x_out = row & 3
    for k in range(7):
        if k < 4:
            ext_ref[k] = m_ref[k]
            held = ext_ref[k, pl.ds(0, 40, stride=4), :]
            ext_ref[k, pl.ds(0, 40, stride=4), :] = jnp.where(
                lane40 < 16, lroll(x_low, -16 * k), held
            )
            ext_ref[k, 0:4, :] = y_low[4 * k : 4 * k + 4]
            ext_ref[k, 128:132, :] = y_high[4 * k : 4 * k + 4]
            amount = 112 - 16 * k
        else:
            c = k - 4
            ext_ref[k, 0:TILES, :] = n_ref[c]
            ext_ref[k, 128:132, :] = y_high[20 + 4 * c : 24 + 4 * c]
            amount = 32 - 16 * c
        end_ref[k, pl.ds(3, 40, stride=4), :] = lroll(x_high, amount)
        end_ref[k, 131:132, :] = lroll(y_high[32:33], amount)
        if k < 4:
            end_ref[k, 3:4, :] = lroll(y_low[32:33], amount)

    def pair(k):
        main = ext_ref[k, 0:VROWS, :]
        end = end_ref[k, 0:VROWS, :]
        if k < 4:
            main = jnp.where(z == 0, lroll(z_low, -k), main)
            end = jnp.where(z == 0, lroll(z_low, -8 - k), end)
        main1 = jnp.where(z < 15, lroll(main, -1), lroll(z_high, 15 - k))
        end1 = jnp.where(z < 15, lroll(end, -1), lroll(z_high, 7 - k))
        return (main, main1), (end, end1)

    count_main, count_end = pair(3)
    inv_main = [1.0 / jnp.maximum(a, 1.0) for a in count_main]
    inv_end = [1.0 / jnp.maximum(a, 1.0) for a in count_end]
    for slot, k in enumerate((0, 1, 2, 4, 5, 6)):
        mains, ends = pair(k)
        for bz in range(2):
            main, end = mains[bz], ends[bz]
            if k < 3:
                main = main * inv_main[bz]
                end = end * inv_end[bz]
            rolled = lroll(main, -16)
            ahead = jnp.where(x_in < 7, rolled, jnp.where(x_out == 3, end, sroll(rolled, -1)))
            view_ref[bz * 6 + slot] = main
            view_ref[(2 + bz) * 6 + slot] = ahead

    def group(g, carry):
        first = pl.multiple_of(g * 8, 8)
        acc = [jnp.zeros((8, 128), F32) for _ in range(3)]
        total = jnp.zeros((8, 128), F32)
        for bx in range(2):
            for bz in range(2):
                wide = [view_ref[(bx * 2 + bz) * 6 + k, pl.ds(first, 16), :] for k in range(6)]
                for by in range(2):
                    o = bx * 4 + by * 2 + bz
                    ux, uy, uz, nx, ny, nz = [w[4 * by : 4 * by + 8] for w in wide]
                    sx, sy, sz, num = [s_ref[o * 4 + q, pl.ds(first, 8), :] for q in range(4)]
                    mx, my, mz = num * ux, num * uy, num * uz
                    wx, wy, wz = sx - mx, sy - my, sz - mz
                    along = (1.0 - ROT_COS) * (nx * wx + ny * wy + nz * wz)
                    acc[0] += mx + ROT_COS * wx + ROT_SIN * (ny * wz - nz * wy) + along * nx
                    acc[1] += my + ROT_COS * wy + ROT_SIN * (nz * wx - nx * wz) + along * ny
                    acc[2] += mz + ROT_COS * wz + ROT_SIN * (nx * wy - ny * wx) + along * nz
                    total += num
        inverse = 1.0 / jnp.maximum(total, 1.0)
        for c in range(3):
            vel_ref[c, pl.ds(first, 8), :] = acc[c] * inverse
        return carry

    lax.fori_loop(0, TILES // 8, group, 0)
    lane = iota((TILES, 128), 1)
    row = iota((TILES, 128), 0)
    for c in range(3):
        plane = vel_ref[c]
        for bit in range(4):
            size = 1 << bit
            row_bit = (row >> bit) & 1
            lane_bit = (lane >> bit) & 1
            down = sroll(lroll(plane, size), -size)
            up = sroll(lroll(plane, -size), size)
            plane = jnp.where(row_bit == lane_bit, plane, jnp.where(row_bit == 0, down, up))
        for part in range(8):
            send_ref[part, 16 * c : 16 * c + 16, :] = plane[16 * part : 16 * part + 16]


def collide_body(shift_ref, v_ref, p_ref, view_ref, out_ref, turn_ref):
    step = pl.program_id(0)
    cells = iota((TILE, TILE), 0)

    @pl.when(step == 0)
    def _():
        turn_ref[...] = jnp.zeros(turn_ref.shape, F32)

    def group(g, carry):
        place = p_ref[pl.ds(pl.multiple_of(g * 40, 8), 40), :]
        member = place >> 6
        octant = octants(place, shift_ref)
        first = pl.multiple_of((step * GROUPS + g) * 8, 8)
        for bx in range(2):
            for bz in range(2):
                for k in range(6):
                    wide = view_ref[(bx * 2 + bz) * 6 + k, pl.ds(first, 16), :]
                    for by in range(2):
                        o = bx * 4 + by * 2 + bz
                        turn_ref[pl.ds(8 * o + k, 8, stride=LROW), :] = wide[4 * by : 4 * by + 8]
        for t in range(8):
            high, low = split(turn_ref[LROW * t : LROW * t + 64, :])
            onehot = onehot_of(member, t, cells)
            picked = dot(
                jnp.concatenate([high, low], axis=1), jnp.concatenate([onehot, onehot], axis=0)
            )
            code = jnp.broadcast_to(tile_row(octant, t), (8, 640))
            chosen = picked[0:8]
            for o in range(1, 8):
                chosen = jnp.where(code == o, picked[8 * o : 8 * o + 8], chosen)
            speed = v_ref[:, pl.ds(pl.multiple_of(g * 5120 + t * 640, 128), 640)]
            ux, uy, uz, nx, ny, nz = [chosen[k : k + 1] for k in range(6)]
            wx, wy, wz = speed[0:1] - ux, speed[1:2] - uy, speed[2:3] - uz
            along = (1.0 - ROT_COS) * (nx * wx + ny * wy + nz * wz)
            new = [
                ux + ROT_COS * wx + ROT_SIN * (ny * wz - nz * wy) + along * nx,
                uy + ROT_COS * wy + ROT_SIN * (nz * wx - nx * wz) + along * ny,
                uz + ROT_COS * wz + ROT_SIN * (nx * wy - ny * wx) + along * nz,
            ]
            out_ref[:, pl.ds(pl.multiple_of(g * 5120 + t * 640, 128), 640)] = jnp.concatenate(
                new, axis=0
            )
        return carry

    lax.fori_loop(0, GROUPS, group, 0)


def table_parts(table):
    table = np.asarray(table, np.float32)
    high = table.astype(BF16)
    low = (table - high.astype(np.float32)).astype(BF16)
    return high, low


def z_tables():
    kz_high = np.arange(64)[:, None]
    pos = np.arange(NZ)[None, :]
    rows = []
    for q in range(4):
        phase = (2 * kz_high + q // 2) * pos % NZ * (2.0 * np.pi / NZ)
        rows.append(-np.sin(phase) if q % 2 else np.cos(phase))
    return table_parts(np.concatenate(rows, axis=0))


def y_tables():
    phase = np.arange(NY)[:, None] * np.arange(NY)[None, :] % NY * (2.0 * np.pi / NY)
    return table_parts(np.concatenate([np.cos(phase), np.sin(phase)], axis=0))


def x_tables():
    k = np.arange(512)
    lane = k % 128
    x = k // 128 * 32 + (lane & 3) * 8 + lane // 16
    kz = (lane >> 3) & 1
    part = (lane >> 2) & 1
    n = np.arange(512)
    part_out, kz_out, kx = n // 256, n // 128 % 2, n % 128
    phase = x[:, None] * kx[None, :] % NX * (2.0 * np.pi / NX)
    same = kz[:, None] == kz_out[None, :]
    c, s = np.cos(phase), np.sin(phase)
    real = np.where(part[:, None] == 0, c, s)
    imag = np.where(part[:, None] == 0, -s, c)
    table = np.where(part_out[None, :] == 0, real, imag) * same / math.sqrt(NX * NY * NZ)
    return table_parts(table)


def shell_counts():
    def wave(n):
        k = np.arange(n)
        return np.where(k >= n // 2, k - n, k)

    square = wave(NZ)[:, None, None] ** 2 + wave(NY)[None, :, None] ** 2 + wave(NX)[None, None, :] ** 2
    edges = np.arange(NSHELL + 1) ** 2
    below = np.searchsorted(np.sort(square.reshape(-1)), edges, side="left")
    return np.diff(below).astype(np.float32)


def z_body(in_ref, fh_ref, fl_ref, out_ref):
    lane = iota((64, 128), 1)
    fh, fl = fh_ref[...], fl_ref[...]
    for c in range(3):
        data = in_ref[:, 16 * c : 16 * c + 16, :].reshape(128, 128)
        high, low = split(data)
        res = dot(fh, high) + dot(fh, low) + dot(fl, high)
        g = [res[64 * q : 64 * q + 64] for q in range(4)]
        for bit, size in ((2, 8), (1, 4)):
            clear = (lane & size) == 0
            new = list(g)
            for q in range(4):
                if not q & bit:
                    a, b = g[q], g[q | bit]
                    new[q] = jnp.where(clear, a, lroll(b, size))
                    new[q | bit] = jnp.where(clear, lroll(a, -size), b)
            g = new
        for r in range(4):
            out_ref[pl.ds(4 * c + r, 64, stride=12), :] = g[r]


def y_body(in_ref, fh_ref, fl_ref, out_ref):
    both = in_ref[...].reshape(32, 24, 128)
    v0, v1, v2 = both[:, 0:8], both[:, 8:16], both[:, 16:24]
    upper = iota((32, 8, 128), 1) < 4
    d0 = jnp.where(upper, v0, v1)
    d1 = pltpu.roll(jnp.where(upper, v2, v0), 4, 1)
    d2 = jnp.where(upper, v1, v2)
    data = jnp.concatenate([d.reshape(256, 128) for d in (d0, d1, d2)], axis=1)
    high, low = split(data)
    fh, fl = fh_ref[...], fl_ref[...]
    res = dot(fh, high) + dot(fh, low) + dot(fl, high)
    is_real = (iota((256, 128), 1) & 4) == 0
    for c in range(3):
        even = res[0:256, 128 * c : 128 * c + 128]
        odd = res[256:512, 128 * c : 128 * c + 128]
        out = even + jnp.where(is_real, lroll(odd, -4), -lroll(odd, 4))
        for d in range(4):
            out_ref[d, 64 * c : 64 * c + 64, :] = out[64 * d : 64 * d + 64]


def x_body(first_ref, in_ref, fh_ref, fl_ref, out_ref, shell_ref, sums_ref):
    data = jnp.concatenate([in_ref[s] for s in range(4)], axis=1)
    high, low = split(data)
    fh, fl = fh_ref[...], fl_ref[...]
    res = dot(high, fh) + dot(low, fh) + dot(high, fl)
    ky = first_ref[1] + iota((64, 128), 0)
    ky = jnp.where(ky >= NY // 2, ky - NY, ky)
    kx = iota((64, 128), 1)
    kx = jnp.where(kx >= NX // 2, kx - NX, kx)
    plane = ky * ky + kx * kx
    energy, square = [], []
    for kz in range(2):
        total = jnp.zeros((64, 128), F32)
        for part in range(2):
            for c in range(3):
                block = res[64 * c : 64 * c + 64, 256 * part + 128 * kz : 256 * part + 128 * kz + 128]
                out_ref[part, c, kz] = block
                total += block * block
        wave = first_ref[0] + kz
        wave = jnp.where(wave >= NZ // 2, wave - NZ, wave)
        energy.append(total)
        square.append(plane + wave * wave)
    energy = jnp.concatenate(energy, axis=0)
    square = jnp.concatenate(square, axis=0)
    for s in range(NSHELL):
        kept = jnp.where(square < (s + 1) * (s + 1), energy, 0.0)
        sums_ref[s : s + 1, :] = jnp.sum(kept, axis=0, keepdims=True)
    cumulative = sums_ref[...]
    before = jnp.where(iota((NSHELL, 128), 0) == 0, 0.0, sroll(cumulative, 1))
    own = jnp.concatenate([cumulative - before, jnp.zeros((64, 128), F32)], axis=0)
    shell_ref[...] = jnp.sum(own.T, axis=0, keepdims=True)


def struct(*shape):
    return jax.ShapeDtypeStruct(shape, F32)


SMEM = pl.BlockSpec(memory_space=pltpu.SMEM)


def ring(x, axis):
    count = lax.axis_size(axis)
    forward = [(i, (i + 1) % count) for i in range(count)]
    backward = [(target, source) for source, target in forward]
    low, high = x
    return lax.ppermute(high, axis, forward), lax.ppermute(low, axis, backward)


def gathered_sum(x, axes):
    count = lax.axis_size(axes)
    copies = jnp.broadcast_to(x[None], (count, *x.shape))
    return jnp.sum(lax.all_to_all(copies, axes, split_axis=0, concat_axis=0, tiled=True), axis=0)


def params(mib):
    return pltpu.CompilerParams(vmem_limit_bytes=mib * 1024 * 1024)


def whole(*shape):
    return pl.BlockSpec(shape, lambda i: (0,) * len(shape))


def per_device(velocity, particle_place, grid_shift, rotation_axis):
    place = particle_place.reshape(640, 128)
    axis_index = rotation_axis.reshape(TILES, 128)
    span = TILES * TILE * PPC // BLOCKS
    speed_spec = pl.BlockSpec((3, span), lambda i: (0, i))
    place_spec = pl.BlockSpec((640 // BLOCKS, 128), lambda i: (i, 0))
    out_shapes = [(32, TILES, 128), (4, ROWS, 128), (3, TILES, 128)]
    out_shapes += [(40, 128)] * 4 + [(ROWS, 128)] * 2
    sums, main, normal, x_lo, x_hi, y_lo, y_hi, z_lo, z_hi = pl.pallas_call(
        scatter_body,
        name="scatter",
        grid=(BLOCKS,),
        in_specs=[SMEM, speed_spec, place_spec, whole(TILES, 128)],
        out_specs=[whole(*s) for s in out_shapes],
        out_shape=[struct(*s) for s in out_shapes],
        scratch_shapes=[
            pltpu.VMEM((8 * SROW, 128), F32),
            pltpu.VMEM((5, ROWS, 128), F32),
            pltpu.VMEM((1, ROWS, 128), F32),
        ],
        compiler_params=params(12),
    )(grid_shift, velocity, place, axis_index)
    below, above = ring((x_lo, x_hi), "gx")
    x_lo, x_hi, y_lo, y_hi = pl.pallas_call(
        fold_x_body, name="fold_x", out_shape=[struct(40, 128)] * 4, compiler_params=params(2)
    )(x_lo, x_hi, below, above, y_lo, y_hi)
    below, above = ring((y_lo, y_hi), GY)
    y_lo, y_hi, z_lo, z_hi = pl.pallas_call(
        fold_y_body, name="fold_y", out_shape=[struct(40, 128)] * 2 + [struct(ROWS, 128)] * 2,
        compiler_params=params(3),
    )(y_lo, y_hi, below, above, x_lo, x_hi, z_lo, z_hi)
    below, above = ring((z_lo, z_hi), GZ)
    views, sent = pl.pallas_call(
        cell_body,
        name="cells",
        out_shape=[struct(24, VROWS, 128), struct(8, 48, 128)],
        scratch_shapes=[
            pltpu.VMEM((7, ROWS, 128), F32),
            pltpu.VMEM((7, ROWS, 128), F32),
            pltpu.VMEM((3, TILES, 128), F32),
        ],
        compiler_params=params(12),
    )(sums, main, normal, x_lo, x_hi, y_lo, y_hi, z_lo, z_hi, below, above)
    arrived = lax.all_to_all(sent, GZ, split_axis=0, concat_axis=0, tiled=True)
    lines = pl.pallas_call(z_body, name="z_lines", out_shape=struct(768, 128), compiler_params=params(12))(
        arrived, *z_tables()
    )
    new_velocity = pl.pallas_call(
        collide_body,
        name="collide",
        grid=(BLOCKS,),
        in_specs=[SMEM, speed_spec, place_spec, whole(24, VROWS, 128)],
        out_specs=speed_spec,
        out_shape=struct(*velocity.shape),
        scratch_shapes=[pltpu.VMEM((8 * LROW, 128), F32)],
        compiler_params=params(12),
        cost_estimate=pl.CostEstimate(flops=6_000_000_000, bytes_accessed=4_000_000, transcendentals=0),
    )(grid_shift, velocity, place, views)
    pencil = lax.all_to_all(lines.reshape(64, 12, 128), GY_GZ, split_axis=0, concat_axis=0, tiled=True)
    pencil, new_velocity = lax.optimization_barrier((pencil, new_velocity))
    rows = pl.pallas_call(y_body, name="y_lines", out_shape=struct(4, 192, 128), compiler_params=params(12))(
        pencil.reshape(768, 128), *y_tables()
    )
    columns = lax.all_to_all(rows, "gx", split_axis=0, concat_axis=0, tiled=True)
    first = jnp.stack([lax.axis_index(GY_GZ) * 2, lax.axis_index("gx") * 64]).astype(jnp.int32)
    modes, shells = pl.pallas_call(
        x_body,
        name="x_lines",
        in_specs=[SMEM] + [pl.BlockSpec(memory_space=pltpu.VMEM)] * 3,
        out_shape=[struct(2, 3, 2, 64, 128), struct(1, 128)],
        scratch_shapes=[pltpu.VMEM((NSHELL, 128), F32)],
        compiler_params=params(12),
    )(first, columns, *x_tables())
    total = gathered_sum(gathered_sum(shells, GY_GZ), "gx")
    spectrum = total[0, :NSHELL] / shell_counts()
    return new_velocity, modes, spectrum


def solution(mesh):
    torus = Mesh(
        mesh.devices.reshape(mesh.shape["gx"], 4, 2, 2, 4), ("gx", "gy_0", "gy_1", "gz_0", "gz_1")
    )
    in_specs = (P(None, GX_GY_GZ), P(GX_GY_GZ), P(), P(GY, "gx", GZ))
    out_specs = (P(None, GX_GY_GZ), P(None, None, GY_GZ, "gx", None), P())
    return jax.shard_map(
        per_device, mesh=torus, in_specs=in_specs, out_specs=out_specs, check_vma=False
    )
```

profile of v0, /device:TPU:1, one launch (start us, length us, event | category | flops | bytes accessed | tf_op | source)
XLA Modules:
  0.0 122.8 jit_solution(9615104558585807155)
XLA Ops:
  0.6 1.3 %copy.17 = s32[32,32,16]{2,1,0:T(8,128)S(1)} copy(s32[32,32,16]{1,2,0:T(8,128)} %param.14) | data formatting | bytes 131072 | tf_op args[3]
  1.9 0.2 reshape.28.axis_ref
  2.1 1.0 copy-done.3
  3.1 0.7 copy-done.9
  3.8 13.2 %scatter.1 = (f32[32,128,128]{2,1,0:T(8,128)S(1)}, f32[4,160,128]{2,1,0:T(8,128)S(1)}, f32[3,128,128]{2,1,0:T(8,128)S(1)}, f32[40,128]{1,0:T(8,128)S(1)}, f32[40...) custom-call(s32[3]{0:T(128)S(1)} %copy-done.9, ...), custom_call_target="tpu_custom_call" | custom-call | tf_op jit(solution)/shard_map/scatter/pallas_call | solution.py:584
  17.0 2.1 %collective-permute-start = (f32[40,128]{1,0:T(8,128)S(1)}, f32[40,128]{1,0:T(8,128)S(1)}, u32[]{:S(2)}, u32[]{:S(2)}) collective-permute-start(f32[40,128]{1,0:T(8,128)S(1)} %get-tuple-element.30.xhi_ref), channel_id=1, source_target_pairs={{0,64},{64,128},{128,192},{192,0},{1,65},{65,129},{129,193},{193,1... | collective-permute-start | bytes 61448 | tf_op jit(solution)/shard_map/ppermute | solution.py:559
  19.1 1.4 %collective-permute-start.1 = (f32[40,128]{1,0:T(8,128)S(1)}, f32[40,128]{1,0:T(8,128)S(1)}, u32[]{:S(2)}, u32[]{:S(2)}) collective-permute-start(f32[40,128]{1,0:T(8,128)S(1)} %get-tuple-element.29.xlo_ref), channel_id=1, source_target_pairs={{64,0},{128,64},{192,128},{0,192},{65,1},{129,65},{193,129},{1,193... | collective-permute-start | bytes 61448 | tf_op jit(solution)/shard_map/ppermute | solution.py:559
  20.4 1.1 collective-permute-done.from_low
  21.5 0.2 collective-permute-done.1.from_high
  21.8 5.0 %collective-permute-start.2 = (f32[40,128]{1,0:T(8,128)S(1)}, f32[40,128]{1,0:T(8,128)S(1)}, u32[]{:S(2)}, u32[]{:S(2)}) collective-permute-start(f32[40,128]{1,0:T(8,128)S(1)} %get-tuple-element.36.yhi_ref), channel_id=1, source_target_pairs={{0,8},{8,16},{16,24},{24,32},{32,40},{40,48},{48,56},{56,0},{1,9},... | collective-permute-start | bytes 61448 | tf_op jit(solution)/shard_map/ppermute | solution.py:559
  26.8 0.9 collective-permute-done.2.from_low
  27.7 3.3 %collective-permute-done.3.from_high = f32[40,128]{1,0:T(8,128)S(1)} collective-permute-done((f32[40,128]{1,0:T(8,128)S(1)}, f32[40,128]{1,0:T(8,128)S(1)}, u32[]{:S(2)}, u32[]{:S(2)}) %collective-permute-start.3) | collective-permute-done | bytes 20512 | tf_op jit(solution)/shard_map/ppermute | solution.py:559
  31.0 0.2 fold_y.1
  31.1 1.4 %collective-permute-start.4 = (f32[160,128]{1,0:T(8,128)S(1)}, f32[160,128]{1,0:T(8,128)S(1)}, u32[]{:S(2)}, u32[]{:S(2)}) collective-permute-start(f32[160,128]{1,0:T(8,128)S(1)} %get-tuple-element.42.zhi_ref), channel_id=1, source_target_pairs={{0,1},{1,2},{2,3},{3,4},{4,5},{5,6},{6,7},{7,0},{8,9},{9,10},{10,1... | collective-permute-start | bytes 245768 | tf_op jit(solution)/shard_map/ppermute | solution.py:559
  32.5 2.8 %collective-permute-start.5 = (f32[160,128]{1,0:T(8,128)S(1)}, f32[160,128]{1,0:T(8,128)S(1)}, u32[]{:S(2)}, u32[]{:S(2)}) collective-permute-start(f32[160,128]{1,0:T(8,128)S(1)} %get-tuple-element.41.zlo_ref), channel_id=1, source_target_pairs={{1,0},{2,1},{3,2},{4,3},{5,4},{6,5},{7,6},{0,7},{9,8},{10,9},{11,1... | collective-permute-start | bytes 245768 | tf_op jit(solution)/shard_map/ppermute | solution.py:559
  35.3 2.4 %collective-permute-done.4.from_low = f32[160,128]{1,0:T(8,128)S(1)} collective-permute-done((f32[160,128]{1,0:T(8,128)S(1)}, f32[160,128]{1,0:T(8,128)S(1)}, u32[]{:S(2)}, u32[]{:S(2)}) %collective-permute-start.4) | collective-permute-done | bytes 81952 | tf_op jit(solution)/shard_map/ppermute | solution.py:559
  37.7 3.4 %cells.1 = (f32[24,136,128]{2,1,0:T(8,128)S(1)}, f32[8,48,128]{2,1,0:T(8,128)S(1)}) custom-call(f32[32,128,128]{2,1,0:T(8,128)S(1)} %get-tuple-element.26.s_ref, f32[4,160,128]{2,1,0:T(8,128)S(1)} %get-tuple-element.27.m_ref, f32[3,128,128]{2,1,0:T(8,128)S(1)} %get-tuple-element.28.n_ref, f32[40,128]{1,0:T(8,128)S(1)} %get-tuple-element.33.xlo_ref, ...), custom_call_target="tpu_custom_call" | custom-call | tf_op jit(solution)/shard_map/cells/pallas_call | solution.py:608
  41.1 1.2 copy-done.11
  42.3 11.2 %all_to_all.25.in_ref = f32[8,48,128]{2,1,0:T(8,128)S(1)} all-to-all(f32[8,48,128]{2,1,0:T(8,128)S(1)} %get-tuple-element.43), channel_id=1, replica_groups=mesh['gx'=4,'gy_0'=4,'gy_1'=2,'gz_0'=2,'gz_1'=4] {'gz_0','gz_1'}, dimensions={0} | all-to-all | bytes 393216 | tf_op jit(solution)/shard_map/all_to_all | solution.py:619
  53.5 0.5 z_lines.1
  54.0 0.8 reshape.29
  54.8 8.9 %all-to-all-start.1 = ((f32[64,12,128]{2,1,0:T(8,128)}), f32[64,12,128]{2,1,0:T(8,128)S(1)}, u32[]{:S(2)}, u32[]{:S(2)}) async-start(f32[64,12,128]{2,1,0:T(8,128)} %reshape.29), calls=%async_computation.1 | async-start | bytes 1048576 | tf_op jit(solution)/shard_map/all_to_all | solution.py:634
  63.7 1.4 %copy-done.12 = f32[24,136,128]{2,1,0:T(8,128)S(1)} copy-done((f32[24,136,128]{2,1,0:T(8,128)S(1)}, f32[24,136,128]{2,1,0:T(8,128)}, u32[]{:S(2)}) %copy-start.12) | copy-done | bytes 1671192
  65.1 15.2 %collide.1 = f32[3,81920]{1,0:T(4,128)} custom-call(s32[3]{0:T(128)S(1)} %copy-done.10, f32[3,81920]{1,0:T(4,128)S(1)} %copy-done, s32[640,128]{1,0:T(8,128)S(1)} %bitcast.10, f32[24,136,128]{2,1,0:T(8,128)S(1)} %copy-done.12), custom_call_target="tpu_custom_call" | custom-call | flops 6000000000 | bytes 4000000 | tf_op jit(solution)/shard_map/collide/pallas_call | solution.py:623
  80.4 0.7 all-to-all-done.1
  81.1 1.6 %y_lines.1 = f32[4,192,128]{2,1,0:T(8,128)} custom-call(f32[768,128]{1,0:T(8,128)S(1)} %reshape.30.in_ref, bf16[512,256]{1,0:T(8,128)(2,1)S(1)} %copy-done.5, bf16[512,256]{1,0:T(8,128)(2,1)S(1)} %copy-done.6), custom_call_target="tpu_custom_call" | custom-call | tf_op jit(solution)/shard_map/y_lines/pallas_call | solution.py:636
  82.7 4.0 %all-to-all-start.2 = ((f32[4,192,128]{2,1,0:T(8,128)}), f32[4,192,128]{2,1,0:T(8,128)S(1)}, u32[]{:S(2)}, u32[]{:S(2)}) async-start(f32[4,192,128]{2,1,0:T(8,128)} %y_lines.1), calls=%async_computation.2 | async-start | bytes 786432 | tf_op jit(solution)/shard_map/all_to_all | solution.py:639
  86.7 6.3 %all-to-all-done.2.in_ref = f32[4,192,128]{2,1,0:T(8,128)S(1)} async-done(((f32[4,192,128]{2,1,0:T(8,128)}), f32[4,192,128]{2,1,0:T(8,128)S(1)}, u32[]{:S(2)}, u32[]{:S(2)}) %all-to-all-start.2) | async-done | bytes 393248 | tf_op jit(solution)/shard_map/all_to_all | solution.py:639
  93.0 1.8 %x_lines.1 = (f32[2,3,2,64,128]{4,3,2,1,0:T(8,128)}, f32[1,128]{1,0:T(1,128)S(1)}) custom-call(s32[2]{0:T(128)S(1)} %pad_add_fusion.first_ref, f32[4,192,128]{2,1,0:T(8,128)S(1)} %all-to-all-done.2.in_ref, bf16[512,512]{1,0:T(8,128)(2,1)S(1)} %copy-done.1, bf16[512,512]{1,0:T(8,128)(2,1)S(1)} %copy-done.2), custom_call_target="tpu_custom_call" | custom-call | tf_op jit(solution)/shard_map/x_lines/pallas_call | solution.py:641
  94.8 20.9 %all_to_all.26 = f32[64,1,128]{2,1,0:T(1,128)S(1)} all-to-all(f32[64,1,128]{2,1,0:T(1,128)S(1)} %broadcast_in_dim.7), channel_id=1, replica_groups=mesh['gx'=4,'gy_0'=4,'gy_1'=2,'gz_0'=2,'gz_1'=4] {'gy_0','gy_1','gz_0','..., dimensions={0} | all-to-all | bytes 65536 | tf_op jit(solution)/shard_map/all_to_all | solution.py:565
  115.8 6.5 %all_to_all.27 = f32[4,1,128]{2,1,0:T(1,128)S(1)} all-to-all(f32[4,1,128]{2,1,0:T(1,128)S(1)} %broadcast_in_dim.16), channel_id=1, replica_groups=mesh['gx'=4,'gy_0'=4,'gy_1'=2,'gz_0'=2,'gz_1'=4] {'gx'}, dimensions={0} | all-to-all | bytes 4096 | tf_op jit(solution)/shard_map/all_to_all | solution.py:565
  122.3 0.5 multiply_bitcast_fusion
  (33 shorter events, 0.3 us)
Async XLA Ops:
  0.6 1.5 %copy-start = (f32[3,81920]{1,0:T(4,128)S(1)}, f32[3,81920]{1,0:T(4,128)}, u32[]{:S(2)}) copy-start(f32[3,81920]{1,0:T(4,128)} %v_ref.3) | copy-start | bytes 2949124
  2.1 1.0 copy-start.3
  3.1 0.7 copy-start.9
  17.0 4.5 %collective-permute-start = (f32[40,128]{1,0:T(8,128)S(1)}, f32[40,128]{1,0:T(8,128)S(1)}, u32[]{:S(2)}, u32[]{:S(2)}) collective-permute-start(f32[40,128]{1,0:T(8,128)S(1)} %get-tuple-element.30.xhi_ref), channel_id=1, source_target_pairs={{0,64},{64,128},{128,192},{192,0},{1,65},{65,129},{129,193},{193,1... | collective-permute-start | bytes 61448 | tf_op jit(solution)/shard_map/ppermute | solution.py:559
  19.1 2.6 %collective-permute-start.1 = (f32[40,128]{1,0:T(8,128)S(1)}, f32[40,128]{1,0:T(8,128)S(1)}, u32[]{:S(2)}, u32[]{:S(2)}) collective-permute-start(f32[40,128]{1,0:T(8,128)S(1)} %get-tuple-element.29.xlo_ref), channel_id=1, source_target_pairs={{64,0},{128,64},{192,128},{0,192},{65,1},{129,65},{193,129},{1,193... | collective-permute-start | bytes 61448 | tf_op jit(solution)/shard_map/ppermute | solution.py:559
  21.8 5.9 %collective-permute-start.2 = (f32[40,128]{1,0:T(8,128)S(1)}, f32[40,128]{1,0:T(8,128)S(1)}, u32[]{:S(2)}, u32[]{:S(2)}) collective-permute-start(f32[40,128]{1,0:T(8,128)S(1)} %get-tuple-element.36.yhi_ref), channel_id=1, source_target_pairs={{0,8},{8,16},{16,24},{24,32},{32,40},{40,48},{48,56},{56,0},{1,9},... | collective-permute-start | bytes 61448 | tf_op jit(solution)/shard_map/ppermute | solution.py:559
  26.8 4.2 %collective-permute-start.3 = (f32[40,128]{1,0:T(8,128)S(1)}, f32[40,128]{1,0:T(8,128)S(1)}, u32[]{:S(2)}, u32[]{:S(2)}) collective-permute-start(f32[40,128]{1,0:T(8,128)S(1)} %get-tuple-element.35.ylo_ref), channel_id=1, source_target_pairs={{8,0},{16,8},{24,16},{32,24},{40,32},{48,40},{56,48},{0,56},{9,1},... | collective-permute-start | bytes 61448 | tf_op jit(solution)/shard_map/ppermute | solution.py:559
  31.1 6.6 %collective-permute-start.4 = (f32[160,128]{1,0:T(8,128)S(1)}, f32[160,128]{1,0:T(8,128)S(1)}, u32[]{:S(2)}, u32[]{:S(2)}) collective-permute-start(f32[160,128]{1,0:T(8,128)S(1)} %get-tuple-element.42.zhi_ref), channel_id=1, source_target_pairs={{0,1},{1,2},{2,3},{3,4},{4,5},{5,6},{6,7},{7,0},{8,9},{9,10},{10,1... | collective-permute-start | bytes 245768 | tf_op jit(solution)/shard_map/ppermute | solution.py:559
  32.5 5.2 %collective-permute-start.5 = (f32[160,128]{1,0:T(8,128)S(1)}, f32[160,128]{1,0:T(8,128)S(1)}, u32[]{:S(2)}, u32[]{:S(2)}) collective-permute-start(f32[160,128]{1,0:T(8,128)S(1)} %get-tuple-element.41.zlo_ref), channel_id=1, source_target_pairs={{1,0},{2,1},{3,2},{4,3},{5,4},{6,5},{7,6},{0,7},{9,8},{10,9},{11,1... | collective-permute-start | bytes 245768 | tf_op jit(solution)/shard_map/ppermute | solution.py:559
  37.7 15.8 %copy-start.7 = (bf16[256,128]{1,0:T(8,128)(2,1)S(1)}, bf16[256,128]{1,0:T(8,128)(2,1)}, u32[]{:S(2)}) copy-start(bf16[256,128]{1,0:T(8,128)(2,1)} %constant.46.clone.fh_ref) | copy-start | bytes 196612
  37.7 15.8 %copy-start.8 = (bf16[256,128]{1,0:T(8,128)(2,1)S(1)}, bf16[256,128]{1,0:T(8,128)(2,1)}, u32[]{:S(2)}) copy-start(bf16[256,128]{1,0:T(8,128)(2,1)} %constant.47.clone.fl_ref) | copy-start | bytes 196612
  41.1 1.2 copy-start.11
  42.3 21.3 %copy-start.4 = (s32[81920]{0:T(1024)S(1)}, s32[81920]{0:T(1024)}, u32[]{:S(2)}) copy-start(s32[81920]{0:T(1024)} %param.12) | copy-start | bytes 983044
  42.3 21.3 %copy-start.10 = (s32[3]{0:T(128)S(1)}, s32[3]{0:T(128)}, u32[]{:S(2)}) copy-start(s32[3]{0:T(128)} %shift_ref.3) | copy-start | bytes 40
  54.8 26.2 %all-to-all-start.1 = ((f32[64,12,128]{2,1,0:T(8,128)}), f32[64,12,128]{2,1,0:T(8,128)S(1)}, u32[]{:S(2)}, u32[]{:S(2)}) async-start(f32[64,12,128]{2,1,0:T(8,128)} %reshape.29), calls=%async_computation.1 | async-start | bytes 1048576 | tf_op jit(solution)/shard_map/all_to_all | solution.py:634
  63.7 1.4 %copy-start.12 = (f32[24,136,128]{2,1,0:T(8,128)S(1)}, f32[24,136,128]{2,1,0:T(8,128)}, u32[]{:S(2)}) copy-start(f32[24,136,128]{2,1,0:T(8,128)} %copy-done.11) | copy-start | bytes 5013508
  65.1 16.0 %copy-start.5 = (bf16[512,256]{1,0:T(8,128)(2,1)S(1)}, bf16[512,256]{1,0:T(8,128)(2,1)}, u32[]{:S(2)}) copy-start(bf16[512,256]{1,0:T(8,128)(2,1)} %constant.48.clone.fh_ref) | copy-start | bytes 786436
  65.1 16.0 %copy-start.6 = (bf16[512,256]{1,0:T(8,128)(2,1)S(1)}, bf16[512,256]{1,0:T(8,128)(2,1)}, u32[]{:S(2)}) copy-start(bf16[512,256]{1,0:T(8,128)(2,1)} %constant.49.clone.fl_ref) | copy-start | bytes 786436
  80.4 12.7 %copy-start.1 = (bf16[512,512]{1,0:T(8,128)(2,1)S(1)}, bf16[512,512]{1,0:T(8,128)(2,1)}, u32[]{:S(2)}) copy-start(bf16[512,512]{1,0:T(8,128)(2,1)} %constant.50.clone.fh_ref) | copy-start | bytes 1572868
  80.4 12.7 %copy-start.2 = (bf16[512,512]{1,0:T(8,128)(2,1)S(1)}, bf16[512,512]{1,0:T(8,128)(2,1)}, u32[]{:S(2)}) copy-start(bf16[512,512]{1,0:T(8,128)(2,1)} %constant.51.clone.fl_ref) | copy-start | bytes 1572868
  81.1 41.2 %copy-start.13 = (f32[1,64]{1,0:T(1,128)S(1)}, f32[1,64]{1,0:T(1,128)}, u32[]{:S(2)}) copy-start(f32[1,64]{1,0:T(1,128)} %constant.54) | copy-start | bytes 772
  82.7 10.4 %all-to-all-start.2 = ((f32[4,192,128]{2,1,0:T(8,128)}), f32[4,192,128]{2,1,0:T(8,128)S(1)}, u32[]{:S(2)}, u32[]{:S(2)}) async-start(f32[4,192,128]{2,1,0:T(8,128)} %y_lines.1), calls=%async_computation.2 | async-start | bytes 786432 | tf_op jit(solution)/shard_map/all_to_all | solution.py:639
where the time goes:
time: 123 us
  blocking collectives  38.6 us (31%)
  Pallas kernels  35.9 us (29%)
  starting transfers between devices  25.5 us (21%)
  waiting for transfers between devices  14.8 us (12%)
  local copies, waits for them, and re-layouts  6.65 us (5%)
    all_to_all x2, blocking collectives, gathered_sum(): lax.all_to_all(copies, axes, split_axis=0, concat_axis=0, tiled=True)  27.4 us
    pallas_call x1, Pallas kernels, per_device(): pl.pallas_call(collide_body, name='collide', grid=(BLOCKS,), in_specs=[SM...  15.2 us
    pallas_call x1, Pallas kernels, per_device(): pl.pallas_call(scatter_body, name='scatter', grid=(BLOCKS,), in_specs=[SM...  13.2 us
    all_to_all x1, blocking collectives, per_device(): arrived = lax.all_to_all(sent, GZ, split_axis=0, concat_axis=0, tiled=True)  11.2 us
    all_to_all x1, starting transfers between devices, per_device(): lax.all_to_all(lines.reshape(64, 12, 128), GY_GZ, split_axis=0, concat_ax...  8.85 us
    ppermute x3, starting transfers between devices, ring(): lax.ppermute(high, axis, forward)  8.48 us
    all_to_all x1, waiting for transfers between devices, per_device(): lax.all_to_all(rows, 'gx', split_axis=0, concat_axis=0, tiled=True)  6.35 us
    unnamed x29, local copies, waits for them, and re-layouts  5.57 us
  transfers between devices with their start and end apart: 8, of which 7 were waited for; matrix products, arithmetic and copies ran while one was open for 0% of the time, Pallas kernels for 12%

commit v1 on v0

--- a/solution.py
+++ b/solution.py
@@ -27,8 +27,11 @@
 ROWS = 160
 SROW = 36
 LROW = 68
-BLOCKS = 4
+BLOCKS = 1
 GROUPS = TILES // 8 // BLOCKS
+STEPS = 8
+EARLY = 4
+PARTS = TILES // 8 // STEPS
 
 
 def axis_vectors(axis_index):
@@ -76,7 +79,14 @@
 def onehot_of(member, t, cells):
     return jnp.concatenate(
         [
-            (cells == member[PPC * t + r : PPC * t + r + 1, :]).astype(F32).astype(BF16)
+            jnp.where(
+                cells
+                == jnp.broadcast_to(
+                    member[PPC * t + r : PPC * t + r + 1, :], cells.shape
+                ).astype(BF16),
+                jnp.ones(cells.shape, BF16),
+                jnp.zeros(cells.shape, BF16),
+            )
             for r in range(PPC)
         ],
         axis=1,
@@ -86,12 +96,12 @@
 def scatter_body(shift_ref, v_ref, p_ref, axis_ref, s_ref, m_ref, n_ref, xlo_ref, xhi_ref, ylo_ref,
                  yhi_ref, zlo_ref, zhi_ref, turn_ref, edge_ref, zed_ref):
     step = pl.program_id(0)
-    cells = iota((TILE, TILE), 0)
+    cells = iota((TILE, TILE), 0).astype(F32).astype(BF16)
     upper = iota((8, TILE), 0) < 4
 
     def group(g, carry):
         place = p_ref[pl.ds(pl.multiple_of(g * 40, 8), 40), :]
-        member = place >> 6
+        member = (place >> 6).astype(F32)
         octant = octants(place, shift_ref)
         speed = v_ref[:, pl.ds(pl.multiple_of(g * 5120, 128), 5120)]
         high = speed.astype(BF16).astype(F32)
@@ -107,8 +117,8 @@
                 [jnp.where(code == o, values, 0.0) for o in range(8)], axis=0
             ).astype(BF16)
             sums = lax.dot_general(
-                weighted, onehot, (((1,), (1,)), ((), ())), preferred_element_type=F32
-            )
+                onehot, weighted, (((1,), (1,)), ((), ())), preferred_element_type=F32
+            ).T
             for pair in range(4):
                 even = sums[16 * pair : 16 * pair + 8]
                 odd = sums[16 * pair + 8 : 16 * pair + 16]
@@ -370,22 +380,23 @@
             up = sroll(lroll(plane, -size), size)
             plane = jnp.where(row_bit == lane_bit, plane, jnp.where(row_bit == 0, down, up))
         for part in range(8):
-            send_ref[part, 16 * c : 16 * c + 16, :] = plane[16 * part : 16 * part + 16]
-
-
-def collide_body(shift_ref, v_ref, p_ref, view_ref, out_ref, turn_ref):
-    step = pl.program_id(0)
-    cells = iota((TILE, TILE), 0)
-
-    @pl.when(step == 0)
+            send_ref[part, 32 * c : 32 * c + 32, :] = plane[32 * (part % 4) : 32 * (part % 4) + 32]
+
+
+def collide_body(start, shift_ref, v_ref, p_ref, view_ref, *refs):
+    out_ref, turn_ref = refs[-2:]
+    step = pl.program_id(0) + start
+    cells = iota((TILE, TILE), 0).astype(F32).astype(BF16)
+
+    @pl.when(step == start)
     def _():
         turn_ref[...] = jnp.zeros(turn_ref.shape, F32)
 
     def group(g, carry):
         place = p_ref[pl.ds(pl.multiple_of(g * 40, 8), 40), :]
-        member = place >> 6
+        member = (place >> 6).astype(F32)
         octant = octants(place, shift_ref)
-        first = pl.multiple_of((step * GROUPS + g) * 8, 8)
+        first = pl.multiple_of((step * PARTS + g) * 8, 8)
         for bx in range(2):
             for bz in range(2):
                 for k in range(6):
@@ -417,7 +428,7 @@
             )
         return carry
 
-    lax.fori_loop(0, GROUPS, group, 0)
+    lax.fori_loop(0, PARTS, group, 0)
 
 
 def table_parts(table):
@@ -428,13 +439,15 @@
 
 
 def z_tables():
-    kz_high = np.arange(64)[:, None]
     pos = np.arange(NZ)[None, :]
-    rows = []
-    for q in range(4):
-        phase = (2 * kz_high + q // 2) * pos % NZ * (2.0 * np.pi / NZ)
-        rows.append(-np.sin(phase) if q % 2 else np.cos(phase))
-    return table_parts(np.concatenate(rows, axis=0))
+    line = np.arange(32)[:, None]
+    halves = []
+    for half in range(2):
+        owner = line // 4 * 8 + half * 4 + line % 4
+        for q in range(4):
+            phase = (2 * owner + q // 2) * pos % NZ * (2.0 * np.pi / NZ)
+            halves.append(-np.sin(phase) if q % 2 else np.cos(phase))
+    return table_parts(np.concatenate(halves, axis=0).reshape(2, 128, NZ))
 
 
 def y_tables():
@@ -470,35 +483,39 @@
     return np.diff(below).astype(np.float32)
 
 
-def z_body(in_ref, fh_ref, fl_ref, out_ref):
-    lane = iota((64, 128), 1)
-    fh, fl = fh_ref[...], fl_ref[...]
+def z_body(first_ref, in_ref, fh_ref, fl_ref, out_ref):
+    lane = iota((32, 128), 1)
+    fh, fl = fh_ref[first_ref[2]], fl_ref[first_ref[2]]
     for c in range(3):
-        data = in_ref[:, 16 * c : 16 * c + 16, :].reshape(128, 128)
+        data = jnp.concatenate(
+            [
+                in_ref[:, 32 * c + 16 * r : 32 * c + 16 * r + 16, :].reshape(128, 128)
+                for r in range(2)
+            ],
+            axis=1,
+        )
         high, low = split(data)
         res = dot(fh, high) + dot(fh, low) + dot(fl, high)
-        g = [res[64 * q : 64 * q + 64] for q in range(4)]
-        for bit, size in ((2, 8), (1, 4)):
-            clear = (lane & size) == 0
-            new = list(g)
-            for q in range(4):
-                if not q & bit:
-                    a, b = g[q], g[q | bit]
-                    new[q] = jnp.where(clear, a, lroll(b, size))
-                    new[q | bit] = jnp.where(clear, lroll(a, -size), b)
-            g = new
-        for r in range(4):
-            out_ref[pl.ds(4 * c + r, 64, stride=12), :] = g[r]
+        for r in range(2):
+            g = [res[32 * q : 32 * q + 32, 128 * r : 128 * r + 128] for q in range(4)]
+            for bit, size in ((2, 8), (1, 4)):
+                clear = (lane & size) == 0
+                new = list(g)
+                for q in range(4):
+                    if not q & bit:
+                        a, b = g[q], g[q | bit]
+                        new[q] = jnp.where(clear, a, lroll(b, size))
+                        new[q | bit] = jnp.where(clear, lroll(a, -size), b)
+                g = new
+            for k in range(4):
+                out_ref[pl.ds(8 * c + 4 * r + k, 32, stride=24), :] = g[k]
 
 
 def y_body(in_ref, fh_ref, fl_ref, out_ref):
     both = in_ref[...].reshape(32, 24, 128)
-    v0, v1, v2 = both[:, 0:8], both[:, 8:16], both[:, 16:24]
-    upper = iota((32, 8, 128), 1) < 4
-    d0 = jnp.where(upper, v0, v1)
-    d1 = pltpu.roll(jnp.where(upper, v2, v0), 4, 1)
-    d2 = jnp.where(upper, v1, v2)
-    data = jnp.concatenate([d.reshape(256, 128) for d in (d0, d1, d2)], axis=1)
+    data = jnp.concatenate(
+        [both[:, 8 * c : 8 * c + 8].reshape(256, 128) for c in range(3)], axis=1
+    )
     high, low = split(data)
     fh, fl = fh_ref[...], fl_ref[...]
     res = dot(fh, high) + dot(fh, low) + dot(fl, high)
@@ -509,6 +526,7 @@
         out = even + jnp.where(is_real, lroll(odd, -4), -lroll(odd, 4))
         for d in range(4):
             out_ref[d, 64 * c : 64 * c + 64, :] = out[64 * d : 64 * d + 64]
+            out_ref[d, 192 + 64 * c : 256 + 64 * c, :] = out[0:64]
 
 
 def x_body(first_ref, in_ref, fh_ref, fl_ref, out_ref, shell_ref, sums_ref):
@@ -516,22 +534,23 @@
     high, low = split(data)
     fh, fl = fh_ref[...], fl_ref[...]
     res = dot(high, fh) + dot(low, fh) + dot(high, fl)
-    ky = first_ref[1] + iota((64, 128), 0)
-    ky = jnp.where(ky >= NY // 2, ky - NY, ky)
+    ky = iota((64, 128), 0)
     kx = iota((64, 128), 1)
     kx = jnp.where(kx >= NX // 2, kx - NX, kx)
     plane = ky * ky + kx * kx
+    weight = jnp.where(ky == 0, 1.0, 2.0)
     energy, square = [], []
     for kz in range(2):
         total = jnp.zeros((64, 128), F32)
         for part in range(2):
             for c in range(3):
-                block = res[64 * c : 64 * c + 64, 256 * part + 128 * kz : 256 * part + 128 * kz + 128]
-                out_ref[part, c, kz] = block
+                here = slice(256 * part + 128 * kz, 256 * part + 128 * kz + 128)
+                out_ref[part, c, kz] = res[64 * c : 64 * c + 64, here]
+                block = res[192 + 64 * c : 256 + 64 * c, here]
                 total += block * block
         wave = first_ref[0] + kz
         wave = jnp.where(wave >= NZ // 2, wave - NZ, wave)
-        energy.append(total)
+        energy.append(total * weight)
         square.append(plane + wave * wave)
     energy = jnp.concatenate(energy, axis=0)
     square = jnp.concatenate(square, axis=0)
@@ -571,6 +590,28 @@
 
 def whole(*shape):
     return pl.BlockSpec(shape, lambda i: (0,) * len(shape))
+
+
+def collide(start, stop, grid_shift, velocity, place, views, earlier):
+    span = TILES * TILE * PPC // STEPS
+    speed_spec = pl.BlockSpec((3, span), lambda i: (0, i + start))
+    place_spec = pl.BlockSpec((640 // STEPS, 128), lambda i: (i + start, 0))
+    more = [] if earlier is None else [earlier]
+    return pl.pallas_call(
+        lambda *refs: collide_body(start, *refs),
+        name="collide",
+        grid=(stop - start,),
+        in_specs=[SMEM, speed_spec, place_spec, whole(24, VROWS, 128)]
+        + [pl.BlockSpec(memory_space=pl.ANY)] * len(more),
+        out_specs=speed_spec,
+        out_shape=struct(*velocity.shape),
+        scratch_shapes=[pltpu.VMEM((8 * LROW, 128), F32)],
+        input_output_aliases={4: 0} if more else {},
+        compiler_params=params(12),
+        cost_estimate=pl.CostEstimate(
+            flops=800_000_000 * (stop - start), bytes_accessed=4_000_000, transcendentals=0
+        ),
+    )(grid_shift, velocity, place, views, *more)
 
 
 def per_device(velocity, particle_place, grid_shift, rotation_axis):
@@ -608,7 +649,7 @@
     views, sent = pl.pallas_call(
         cell_body,
         name="cells",
-        out_shape=[struct(24, VROWS, 128), struct(8, 48, 128)],
+        out_shape=[struct(24, VROWS, 128), struct(8, 96, 128)],
         scratch_shapes=[
             pltpu.VMEM((7, ROWS, 128), F32),
             pltpu.VMEM((7, ROWS, 128), F32),
@@ -616,37 +657,38 @@
         ],
         compiler_params=params(12),
     )(sums, main, normal, x_lo, x_hi, y_lo, y_hi, z_lo, z_hi, below, above)
+    first = jnp.stack(
+        [lax.axis_index(GY_GZ) * 2, lax.axis_index("gx") * 64, lax.axis_index("gz_0")]
+    ).astype(jnp.int32)
     arrived = lax.all_to_all(sent, GZ, split_axis=0, concat_axis=0, tiled=True)
-    lines = pl.pallas_call(z_body, name="z_lines", out_shape=struct(768, 128), compiler_params=params(12))(
-        arrived, *z_tables()
+    updated = collide(0, EARLY, grid_shift, velocity, place, views, None)
+    arrived, updated = lax.optimization_barrier((arrived, updated))
+    vmem = pl.BlockSpec(memory_space=pltpu.VMEM)
+    lines = pl.pallas_call(
+        z_body,
+        name="z_lines",
+        in_specs=[SMEM, vmem, vmem, vmem],
+        out_shape=struct(768, 128),
+        compiler_params=params(6),
+    )(first, arrived, *z_tables())
+    pencil = lax.all_to_all(
+        lines.reshape(32, 24, 128), ("gy_0", "gy_1", "gz_1"), split_axis=0, concat_axis=0, tiled=True
     )
-    new_velocity = pl.pallas_call(
-        collide_body,
-        name="collide",
-        grid=(BLOCKS,),
-        in_specs=[SMEM, speed_spec, place_spec, whole(24, VROWS, 128)],
-        out_specs=speed_spec,
-        out_shape=struct(*velocity.shape),
-        scratch_shapes=[pltpu.VMEM((8 * LROW, 128), F32)],
-        compiler_params=params(12),
-        cost_estimate=pl.CostEstimate(flops=6_000_000_000, bytes_accessed=4_000_000, transcendentals=0),
-    )(grid_shift, velocity, place, views)
-    pencil = lax.all_to_all(lines.reshape(64, 12, 128), GY_GZ, split_axis=0, concat_axis=0, tiled=True)
+    new_velocity = collide(EARLY, STEPS, grid_shift, velocity, place, views, updated)
     pencil, new_velocity = lax.optimization_barrier((pencil, new_velocity))
-    rows = pl.pallas_call(y_body, name="y_lines", out_shape=struct(4, 192, 128), compiler_params=params(12))(
+    rows = pl.pallas_call(y_body, name="y_lines", out_shape=struct(4, 384, 128), compiler_params=params(12))(
         pencil.reshape(768, 128), *y_tables()
     )
     columns = lax.all_to_all(rows, "gx", split_axis=0, concat_axis=0, tiled=True)
-    first = jnp.stack([lax.axis_index(GY_GZ) * 2, lax.axis_index("gx") * 64]).astype(jnp.int32)
     modes, shells = pl.pallas_call(
         x_body,
         name="x_lines",
-        in_specs=[SMEM] + [pl.BlockSpec(memory_space=pltpu.VMEM)] * 3,
+        in_specs=[SMEM, vmem, vmem, vmem],
         out_shape=[struct(2, 3, 2, 64, 128), struct(1, 128)],
         scratch_shapes=[pltpu.VMEM((NSHELL, 128), F32)],
         compiler_params=params(12),
     )(first, columns, *x_tables())
-    total = gathered_sum(gathered_sum(shells, GY_GZ), "gx")
+    total = gathered_sum(shells, GY_GZ)
     spectrum = total[0, :NSHELL] / shell_counts()
     return new_velocity, modes, spectrum
 

time: 123 us -> 116 us (0.943)
  blocking collectives: 38.6 us -> 31.9 us
  starting transfers between devices: 25.5 us -> 28 us
  Pallas kernels: 35.9 us -> 33.7 us
    all_to_all x2 -> x1, blocking collectives: 27.4 us -> 18.2 us  [gathered_sum(): lax.all_to_all(copies, axes, split_axis=0, concat_axis=0, tiled=True)]
    all_to_all x1, blocking collectives: 11.2 us -> 13.7 us  [per_device(): lax.all_to_all(rows, 'gx', split_axis=0, concat_axis=0, tiled=True)]
    all_to_all x2, starting transfers between devices: 12.8 us -> 15.4 us  [the longest x1 10 us: per_device(): lax.all_to_all(lines.reshape(32, 24, 128), ('gy_0', 'gy_1', 'gz_1'), spli...]
    pallas_call x1, Pallas kernels: 13.2 us -> 11.7 us  [per_device(): pl.pallas_call(scatter_body, name='scatter', grid=(BLOCKS,), in_specs=[SM...]
    pallas_call x4 -> x5, Pallas kernels: 19 us -> 17.6 us  [the longest x2 13 us: collide(): pl.pallas_call(lambda *refs: collide_body(start, *refs), name='collide',...]
  transfers between devices with their start and end apart: 8 -> 8, of which waited for: 7 -> 6; matrix products, arithmetic and copies ran while one was open for 0% -> 0% of each run, Pallas kernels for 12% -> 11%
where the time goes in v1:
time: 116 us; the launch traced here: 115 us
  Pallas kernels  33.7 us (29%)
  blocking collectives  31.9 us (28%)
  starting transfers between devices  28 us (24%)
  waiting for transfers between devices  13.7 us (12%)
  local copies, waits for them, and re-layouts  6.57 us (6%)
    all_to_all x1, blocking collectives, gathered_sum(): lax.all_to_all(copies, axes, split_axis=0, concat_axis=0, tiled=True)  18.2 us
    all_to_all x1, blocking collectives, per_device(): lax.all_to_all(rows, 'gx', split_axis=0, concat_axis=0, tiled=True)  13.7 us
    pallas_call x2, Pallas kernels, collide(): pl.pallas_call(lambda *refs: collide_body(start, *refs), name='collide',...  13 us
    pallas_call x1, Pallas kernels, per_device(): pl.pallas_call(scatter_body, name='scatter', grid=(BLOCKS,), in_specs=[SM...  11.7 us
    all_to_all x1, starting transfers between devices, per_device(): lax.all_to_all(lines.reshape(32, 24, 128), ('gy_0', 'gy_1', 'gz_1'), spli...  10 us
    ppermute x3, starting transfers between devices, ring(): lax.ppermute(high, axis, forward)  8.5 us
    unnamed x29, local copies, waits for them, and re-layouts  6.37 us
    all_to_all x1, waiting for transfers between devices, per_device(): lax.all_to_all(lines.reshape(32, 24, 128), ('gy_0', 'gy_1', 'gz_1'), spli...  5.95 us
  transfers between devices with their start and end apart: 8, of which 6 were waited for; matrix products, arithmetic and copies ran while one was open for 0% of the time, Pallas kernels for 11%

profile of v1, /device:TPU:1, one launch (start us, length us, event | category | flops | bytes accessed | tf_op | source)
XLA Modules:
  0.0 115.4 jit_solution(15640210046018674323)
XLA Ops:
  0.7 1.3 %copy.18 = s32[32,32,16]{2,1,0:T(8,128)S(1)} copy(s32[32,32,16]{1,2,0:T(8,128)} %param.14) | data formatting | bytes 131072 | tf_op args[3]
  1.9 0.2 reshape.23.axis_ref
  2.1 1.0 copy-done.3
  3.1 11.7 %scatter.1 = (f32[32,128,128]{2,1,0:T(8,128)S(1)}, f32[4,160,128]{2,1,0:T(8,128)S(1)}, f32[3,128,128]{2,1,0:T(8,128)S(1)}, f32[40,128]{1,0:T(8,128)S(1)}, f32[40...) custom-call(s32[3]{0:T(128)S(1)} %copy-done.9, ...), custom_call_target="tpu_custom_call" | custom-call | tf_op jit(solution)/shard_map/scatter/pallas_call | solution.py:625
  14.8 2.1 %collective-permute-start = (f32[40,128]{1,0:T(8,128)S(1)}, f32[40,128]{1,0:T(8,128)S(1)}, u32[]{:S(2)}, u32[]{:S(2)}) collective-permute-start(f32[40,128]{1,0:T(8,128)S(1)} %get-tuple-element.32.xhi_ref), channel_id=1, source_target_pairs={{0,64},{64,128},{128,192},{192,0},{1,65},{65,129},{129,193},{193,1... | collective-permute-start | bytes 61448 | tf_op jit(solution)/shard_map/ppermute | solution.py:578
  16.9 1.4 %collective-permute-start.1 = (f32[40,128]{1,0:T(8,128)S(1)}, f32[40,128]{1,0:T(8,128)S(1)}, u32[]{:S(2)}, u32[]{:S(2)}) collective-permute-start(f32[40,128]{1,0:T(8,128)S(1)} %get-tuple-element.31.xlo_ref), channel_id=1, source_target_pairs={{64,0},{128,64},{192,128},{0,192},{65,1},{129,65},{193,129},{1,193... | collective-permute-start | bytes 61448 | tf_op jit(solution)/shard_map/ppermute | solution.py:578
  18.3 1.1 collective-permute-done.from_low
  19.4 0.2 collective-permute-done.1.from_high
  19.6 0.1 fold_x.1
  19.7 5.0 %collective-permute-start.2 = (f32[40,128]{1,0:T(8,128)S(1)}, f32[40,128]{1,0:T(8,128)S(1)}, u32[]{:S(2)}, u32[]{:S(2)}) collective-permute-start(f32[40,128]{1,0:T(8,128)S(1)} %get-tuple-element.38.yhi_ref), channel_id=1, source_target_pairs={{0,8},{8,16},{16,24},{24,32},{32,40},{40,48},{48,56},{56,0},{1,9},... | collective-permute-start | bytes 61448 | tf_op jit(solution)/shard_map/ppermute | solution.py:578
  24.7 0.9 collective-permute-done.2.from_low
  25.6 3.3 %collective-permute-done.3.from_high = f32[40,128]{1,0:T(8,128)S(1)} collective-permute-done((f32[40,128]{1,0:T(8,128)S(1)}, f32[40,128]{1,0:T(8,128)S(1)}, u32[]{:S(2)}, u32[]{:S(2)}) %collective-permute-start.3) | collective-permute-done | bytes 20512 | tf_op jit(solution)/shard_map/ppermute | solution.py:578
  28.8 0.2 fold_y.1
  29.0 1.4 %collective-permute-start.4 = (f32[160,128]{1,0:T(8,128)S(1)}, f32[160,128]{1,0:T(8,128)S(1)}, u32[]{:S(2)}, u32[]{:S(2)}) collective-permute-start(f32[160,128]{1,0:T(8,128)S(1)} %get-tuple-element.44.zhi_ref), channel_id=1, source_target_pairs={{0,1},{1,2},{2,3},{3,4},{4,5},{5,6},{6,7},{7,0},{8,9},{9,10},{10,1... | collective-permute-start | bytes 245768 | tf_op jit(solution)/shard_map/ppermute | solution.py:578
  30.4 2.8 %collective-permute-start.5 = (f32[160,128]{1,0:T(8,128)S(1)}, f32[160,128]{1,0:T(8,128)S(1)}, u32[]{:S(2)}, u32[]{:S(2)}) collective-permute-start(f32[160,128]{1,0:T(8,128)S(1)} %get-tuple-element.43.zlo_ref), channel_id=1, source_target_pairs={{1,0},{2,1},{3,2},{4,3},{5,4},{6,5},{7,6},{0,7},{9,8},{10,9},{11,1... | collective-permute-start | bytes 245768 | tf_op jit(solution)/shard_map/ppermute | solution.py:578
  33.2 2.3 %collective-permute-done.4.from_low = f32[160,128]{1,0:T(8,128)S(1)} collective-permute-done((f32[160,128]{1,0:T(8,128)S(1)}, f32[160,128]{1,0:T(8,128)S(1)}, u32[]{:S(2)}, u32[]{:S(2)}) %collective-permute-start.4) | collective-permute-done | bytes 81952 | tf_op jit(solution)/shard_map/ppermute | solution.py:578
  35.6 4.1 %cells.1 = (f32[24,136,128]{2,1,0:T(8,128)S(1)}, f32[8,96,128]{2,1,0:T(8,128)}) custom-call(f32[32,128,128]{2,1,0:T(8,128)S(1)} %get-tuple-element.28.s_ref, f32[4,160,128]{2,1,0:T(8,128)S(1)} %get-tuple-element.29.m_ref, f32[3,128,128]{2,1,0:T(8,128)S(1)} %get-tuple-element.30.n_ref, f32[40,128]{1,0:T(8,128)S(1)} %get-tuple-element.35.xlo_ref, ...), custom_call_target="tpu_custom_call" | custom-call | tf_op jit(solution)/shard_map/cells/pallas_call | solution.py:649
  39.7 1.2 %copy-done.10 = f32[24,136,128]{2,1,0:T(8,128)} copy-done((f32[24,136,128]{2,1,0:T(8,128)}, f32[24,136,128]{2,1,0:T(8,128)S(1)}, u32[]{:S(2)}) %copy-start.10) | copy-done | bytes 1671192
  40.9 5.3 %all-to-all-start = ((f32[8,96,128]{2,1,0:T(8,128)}), f32[8,96,128]{2,1,0:T(8,128)S(1)}, u32[]{:S(2)}, u32[]{:S(2)}) async-start(f32[8,96,128]{2,1,0:T(8,128)} %get-tuple-element.45), calls=%async_computation | async-start | bytes 786432 | tf_op jit(solution)/shard_map/all_to_all | solution.py:663
  46.2 0.1 pad_add_fusion.first_ref
  46.3 1.4 %copy-done.11 = f32[24,136,128]{2,1,0:T(8,128)S(1)} copy-done((f32[24,136,128]{2,1,0:T(8,128)S(1)}, f32[24,136,128]{2,1,0:T(8,128)}, u32[]{:S(2)}) %copy-start.11) | copy-done | bytes 1671192
  47.8 6.5 %collide.2.refs_4_ = f32[3,81920]{1,0:T(4,128)} custom-call(s32[3]{0:T(128)S(1)} %copy-done.9, f32[3,81920]{1,0:T(4,128)S(1)} %copy-done, s32[640,128]{1,0:T(8,128)S(1)} %bitcast.13, f32[24,136,128]{2,1,0:T(8,128)S(1)} %copy-done.11), custom_call_target="tpu_custom_call" | custom-call | flops 3200000000 | bytes 4000000 | tf_op jit(solution)/shard_map/collide/pallas_call | solution.py:600
  54.3 1.8 %z_lines.1 = f32[768,128]{1,0:T(8,128)} custom-call(s32[3]{0:T(128)S(1)} %pad_add_fusion.first_ref, f32[8,96,128]{2,1,0:T(8,128)S(1)} %all-to-all-done.in_ref, bf16[2,128,128]{2,1,0:T(8,128)(2,1)S(1)} %copy-done.7, bf16[2,128,128]{2,1,0:T(8,128)(2,1)S(1)} %copy-done.8), custom_call_target="tpu_custom_call" | custom-call | tf_op jit(solution)/shard_map/z_lines/pallas_call | solution.py:667
  56.1 10.0 %all-to-all-start.1 = ((f32[32,24,128]{2,1,0:T(8,128)}), f32[32,24,128]{2,1,0:T(8,128)S(1)}, u32[]{:S(2)}, u32[]{:S(2)}) async-start(f32[32,24,128]{2,1,0:T(8,128)} %bitcast.4), calls=%async_computation.1 | async-start | bytes 786432 | tf_op jit(solution)/shard_map/all_to_all | solution.py:674
  66.1 1.4 %copy-done.12 = f32[24,136,128]{2,1,0:T(8,128)S(1)} copy-done((f32[24,136,128]{2,1,0:T(8,128)S(1)}, f32[24,136,128]{2,1,0:T(8,128)}, u32[]{:S(2)}) %copy-start.12) | copy-done | bytes 1671192
  67.6 6.5 %collide.3 = f32[3,81920]{1,0:T(4,128)} custom-call(s32[3]{0:T(128)S(1)} %copy-done.9, f32[3,81920]{1,0:T(4,128)S(1)} %copy-done, s32[640,128]{1,0:T(8,128)S(1)} %bitcast.14, f32[24,136,128]{2,1,0:T(8,128)S(1)} %copy-done.12, f32[3,81920]{1,0:T(4,128)} %collide.2.refs_4_), custom_call_target="tpu_custom_call", output_to_operand_aliasing={{}: (4, {})} | custom-call | flops 3200000000 | bytes 4000000 | tf_op jit(solution)/shard_map/collide/pallas_call | solution.py:600
  74.1 6.0 %all-to-all-done.1 = f32[32,24,128]{2,1,0:T(8,128)S(1)} async-done(((f32[32,24,128]{2,1,0:T(8,128)}), f32[32,24,128]{2,1,0:T(8,128)S(1)}, u32[]{:S(2)}, u32[]{:S(2)}) %all-to-all-start.1) | async-done | bytes 393248 | tf_op jit(solution)/shard_map/all_to_all | solution.py:674
  80.0 0.8 y_lines.1
  80.8 13.7 %all_to_all.20.in_ref = f32[4,384,128]{2,1,0:T(8,128)S(1)} all-to-all(f32[4,384,128]{2,1,0:T(8,128)S(1)} %y_lines.1), channel_id=1, replica_groups=mesh['gx'=4,'gy_0'=4,'gy_1'=2,'gz_0'=2,'gz_1'=4] {'gx'}, dimensions={0} | all-to-all | bytes 1572864 | tf_op jit(solution)/shard_map/all_to_all | solution.py:682
  94.5 2.0 %x_lines.1 = (f32[2,3,2,64,128]{4,3,2,1,0:T(8,128)}, f32[1,128]{1,0:T(1,128)S(1)}) custom-call(s32[3]{0:T(128)S(1)} %pad_add_fusion.first_ref, f32[4,384,128]{2,1,0:T(8,128)S(1)} %all_to_all.20.in_ref, bf16[512,512]{1,0:T(8,128)(2,1)S(1)} %copy-done.1, bf16[512,512]{1,0:T(8,128)(2,1)S(1)} %copy-done.2), custom_call_target="tpu_custom_call" | custom-call | tf_op jit(solution)/shard_map/x_lines/pallas_call | solution.py:683
  96.6 18.2 %all_to_all.21 = f32[64,1,128]{2,1,0:T(1,128)S(1)} all-to-all(f32[64,1,128]{2,1,0:T(1,128)S(1)} %broadcast_in_dim.9), channel_id=1, replica_groups=mesh['gx'=4,'gy_0'=4,'gy_1'=2,'gz_0'=2,'gz_1'=4] {'gy_0','gy_1','gz_0','..., dimensions={0} | all-to-all | bytes 65536 | tf_op jit(solution)/shard_map/all_to_all | solution.py:584
  114.8 0.5 multiply_bitcast_fusion
  (29 shorter events, 0.1 us)
Async XLA Ops:
  0.6 1.5 %copy-start = (f32[3,81920]{1,0:T(4,128)S(1)}, f32[3,81920]{1,0:T(4,128)}, u32[]{:S(2)}) copy-start(f32[3,81920]{1,0:T(4,128)} %refs_1_.3) | copy-start | bytes 2949124
  0.6 1.5 %copy-start.9 = (s32[3]{0:T(128)S(1)}, s32[3]{0:T(128)}, u32[]{:S(2)}) copy-start(s32[3]{0:T(128)} %refs_0_.3) | copy-start | bytes 40
  2.1 1.0 copy-start.3
  14.8 4.5 %collective-permute-start = (f32[40,128]{1,0:T(8,128)S(1)}, f32[40,128]{1,0:T(8,128)S(1)}, u32[]{:S(2)}, u32[]{:S(2)}) collective-permute-start(f32[40,128]{1,0:T(8,128)S(1)} %get-tuple-element.32.xhi_ref), channel_id=1, source_target_pairs={{0,64},{64,128},{128,192},{192,0},{1,65},{65,129},{129,193},{193,1... | collective-permute-start | bytes 61448 | tf_op jit(solution)/shard_map/ppermute | solution.py:578
  16.9 2.6 %collective-permute-start.1 = (f32[40,128]{1,0:T(8,128)S(1)}, f32[40,128]{1,0:T(8,128)S(1)}, u32[]{:S(2)}, u32[]{:S(2)}) collective-permute-start(f32[40,128]{1,0:T(8,128)S(1)} %get-tuple-element.31.xlo_ref), channel_id=1, source_target_pairs={{64,0},{128,64},{192,128},{0,192},{65,1},{129,65},{193,129},{1,193... | collective-permute-start | bytes 61448 | tf_op jit(solution)/shard_map/ppermute | solution.py:578
  19.7 5.9 %collective-permute-start.2 = (f32[40,128]{1,0:T(8,128)S(1)}, f32[40,128]{1,0:T(8,128)S(1)}, u32[]{:S(2)}, u32[]{:S(2)}) collective-permute-start(f32[40,128]{1,0:T(8,128)S(1)} %get-tuple-element.38.yhi_ref), channel_id=1, source_target_pairs={{0,8},{8,16},{16,24},{24,32},{32,40},{40,48},{48,56},{56,0},{1,9},... | collective-permute-start | bytes 61448 | tf_op jit(solution)/shard_map/ppermute | solution.py:578
  24.7 4.2 %collective-permute-start.3 = (f32[40,128]{1,0:T(8,128)S(1)}, f32[40,128]{1,0:T(8,128)S(1)}, u32[]{:S(2)}, u32[]{:S(2)}) collective-permute-start(f32[40,128]{1,0:T(8,128)S(1)} %get-tuple-element.37.ylo_ref), channel_id=1, source_target_pairs={{8,0},{16,8},{24,16},{32,24},{40,32},{48,40},{56,48},{0,56},{9,1},... | collective-permute-start | bytes 61448 | tf_op jit(solution)/shard_map/ppermute | solution.py:578
  29.0 6.5 %collective-permute-start.4 = (f32[160,128]{1,0:T(8,128)S(1)}, f32[160,128]{1,0:T(8,128)S(1)}, u32[]{:S(2)}, u32[]{:S(2)}) collective-permute-start(f32[160,128]{1,0:T(8,128)S(1)} %get-tuple-element.44.zhi_ref), channel_id=1, source_target_pairs={{0,1},{1,2},{2,3},{3,4},{4,5},{5,6},{6,7},{7,0},{8,9},{9,10},{10,1... | collective-permute-start | bytes 245768 | tf_op jit(solution)/shard_map/ppermute | solution.py:578
  30.4 5.2 %collective-permute-start.5 = (f32[160,128]{1,0:T(8,128)S(1)}, f32[160,128]{1,0:T(8,128)S(1)}, u32[]{:S(2)}, u32[]{:S(2)}) collective-permute-start(f32[160,128]{1,0:T(8,128)S(1)} %get-tuple-element.43.zlo_ref), channel_id=1, source_target_pairs={{1,0},{2,1},{3,2},{4,3},{5,4},{6,5},{7,6},{0,7},{9,8},{10,9},{11,1... | collective-permute-start | bytes 245768 | tf_op jit(solution)/shard_map/ppermute | solution.py:578
  35.6 10.8 %copy-start.4 = (s32[81920]{0:T(1024)S(1)}, s32[81920]{0:T(1024)}, u32[]{:S(2)}) copy-start(s32[81920]{0:T(1024)} %param.12) | copy-start | bytes 983044
  39.7 1.2 %copy-start.10 = (f32[24,136,128]{2,1,0:T(8,128)}, f32[24,136,128]{2,1,0:T(8,128)S(1)}, u32[]{:S(2)}) copy-start(f32[24,136,128]{2,1,0:T(8,128)S(1)} %get-tuple-element.46.refs_3_) | copy-start | bytes 5013508
  40.9 13.4 %all-to-all-start = ((f32[8,96,128]{2,1,0:T(8,128)}), f32[8,96,128]{2,1,0:T(8,128)S(1)}, u32[]{:S(2)}, u32[]{:S(2)}) async-start(f32[8,96,128]{2,1,0:T(8,128)} %get-tuple-element.45), calls=%async_computation | async-start | bytes 786432 | tf_op jit(solution)/shard_map/all_to_all | solution.py:663
  46.3 1.4 %copy-start.11 = (f32[24,136,128]{2,1,0:T(8,128)S(1)}, f32[24,136,128]{2,1,0:T(8,128)}, u32[]{:S(2)}) copy-start(f32[24,136,128]{2,1,0:T(8,128)} %copy-done.10) | copy-start | bytes 5013508
  47.8 6.5 %copy-start.7 = (bf16[2,128,128]{2,1,0:T(8,128)(2,1)S(1)}, bf16[2,128,128]{2,1,0:T(8,128)(2,1)}, u32[]{:S(2)}) copy-start(bf16[2,128,128]{2,1,0:T(8,128)(2,1)} %constant.46.clone.fh_ref) | copy-start | bytes 196612
  47.8 6.5 %copy-start.8 = (bf16[2,128,128]{2,1,0:T(8,128)(2,1)S(1)}, bf16[2,128,128]{2,1,0:T(8,128)(2,1)}, u32[]{:S(2)}) copy-start(bf16[2,128,128]{2,1,0:T(8,128)(2,1)} %constant.47.clone.fl_ref) | copy-start | bytes 196612
  56.1 24.0 %all-to-all-start.1 = ((f32[32,24,128]{2,1,0:T(8,128)}), f32[32,24,128]{2,1,0:T(8,128)S(1)}, u32[]{:S(2)}, u32[]{:S(2)}) async-start(f32[32,24,128]{2,1,0:T(8,128)} %bitcast.4), calls=%async_computation.1 | async-start | bytes 786432 | tf_op jit(solution)/shard_map/all_to_all | solution.py:674
  66.1 1.4 %copy-start.12 = (f32[24,136,128]{2,1,0:T(8,128)S(1)}, f32[24,136,128]{2,1,0:T(8,128)}, u32[]{:S(2)}) copy-start(f32[24,136,128]{2,1,0:T(8,128)} %copy-done.10) | copy-start | bytes 5013508
  67.6 12.5 %copy-start.5 = (bf16[512,256]{1,0:T(8,128)(2,1)S(1)}, bf16[512,256]{1,0:T(8,128)(2,1)}, u32[]{:S(2)}) copy-start(bf16[512,256]{1,0:T(8,128)(2,1)} %constant.48.clone.fh_ref) | copy-start | bytes 786436
  67.6 12.5 %copy-start.6 = (bf16[512,256]{1,0:T(8,128)(2,1)S(1)}, bf16[512,256]{1,0:T(8,128)(2,1)}, u32[]{:S(2)}) copy-start(bf16[512,256]{1,0:T(8,128)(2,1)} %constant.49.clone.fl_ref) | copy-start | bytes 786436
  80.0 14.5 %copy-start.1 = (bf16[512,512]{1,0:T(8,128)(2,1)S(1)}, bf16[512,512]{1,0:T(8,128)(2,1)}, u32[]{:S(2)}) copy-start(bf16[512,512]{1,0:T(8,128)(2,1)} %constant.50.clone.fh_ref) | copy-start | bytes 1572868
  80.0 14.5 %copy-start.2 = (bf16[512,512]{1,0:T(8,128)(2,1)S(1)}, bf16[512,512]{1,0:T(8,128)(2,1)}, u32[]{:S(2)}) copy-start(bf16[512,512]{1,0:T(8,128)(2,1)} %constant.51.clone.fl_ref) | copy-start | bytes 1572868
  94.5 20.3 %copy-start.13 = (f32[1,64]{1,0:T(1,128)S(1)}, f32[1,64]{1,0:T(1,128)}, u32[]{:S(2)}) copy-start(f32[1,64]{1,0:T(1,128)} %constant.54) | copy-start | bytes 772

commit v2 on v1

--- a/solution.py
+++ b/solution.py
@@ -30,7 +30,7 @@
 BLOCKS = 1
 GROUPS = TILES // 8 // BLOCKS
 STEPS = 8
-EARLY = 4
+EARLY = 6
 PARTS = TILES // 8 // STEPS
 
 
@@ -93,8 +93,7 @@
     )
 
 
-def scatter_body(shift_ref, v_ref, p_ref, axis_ref, s_ref, m_ref, n_ref, xlo_ref, xhi_ref, ylo_ref,
-                 yhi_ref, zlo_ref, zhi_ref, turn_ref, edge_ref, zed_ref):
+def scatter_body(shift_ref, v_ref, p_ref, axis_ref, s_ref, n_ref, xlo_ref, xhi_ref, turn_ref):
     step = pl.program_id(0)
     cells = iota((TILE, TILE), 0).astype(F32).astype(BF16)
     upper = iota((8, TILE), 0) < 4
@@ -135,85 +134,99 @@
     def _():
         for c, part in enumerate(axis_vectors(axis_ref[...])):
             n_ref[c] = part
-        lane = iota((TILES, 128), 1)
-        row = iota((TILES, 128), 0)
-        z = lane & 15
-        x_in = lane >> 4
-        x_out = row & 3
-        last = (x_in == 7) & (x_out == 3)
-
-        def x_shift(plane):
-            rolled = lroll(plane, 16)
-            return jnp.where(
-                x_in > 0, rolled, jnp.where(x_out > 0, sroll(rolled, 1), 0.0)
-            )
-
-        for q in range(5):
-            for by in range(2):
-                parts = []
-                for bx in range(2):
-                    base = bx * 4 + by * 2
-                    if q < 4:
-                        above = s_ref[(base + 1) * 4 + q]
-                        parts.append(
-                            s_ref[base * 4 + q] + jnp.where(z > 0, lroll(above, 1), 0.0)
-                        )
-                    else:
-                        rim = jnp.zeros((TILES, 128), F32)
-                        for k in range(4):
-                            rim = jnp.where(z == k, lroll(s_ref[(base + 1) * 4 + k], k - 15), rim)
-                        parts.append(rim)
-                main = parts[0] + x_shift(parts[1])
-                edge = jnp.where(last, parts[1], 0.0)
-                dst = m_ref if q < 4 else zed_ref
-                at = q if q < 4 else 0
-                if by == 0:
-                    dst[at, 0:TILES, :] = main
-                    dst[at, TILES:ROWS, :] = jnp.zeros((ROWS - TILES, 128), F32)
-                    edge_ref[q, 0:TILES, :] = edge
-                    edge_ref[q, TILES:ROWS, :] = jnp.zeros((ROWS - TILES, 128), F32)
-                else:
-                    dst[at, 4:132, :] = dst[at, 4:132, :] + main
-                    edge_ref[q, 4:132, :] = edge_ref[q, 4:132, :] + edge
-        lane40 = iota((40, 128), 1)
+        z = iota((32, 128), 1) & 15
+        lane = iota((40, 128), 1)
+        pad = jnp.zeros((8, 128), F32)
         low_face = jnp.zeros((40, 128), F32)
         high_face = jnp.zeros((40, 128), F32)
-        for q in range(4):
-            inside = (lane40 >> 4) == q
-            low_face = jnp.where(inside, lroll(m_ref[q, pl.ds(0, 40, stride=4), :], 16 * q), low_face)
-            high_face = jnp.where(
-                inside, lroll(edge_ref[q, pl.ds(3, 40, stride=4), :], 16 * q - 112), high_face
-            )
-        inside = (lane40 >> 2) == 16
-        low_face = jnp.where(inside, lroll(zed_ref[0, pl.ds(0, 40, stride=4), :], 64), low_face)
-        high_face = jnp.where(inside, lroll(edge_ref[4, pl.ds(3, 40, stride=4), :], 64 - 112), high_face)
+        for q in range(5):
+            faces = []
+            for bx in range(2):
+                parts = []
+                for by in range(2):
+                    base = bx * 4 + by * 2
+                    rows = pl.ds(3 * bx, 32, stride=4)
+                    if q < 4:
+                        above = s_ref[(base + 1) * 4 + q, rows, :]
+                        part = s_ref[base * 4 + q, rows, :] + jnp.where(z > 0, lroll(above, 1), 0.0)
+                    else:
+                        part = jnp.zeros((32, 128), F32)
+                        for k in range(4):
+                            above = s_ref[(base + 1) * 4 + k, rows, :]
+                            part = jnp.where(z == k, lroll(above, k - 15), part)
+                    parts.append(jnp.concatenate([part, pad], axis=0))
+                faces.append(parts[0] + sroll(parts[1], 1))
+            inside = (lane >> 4) == q if q < 4 else (lane >> 2) == 16
+            low_face = jnp.where(inside, lroll(faces[0], 16 * q), low_face)
+            high_face = jnp.where(inside, lroll(faces[1], 16 * q - 112), high_face)
         for c in range(3):
-            inside = ((lane40 >> 4) == 5 + c) & (iota((40, 128), 0) < 32)
-            face = jnp.concatenate(
-                [n_ref[c, pl.ds(0, 32, stride=4), :], jnp.zeros((8, 128), F32)], axis=0
-            )
+            inside = ((lane >> 4) == 5 + c) & (iota((40, 128), 0) < 32)
+            face = jnp.concatenate([n_ref[c, pl.ds(0, 32, stride=4), :], pad], axis=0)
             low_face = jnp.where(inside, lroll(face, 80 + 16 * c), low_face)
         xlo_ref[...] = low_face
         xhi_ref[...] = high_face
-        ylo_ref[...] = jnp.zeros((40, 128), F32)
-        yhi_ref[...] = jnp.zeros((40, 128), F32)
-        for q in range(5):
-            src = m_ref if q < 4 else zed_ref
+
+
+def plane_body(s_ref, n_ref, m_ref, ylo_ref, yhi_ref, zlo_ref, zhi_ref, edge_ref, zed_ref):
+    lane = iota((TILES, 128), 1)
+    row = iota((TILES, 128), 0)
+    z = lane & 15
+    x_in = lane >> 4
+    x_out = row & 3
+    last = (x_in == 7) & (x_out == 3)
+
+    def x_shift(plane):
+        rolled = lroll(plane, 16)
+        return jnp.where(
+            x_in > 0, rolled, jnp.where(x_out > 0, sroll(rolled, 1), 0.0)
+        )
+
+    for q in range(5):
+        for by in range(2):
+            parts = []
+            for bx in range(2):
+                base = bx * 4 + by * 2
+                if q < 4:
+                    above = s_ref[(base + 1) * 4 + q]
+                    parts.append(
+                        s_ref[base * 4 + q] + jnp.where(z > 0, lroll(above, 1), 0.0)
+                    )
+                else:
+                    rim = jnp.zeros((TILES, 128), F32)
+                    for k in range(4):
+                        rim = jnp.where(z == k, lroll(s_ref[(base + 1) * 4 + k], k - 15), rim)
+                    parts.append(rim)
+            main = parts[0] + x_shift(parts[1])
+            edge = jnp.where(last, parts[1], 0.0)
+            dst = m_ref if q < 4 else zed_ref
             at = q if q < 4 else 0
-            ylo_ref[4 * q : 4 * q + 4, :] = src[at, 0:4, :]
-            yhi_ref[4 * q : 4 * q + 4, :] = src[at, 128:132, :]
-        for c in range(3):
-            ylo_ref[20 + 4 * c : 24 + 4 * c, :] = n_ref[c, 0:4, :]
-        big = iota((ROWS, 128), 1)
-        slot = big & 15
-        low_z = jnp.zeros((ROWS, 128), F32)
-        for q in range(4):
-            low_z = jnp.where(slot == q, lroll(m_ref[q], q), low_z)
-        for c in range(3):
-            face = jnp.concatenate([n_ref[c], jnp.zeros((ROWS - TILES, 128), F32)], axis=0)
-            low_z = jnp.where(slot == 4 + c, lroll(face, 4 + c), low_z)
-        zlo_ref[...] = low_z
-        zhi_ref[...] = zed_ref[0]
+            if by == 0:
+                dst[at, 0:TILES, :] = main
+                dst[at, TILES:ROWS, :] = jnp.zeros((ROWS - TILES, 128), F32)
+                edge_ref[q, 0:TILES, :] = edge
+                edge_ref[q, TILES:ROWS, :] = jnp.zeros((ROWS - TILES, 128), F32)
+            else:
+                dst[at, 4:132, :] = dst[at, 4:132, :] + main
+                edge_ref[q, 4:132, :] = edge_ref[q, 4:132, :] + edge
+    ylo_ref[...] = jnp.zeros((40, 128), F32)
+    yhi_ref[...] = jnp.zeros((40, 128), F32)
+    for q in range(5):
+        src = m_ref if q < 4 else zed_ref
+        at = q if q < 4 else 0
+        ylo_ref[4 * q : 4 * q + 4, :] = src[at, 0:4, :]
+        yhi_ref[4 * q : 4 * q + 4, :] = src[at, 128:132, :]
+    for c in range(3):
+        ylo_ref[20 + 4 * c : 24 + 4 * c, :] = n_ref[c, 0:4, :]
+    big = iota((ROWS, 128), 1)
+    slot = big & 15
+    low_z = jnp.zeros((ROWS, 128), F32)
+    for q in range(4):
+        low_z = jnp.where(slot == q, lroll(m_ref[q], q), low_z)
+    for c in range(3):
+        face = jnp.concatenate([n_ref[c], jnp.zeros((ROWS - TILES, 128), F32)], axis=0)
+        low_z = jnp.where(slot == 4 + c, lroll(face, 4 + c), low_z)
+    zlo_ref[...] = low_z
+    zhi_ref[...] = zed_ref[0]
 
 
 def fold_x_body(xlo_ref, xhi_ref, from_low, from_high, ylo_ref, yhi_ref,
@@ -380,7 +393,7 @@
             up = sroll(lroll(plane, -size), size)
             plane = jnp.where(row_bit == lane_bit, plane, jnp.where(row_bit == 0, down, up))
         for part in range(8):
-            send_ref[part, 32 * c : 32 * c + 32, :] = plane[32 * (part % 4) : 32 * (part % 4) + 32]
+            send_ref[part, 64 * c : 64 * c + 64, :] = plane[64 * (part // 4) : 64 * (part // 4) + 64]
 
 
 def collide_body(start, shift_ref, v_ref, p_ref, view_ref, *refs):
@@ -440,14 +453,14 @@
 
 def z_tables():
     pos = np.arange(NZ)[None, :]
-    line = np.arange(32)[:, None]
-    halves = []
-    for half in range(2):
-        owner = line // 4 * 8 + half * 4 + line % 4
+    line = np.arange(16)[:, None]
+    quarters = []
+    for quarter in range(4):
+        owner = line // 2 * 8 + line % 2 * 4 + quarter
         for q in range(4):
             phase = (2 * owner + q // 2) * pos % NZ * (2.0 * np.pi / NZ)
-            halves.append(-np.sin(phase) if q % 2 else np.cos(phase))
-    return table_parts(np.concatenate(halves, axis=0).reshape(2, 128, NZ))
+            quarters.append(-np.sin(phase) if q % 2 else np.cos(phase))
+    return table_parts(np.concatenate(quarters, axis=0).reshape(4, 64, NZ))
 
 
 def y_tables():
@@ -484,20 +497,20 @@
 
 
 def z_body(first_ref, in_ref, fh_ref, fl_ref, out_ref):
-    lane = iota((32, 128), 1)
+    lane = iota((16, 128), 1)
     fh, fl = fh_ref[first_ref[2]], fl_ref[first_ref[2]]
     for c in range(3):
         data = jnp.concatenate(
             [
-                in_ref[:, 32 * c + 16 * r : 32 * c + 16 * r + 16, :].reshape(128, 128)
-                for r in range(2)
+                in_ref[:, 64 * c + 16 * r : 64 * c + 16 * r + 16, :].reshape(128, 128)
+                for r in range(4)
             ],
             axis=1,
         )
         high, low = split(data)
         res = dot(fh, high) + dot(fh, low) + dot(fl, high)
-        for r in range(2):
-            g = [res[32 * q : 32 * q + 32, 128 * r : 128 * r + 128] for q in range(4)]
+        for r in range(4):
+            g = [res[16 * q : 16 * q + 16, 128 * r : 128 * r + 128] for q in range(4)]
             for bit, size in ((2, 8), (1, 4)):
                 clear = (lane & size) == 0
                 new = list(g)
@@ -508,13 +521,13 @@
                         new[q | bit] = jnp.where(clear, lroll(a, -size), b)
                 g = new
             for k in range(4):
-                out_ref[pl.ds(8 * c + 4 * r + k, 32, stride=24), :] = g[k]
+                out_ref[pl.ds(16 * c + 4 * r + k, 16, stride=48), :] = g[k]
 
 
 def y_body(in_ref, fh_ref, fl_ref, out_ref):
-    both = in_ref[...].reshape(32, 24, 128)
+    both = in_ref[...].reshape(16, 48, 128)
     data = jnp.concatenate(
-        [both[:, 8 * c : 8 * c + 8].reshape(256, 128) for c in range(3)], axis=1
+        [both[:, 16 * c : 16 * c + 16].reshape(256, 128) for c in range(3)], axis=1
     )
     high, low = split(data)
     fh, fl = fh_ref[...], fl_ref[...]
@@ -620,22 +633,25 @@
     span = TILES * TILE * PPC // BLOCKS
     speed_spec = pl.BlockSpec((3, span), lambda i: (0, i))
     place_spec = pl.BlockSpec((640 // BLOCKS, 128), lambda i: (i, 0))
-    out_shapes = [(32, TILES, 128), (4, ROWS, 128), (3, TILES, 128)]
-    out_shapes += [(40, 128)] * 4 + [(ROWS, 128)] * 2
-    sums, main, normal, x_lo, x_hi, y_lo, y_hi, z_lo, z_hi = pl.pallas_call(
+    out_shapes = [(32, TILES, 128), (3, TILES, 128), (40, 128), (40, 128)]
+    sums, normal, x_lo, x_hi = pl.pallas_call(
         scatter_body,
         name="scatter",
         grid=(BLOCKS,),
         in_specs=[SMEM, speed_spec, place_spec, whole(TILES, 128)],
         out_specs=[whole(*s) for s in out_shapes],
         out_shape=[struct(*s) for s in out_shapes],
-        scratch_shapes=[
-            pltpu.VMEM((8 * SROW, 128), F32),
-            pltpu.VMEM((5, ROWS, 128), F32),
-            pltpu.VMEM((1, ROWS, 128), F32),
-        ],
+        scratch_shapes=[pltpu.VMEM((8 * SROW, 128), F32)],
         compiler_params=params(12),
     )(grid_shift, velocity, place, axis_index)
+    main, y_lo, y_hi, z_lo, z_hi = pl.pallas_call(
+        plane_body,
+        name="planes",
+        out_shape=[struct(4, ROWS, 128)] + [struct(40, 128)] * 2 + [struct(ROWS, 128)] * 2,
+        scratch_shapes=[pltpu.VMEM((5, ROWS, 128), F32), pltpu.VMEM((1, ROWS, 128), F32)],
+        compiler_params=params(12),
+        cost_estimate=pl.CostEstimate(flops=1_000_000_000, bytes_accessed=3_000_000, transcendentals=0),
+    )(sums, normal)
     below, above = ring((x_lo, x_hi), "gx")
     x_lo, x_hi, y_lo, y_hi = pl.pallas_call(
         fold_x_body, name="fold_x", out_shape=[struct(40, 128)] * 4, compiler_params=params(2)
@@ -649,7 +665,7 @@
     views, sent = pl.pallas_call(
         cell_body,
         name="cells",
-        out_shape=[struct(24, VROWS, 128), struct(8, 96, 128)],
+        out_shape=[struct(24, VROWS, 128), struct(8, 192, 128)],
         scratch_shapes=[
             pltpu.VMEM((7, ROWS, 128), F32),
             pltpu.VMEM((7, ROWS, 128), F32),
@@ -658,7 +674,7 @@
         compiler_params=params(12),
     )(sums, main, normal, x_lo, x_hi, y_lo, y_hi, z_lo, z_hi, below, above)
     first = jnp.stack(
-        [lax.axis_index(GY_GZ) * 2, lax.axis_index("gx") * 64, lax.axis_index("gz_0")]
+        [lax.axis_index(GY_GZ) * 2, lax.axis_index("gx") * 64, lax.axis_index("gz_1")]
     ).astype(jnp.int32)
     arrived = lax.all_to_all(sent, GZ, split_axis=0, concat_axis=0, tiled=True)
     updated = collide(0, EARLY, grid_shift, velocity, place, views, None)
@@ -672,7 +688,7 @@
         compiler_params=params(6),
     )(first, arrived, *z_tables())
     pencil = lax.all_to_all(
-        lines.reshape(32, 24, 128), ("gy_0", "gy_1", "gz_1"), split_axis=0, concat_axis=0, tiled=True
+        lines.reshape(16, 48, 128), ("gy_0", "gy_1", "gz_0"), split_axis=0, concat_axis=0, tiled=True
     )
     new_velocity = collide(EARLY, STEPS, grid_shift, velocity, place, views, updated)
     pencil, new_velocity = lax.optimization_barrier((pencil, new_velocity))

time: 116 us -> 115 us (level)
  starting transfers between devices: 28 us -> 24.3 us
  waiting for transfers between devices: 13.7 us -> 15.3 us
    all_to_all x1, starting transfers between devices: 10 us -> 6.39 us  [per_device(): lax.all_to_all(lines.reshape(16, 48, 128), ('gy_0', 'gy_1', 'gz_0'), spli...]
    all_to_all x1, blocking collectives: 13.7 us -> 15.8 us  [per_device(): lax.all_to_all(rows, 'gx', split_axis=0, concat_axis=0, tiled=True)]
    all_to_all x1, waiting for transfers between devices: 5.95 us -> 7.59 us  [per_device(): lax.all_to_all(lines.reshape(16, 48, 128), ('gy_0', 'gy_1', 'gz_0'), spli...]
    pallas_call x0 -> x1, Pallas kernels: none -> 1.42 us  [per_device(): pl.pallas_call(plane_body, name='planes', out_shape=[struct(4, ROWS, 128)...]
  transfers between devices with their start and end apart: 8 -> 8, of which waited for: 6 -> 5; matrix products, arithmetic and copies ran while one was open for 0% -> 0% of each run, Pallas kernels for 11% -> 13%
where the time goes in v2:
time: 115 us
  Pallas kernels  34.2 us (30%)
  blocking collectives  33 us (29%)
  starting transfers between devices  24.3 us (21%)
  waiting for transfers between devices  15.3 us (13%)
  local copies, waits for them, and re-layouts  6.57 us (6%)
    all_to_all x1, blocking collectives, gathered_sum(): lax.all_to_all(copies, axes, split_axis=0, concat_axis=0, tiled=True)  17.2 us
    all_to_all x1, blocking collectives, per_device(): lax.all_to_all(rows, 'gx', split_axis=0, concat_axis=0, tiled=True)  15.8 us
    pallas_call x2, Pallas kernels, collide(): pl.pallas_call(lambda *refs: collide_body(start, *refs), name='collide',...  13 us
    pallas_call x1, Pallas kernels, per_device(): pl.pallas_call(scatter_body, name='scatter', grid=(BLOCKS,), in_specs=[SM...  10.6 us
    ppermute x3, starting transfers between devices, ring(): lax.ppermute(high, axis, forward)  8.32 us
    all_to_all x1, waiting for transfers between devices, per_device(): lax.all_to_all(lines.reshape(16, 48, 128), ('gy_0', 'gy_1', 'gz_0'), spli...  7.59 us
    all_to_all x1, starting transfers between devices, per_device(): lax.all_to_all(lines.reshape(16, 48, 128), ('gy_0', 'gy_1', 'gz_0'), spli...  6.39 us
    unnamed x29, local copies, waits for them, and re-layouts  6.37 us
  transfers between devices with their start and end apart: 8, of which 5 were waited for; matrix products, arithmetic and copies ran while one was open for 0% of the time, Pallas kernels for 13%

profile of v2, /device:TPU:1, one launch (start us, length us, event | category | flops | bytes accessed | tf_op | source)
XLA Modules:
  0.0 114.7 jit_solution(4487728346611942346)
XLA Ops:
  0.7 1.3 %copy.18 = s32[32,32,16]{2,1,0:T(8,128)S(1)} copy(s32[32,32,16]{1,2,0:T(8,128)} %param.14) | data formatting | bytes 131072 | tf_op args[3]
  1.9 0.2 reshape.23.axis_ref
  2.1 1.0 copy-done.4
  3.1 10.6 %scatter.1 = (f32[32,128,128]{2,1,0:T(8,128)S(1)}, f32[3,128,128]{2,1,0:T(8,128)S(1)}, f32[40,128]{1,0:T(8,128)S(1)}, f32[40,128]{1,0:T(8,128)S(1)}) custom-call(s32[3]{0:T(128)S(1)} %copy-done.12, f32[3,81920]{1,0:T(4,128)S(1)} %copy-done, s32[640,128]{1,0:T(8,128)S(1)} %bitcast.12, s32[128,128]{1,0:T(8,128)S(1)} %reshape.23.axis_ref), custom_call_target="tpu_custom_call" | custom-call | tf_op jit(solution)/shard_map/scatter/pallas_call | solution.py:637
  13.7 2.1 %collective-permute-start = (f32[40,128]{1,0:T(8,128)S(1)}, f32[40,128]{1,0:T(8,128)S(1)}, u32[]{:S(2)}, u32[]{:S(2)}) collective-permute-start(f32[40,128]{1,0:T(8,128)S(1)} %get-tuple-element.32.xhi_ref), channel_id=1, source_target_pairs={{0,64},{64,128},{128,192},{192,0},{1,65},{65,129},{129,193},{193,1... | collective-permute-start | bytes 61448 | tf_op jit(solution)/shard_map/ppermute | solution.py:591
  15.8 1.3 %collective-permute-start.1 = (f32[40,128]{1,0:T(8,128)S(1)}, f32[40,128]{1,0:T(8,128)S(1)}, u32[]{:S(2)}, u32[]{:S(2)}) collective-permute-start(f32[40,128]{1,0:T(8,128)S(1)} %get-tuple-element.31.xlo_ref), channel_id=1, source_target_pairs={{64,0},{128,64},{192,128},{0,192},{65,1},{129,65},{193,129},{1,193... | collective-permute-start | bytes 61448 | tf_op jit(solution)/shard_map/ppermute | solution.py:591
  17.2 1.4 %planes.1 = (f32[4,160,128]{2,1,0:T(8,128)S(1)}, f32[40,128]{1,0:T(8,128)S(1)}, f32[40,128]{1,0:T(8,128)S(1)}, f32[160,128]{1,0:T(8,128)S(1)}, f32[160,128]{1,0:T(8,128)S(1)}) custom-call(f32[32,128,128]{2,1,0:T(8,128)S(1)} %get-tuple-element.28.s_ref, f32[3,128,128]{2,1,0:T(8,128)S(1)} %get-tuple-element.29.n_ref), custom_call_target="tpu_custom_call" | custom-call | flops 1000000000 | bytes 3000000 | tf_op jit(solution)/shard_map/planes/pallas_call | solution.py:647
  18.6 0.1 fold_x.1
  18.7 4.8 %collective-permute-start.2 = (f32[40,128]{1,0:T(8,128)S(1)}, f32[40,128]{1,0:T(8,128)S(1)}, u32[]{:S(2)}, u32[]{:S(2)}) collective-permute-start(f32[40,128]{1,0:T(8,128)S(1)} %get-tuple-element.38.yhi_ref), channel_id=1, source_target_pairs={{0,8},{8,16},{16,24},{24,32},{32,40},{40,48},{48,56},{56,0},{1,9},... | collective-permute-start | bytes 61448 | tf_op jit(solution)/shard_map/ppermute | solution.py:591
  23.5 0.9 collective-permute-done.2.from_low
  24.4 3.3 %collective-permute-done.3.from_high = f32[40,128]{1,0:T(8,128)S(1)} collective-permute-done((f32[40,128]{1,0:T(8,128)S(1)}, f32[40,128]{1,0:T(8,128)S(1)}, u32[]{:S(2)}, u32[]{:S(2)}) %collective-permute-start.3) | collective-permute-done | bytes 20512 | tf_op jit(solution)/shard_map/ppermute | solution.py:591
  27.7 0.2 fold_y.1
  27.9 1.4 %collective-permute-start.4 = (f32[160,128]{1,0:T(8,128)S(1)}, f32[160,128]{1,0:T(8,128)S(1)}, u32[]{:S(2)}, u32[]{:S(2)}) collective-permute-start(f32[160,128]{1,0:T(8,128)S(1)} %get-tuple-element.44.zhi_ref), channel_id=1, source_target_pairs={{0,1},{1,2},{2,3},{3,4},{4,5},{5,6},{6,7},{7,0},{8,9},{9,10},{10,1... | collective-permute-start | bytes 245768 | tf_op jit(solution)/shard_map/ppermute | solution.py:591
  29.2 2.8 %collective-permute-start.5 = (f32[160,128]{1,0:T(8,128)S(1)}, f32[160,128]{1,0:T(8,128)S(1)}, u32[]{:S(2)}, u32[]{:S(2)}) collective-permute-start(f32[160,128]{1,0:T(8,128)S(1)} %get-tuple-element.43.zlo_ref), channel_id=1, source_target_pairs={{1,0},{2,1},{3,2},{4,3},{5,4},{6,5},{7,6},{0,7},{9,8},{10,9},{11,1... | collective-permute-start | bytes 245768 | tf_op jit(solution)/shard_map/ppermute | solution.py:591
  32.1 2.4 %collective-permute-done.4.from_low = f32[160,128]{1,0:T(8,128)S(1)} collective-permute-done((f32[160,128]{1,0:T(8,128)S(1)}, f32[160,128]{1,0:T(8,128)S(1)}, u32[]{:S(2)}, u32[]{:S(2)}) %collective-permute-start.4) | collective-permute-done | bytes 81952 | tf_op jit(solution)/shard_map/ppermute | solution.py:591
  34.4 4.3 %cells.1 = (f32[24,136,128]{2,1,0:T(8,128)S(1)}, f32[8,192,128]{2,1,0:T(8,128)}) custom-call(f32[32,128,128]{2,1,0:T(8,128)S(1)} %get-tuple-element.28.s_ref, f32[4,160,128]{2,1,0:T(8,128)S(1)} %get-tuple-element.30.m_ref, f32[3,128,128]{2,1,0:T(8,128)S(1)} %get-tuple-element.29.n_ref, f32[40,128]{1,0:T(8,128)S(1)} %get-tuple-element.35.xlo_ref, ...), custom_call_target="tpu_custom_call" | custom-call | tf_op jit(solution)/shard_map/cells/pallas_call | solution.py:665
  38.7 1.2 %copy-done.1 = f32[24,136,128]{2,1,0:T(8,128)} copy-done((f32[24,136,128]{2,1,0:T(8,128)}, f32[24,136,128]{2,1,0:T(8,128)S(1)}, u32[]{:S(2)}) %copy-start.1) | copy-done | bytes 1671192
  40.0 5.5 %all-to-all-start = ((f32[8,192,128]{2,1,0:T(8,128)}), f32[8,192,128]{2,1,0:T(8,128)S(1)}, u32[]{:S(2)}, u32[]{:S(2)}) async-start(f32[8,192,128]{2,1,0:T(8,128)} %get-tuple-element.45), calls=%async_computation | async-start | bytes 1572864 | tf_op jit(solution)/shard_map/all_to_all | solution.py:679
  45.4 0.1 pad_add_fusion.first_ref
  45.5 1.4 %copy-done.2 = f32[24,136,128]{2,1,0:T(8,128)S(1)} copy-done((f32[24,136,128]{2,1,0:T(8,128)S(1)}, f32[24,136,128]{2,1,0:T(8,128)}, u32[]{:S(2)}) %copy-start.2) | copy-done | bytes 1671192
  46.9 9.2 %collide.2.refs_4_ = f32[3,81920]{1,0:T(4,128)} custom-call(s32[3]{0:T(128)S(1)} %copy-done.12, f32[3,81920]{1,0:T(4,128)S(1)} %copy-done, s32[640,128]{1,0:T(8,128)S(1)} %bitcast.13, f32[24,136,128]{2,1,0:T(8,128)S(1)} %copy-done.2), custom_call_target="tpu_custom_call" | custom-call | flops 4800000000 | bytes 4000000 | tf_op jit(solution)/shard_map/collide/pallas_call | solution.py:613
  56.1 1.1 all-to-all-done.in_ref
  57.2 1.8 %z_lines.1 = f32[768,128]{1,0:T(8,128)} custom-call(s32[3]{0:T(128)S(1)} %pad_add_fusion.first_ref, f32[8,192,128]{2,1,0:T(8,128)S(1)} %all-to-all-done.in_ref, bf16[4,64,128]{2,1,0:T(8,128)(2,1)S(1)} %copy-done.10, bf16[4,64,128]{2,1,0:T(8,128)(2,1)S(1)} %copy-done.11), custom_call_target="tpu_custom_call" | custom-call | tf_op jit(solution)/shard_map/z_lines/pallas_call | solution.py:683
  59.0 6.4 %all-to-all-start.1 = ((f32[16,48,128]{2,1,0:T(8,128)}), f32[16,48,128]{2,1,0:T(8,128)S(1)}, u32[]{:S(2)}, u32[]{:S(2)}) async-start(f32[16,48,128]{2,1,0:T(8,128)} %bitcast.4), calls=%async_computation.1 | async-start | bytes 786432 | tf_op jit(solution)/shard_map/all_to_all | solution.py:690
  65.4 1.4 %copy-done.3 = f32[24,136,128]{2,1,0:T(8,128)S(1)} copy-done((f32[24,136,128]{2,1,0:T(8,128)S(1)}, f32[24,136,128]{2,1,0:T(8,128)}, u32[]{:S(2)}) %copy-start.3) | copy-done | bytes 1671192
  66.9 3.9 %collide.3 = f32[3,81920]{1,0:T(4,128)} custom-call(s32[3]{0:T(128)S(1)} %copy-done.12, f32[3,81920]{1,0:T(4,128)S(1)} %copy-done, s32[640,128]{1,0:T(8,128)S(1)} %bitcast.14, f32[24,136,128]{2,1,0:T(8,128)S(1)} %copy-done.3, f32[3,81920]{1,0:T(4,128)} %collide.2.refs_4_), custom_call_target="tpu_custom_call", output_to_operand_aliasing={{}: (4, {})} | custom-call | flops 1600000000 | bytes 4000000 | tf_op jit(solution)/shard_map/collide/pallas_call | solution.py:613
  70.7 7.6 %all-to-all-done.1 = f32[16,48,128]{2,1,0:T(8,128)S(1)} async-done(((f32[16,48,128]{2,1,0:T(8,128)}), f32[16,48,128]{2,1,0:T(8,128)S(1)}, u32[]{:S(2)}, u32[]{:S(2)}) %all-to-all-start.1) | async-done | bytes 393248 | tf_op jit(solution)/shard_map/all_to_all | solution.py:690
  78.3 0.8 y_lines.1
  79.1 15.8 %all_to_all.20.in_ref = f32[4,384,128]{2,1,0:T(8,128)S(1)} all-to-all(f32[4,384,128]{2,1,0:T(8,128)S(1)} %y_lines.1), channel_id=1, replica_groups=mesh['gx'=4,'gy_0'=4,'gy_1'=2,'gz_0'=2,'gz_1'=4] {'gx'}, dimensions={0} | all-to-all | bytes 1572864 | tf_op jit(solution)/shard_map/all_to_all | solution.py:698
  94.9 2.0 %x_lines.1 = (f32[2,3,2,64,128]{4,3,2,1,0:T(8,128)}, f32[1,128]{1,0:T(1,128)S(1)}) custom-call(s32[3]{0:T(128)S(1)} %pad_add_fusion.first_ref, f32[4,384,128]{2,1,0:T(8,128)S(1)} %all_to_all.20.in_ref, bf16[512,512]{1,0:T(8,128)(2,1)S(1)} %copy-done.6, bf16[512,512]{1,0:T(8,128)(2,1)S(1)} %copy-done.7), custom_call_target="tpu_custom_call" | custom-call | tf_op jit(solution)/shard_map/x_lines/pallas_call | solution.py:699
  97.0 17.2 %all_to_all.21 = f32[64,1,128]{2,1,0:T(1,128)S(1)} all-to-all(f32[64,1,128]{2,1,0:T(1,128)S(1)} %broadcast_in_dim.9), channel_id=1, replica_groups=mesh['gx'=4,'gy_0'=4,'gy_1'=2,'gz_0'=2,'gz_1'=4] {'gy_0','gy_1','gz_0','..., dimensions={0} | all-to-all | bytes 65536 | tf_op jit(solution)/shard_map/all_to_all | solution.py:597
  114.2 0.5 multiply_bitcast_fusion
  (30 shorter events, 0.1 us)
Async XLA Ops:
  0.6 1.5 %copy-start = (f32[3,81920]{1,0:T(4,128)S(1)}, f32[3,81920]{1,0:T(4,128)}, u32[]{:S(2)}) copy-start(f32[3,81920]{1,0:T(4,128)} %refs_1_.3) | copy-start | bytes 2949124
  0.6 1.5 %copy-start.12 = (s32[3]{0:T(128)S(1)}, s32[3]{0:T(128)}, u32[]{:S(2)}) copy-start(s32[3]{0:T(128)} %refs_0_.3) | copy-start | bytes 40
  2.1 1.0 copy-start.4
  13.7 4.9 %collective-permute-start = (f32[40,128]{1,0:T(8,128)S(1)}, f32[40,128]{1,0:T(8,128)S(1)}, u32[]{:S(2)}, u32[]{:S(2)}) collective-permute-start(f32[40,128]{1,0:T(8,128)S(1)} %get-tuple-element.32.xhi_ref), channel_id=1, source_target_pairs={{0,64},{64,128},{128,192},{192,0},{1,65},{65,129},{129,193},{193,1... | collective-permute-start | bytes 61448 | tf_op jit(solution)/shard_map/ppermute | solution.py:591
  15.8 2.8 %collective-permute-start.1 = (f32[40,128]{1,0:T(8,128)S(1)}, f32[40,128]{1,0:T(8,128)S(1)}, u32[]{:S(2)}, u32[]{:S(2)}) collective-permute-start(f32[40,128]{1,0:T(8,128)S(1)} %get-tuple-element.31.xlo_ref), channel_id=1, source_target_pairs={{64,0},{128,64},{192,128},{0,192},{65,1},{129,65},{193,129},{1,193... | collective-permute-start | bytes 61448 | tf_op jit(solution)/shard_map/ppermute | solution.py:591
  18.7 5.7 %collective-permute-start.2 = (f32[40,128]{1,0:T(8,128)S(1)}, f32[40,128]{1,0:T(8,128)S(1)}, u32[]{:S(2)}, u32[]{:S(2)}) collective-permute-start(f32[40,128]{1,0:T(8,128)S(1)} %get-tuple-element.38.yhi_ref), channel_id=1, source_target_pairs={{0,8},{8,16},{16,24},{24,32},{32,40},{40,48},{48,56},{56,0},{1,9},... | collective-permute-start | bytes 61448 | tf_op jit(solution)/shard_map/ppermute | solution.py:591
  23.5 4.2 %collective-permute-start.3 = (f32[40,128]{1,0:T(8,128)S(1)}, f32[40,128]{1,0:T(8,128)S(1)}, u32[]{:S(2)}, u32[]{:S(2)}) collective-permute-start(f32[40,128]{1,0:T(8,128)S(1)} %get-tuple-element.37.ylo_ref), channel_id=1, source_target_pairs={{8,0},{16,8},{24,16},{32,24},{40,32},{48,40},{56,48},{0,56},{9,1},... | collective-permute-start | bytes 61448 | tf_op jit(solution)/shard_map/ppermute | solution.py:591
  27.9 6.5 %collective-permute-start.4 = (f32[160,128]{1,0:T(8,128)S(1)}, f32[160,128]{1,0:T(8,128)S(1)}, u32[]{:S(2)}, u32[]{:S(2)}) collective-permute-start(f32[160,128]{1,0:T(8,128)S(1)} %get-tuple-element.44.zhi_ref), channel_id=1, source_target_pairs={{0,1},{1,2},{2,3},{3,4},{4,5},{5,6},{6,7},{7,0},{8,9},{9,10},{10,1... | collective-permute-start | bytes 245768 | tf_op jit(solution)/shard_map/ppermute | solution.py:591
  29.2 5.2 %collective-permute-start.5 = (f32[160,128]{1,0:T(8,128)S(1)}, f32[160,128]{1,0:T(8,128)S(1)}, u32[]{:S(2)}, u32[]{:S(2)}) collective-permute-start(f32[160,128]{1,0:T(8,128)S(1)} %get-tuple-element.43.zlo_ref), channel_id=1, source_target_pairs={{1,0},{2,1},{3,2},{4,3},{5,4},{6,5},{7,6},{0,7},{9,8},{10,9},{11,1... | collective-permute-start | bytes 245768 | tf_op jit(solution)/shard_map/ppermute | solution.py:591
  38.7 1.2 %copy-start.1 = (f32[24,136,128]{2,1,0:T(8,128)}, f32[24,136,128]{2,1,0:T(8,128)S(1)}, u32[]{:S(2)}) copy-start(f32[24,136,128]{2,1,0:T(8,128)S(1)} %get-tuple-element.46.refs_3_) | copy-start | bytes 5013508
  39.9 5.5 %copy-start.5 = (s32[81920]{0:T(1024)S(1)}, s32[81920]{0:T(1024)}, u32[]{:S(2)}) copy-start(s32[81920]{0:T(1024)} %param.12) | copy-start | bytes 983044
  40.0 17.3 %all-to-all-start = ((f32[8,192,128]{2,1,0:T(8,128)}), f32[8,192,128]{2,1,0:T(8,128)S(1)}, u32[]{:S(2)}, u32[]{:S(2)}) async-start(f32[8,192,128]{2,1,0:T(8,128)} %get-tuple-element.45), calls=%async_computation | async-start | bytes 1572864 | tf_op jit(solution)/shard_map/all_to_all | solution.py:679
  45.5 1.4 %copy-start.2 = (f32[24,136,128]{2,1,0:T(8,128)S(1)}, f32[24,136,128]{2,1,0:T(8,128)}, u32[]{:S(2)}) copy-start(f32[24,136,128]{2,1,0:T(8,128)} %copy-done.1) | copy-start | bytes 5013508
  46.9 10.3 %copy-start.10 = (bf16[4,64,128]{2,1,0:T(8,128)(2,1)S(1)}, bf16[4,64,128]{2,1,0:T(8,128)(2,1)}, u32[]{:S(2)}) copy-start(bf16[4,64,128]{2,1,0:T(8,128)(2,1)} %constant.46.clone.fh_ref) | copy-start | bytes 196612
  46.9 10.3 %copy-start.11 = (bf16[4,64,128]{2,1,0:T(8,128)(2,1)S(1)}, bf16[4,64,128]{2,1,0:T(8,128)(2,1)}, u32[]{:S(2)}) copy-start(bf16[4,64,128]{2,1,0:T(8,128)(2,1)} %constant.47.clone.fl_ref) | copy-start | bytes 196612
  59.0 19.3 %all-to-all-start.1 = ((f32[16,48,128]{2,1,0:T(8,128)}), f32[16,48,128]{2,1,0:T(8,128)S(1)}, u32[]{:S(2)}, u32[]{:S(2)}) async-start(f32[16,48,128]{2,1,0:T(8,128)} %bitcast.4), calls=%async_computation.1 | async-start | bytes 786432 | tf_op jit(solution)/shard_map/all_to_all | solution.py:690
  65.4 1.4 %copy-start.3 = (f32[24,136,128]{2,1,0:T(8,128)S(1)}, f32[24,136,128]{2,1,0:T(8,128)}, u32[]{:S(2)}) copy-start(f32[24,136,128]{2,1,0:T(8,128)} %copy-done.1) | copy-start | bytes 5013508
  66.9 11.5 %copy-start.8 = (bf16[512,256]{1,0:T(8,128)(2,1)S(1)}, bf16[512,256]{1,0:T(8,128)(2,1)}, u32[]{:S(2)}) copy-start(bf16[512,256]{1,0:T(8,128)(2,1)} %constant.48.clone.fh_ref) | copy-start | bytes 786436
  66.9 11.5 %copy-start.9 = (bf16[512,256]{1,0:T(8,128)(2,1)S(1)}, bf16[512,256]{1,0:T(8,128)(2,1)}, u32[]{:S(2)}) copy-start(bf16[512,256]{1,0:T(8,128)(2,1)} %constant.49.clone.fl_ref) | copy-start | bytes 786436
  78.3 16.6 %copy-start.6 = (bf16[512,512]{1,0:T(8,128)(2,1)S(1)}, bf16[512,512]{1,0:T(8,128)(2,1)}, u32[]{:S(2)}) copy-start(bf16[512,512]{1,0:T(8,128)(2,1)} %constant.50.clone.fh_ref) | copy-start | bytes 1572868
  78.3 16.6 %copy-start.7 = (bf16[512,512]{1,0:T(8,128)(2,1)S(1)}, bf16[512,512]{1,0:T(8,128)(2,1)}, u32[]{:S(2)}) copy-start(bf16[512,512]{1,0:T(8,128)(2,1)} %constant.51.clone.fl_ref) | copy-start | bytes 1572868
  94.9 19.2 %copy-start.13 = (f32[1,64]{1,0:T(1,128)S(1)}, f32[1,64]{1,0:T(1,128)}, u32[]{:S(2)}) copy-start(f32[1,64]{1,0:T(1,128)} %constant.54) | copy-start | bytes 772

commit v3 on v2

--- a/solution.py
+++ b/solution.py
@@ -539,7 +539,9 @@
         out = even + jnp.where(is_real, lroll(odd, -4), -lroll(odd, 4))
         for d in range(4):
             out_ref[d, 64 * c : 64 * c + 64, :] = out[64 * d : 64 * d + 64]
-            out_ref[d, 192 + 64 * c : 256 + 64 * c, :] = out[0:64]
+            out_ref[d, 192 + 8 * c : 200 + 8 * c, :] = out[0:8]
+    for d in range(4):
+        out_ref[d, 216:224, :] = jnp.zeros((8, 128), F32)
 
 
 def x_body(first_ref, in_ref, fh_ref, fl_ref, out_ref, shell_ref, sums_ref):
@@ -547,24 +549,30 @@
     high, low = split(data)
     fh, fl = fh_ref[...], fl_ref[...]
     res = dot(high, fh) + dot(low, fh) + dot(high, fl)
-    ky = iota((64, 128), 0)
     kx = iota((64, 128), 1)
     kx = jnp.where(kx >= NX // 2, kx - NX, kx)
+    ky = first_ref[1] + iota((64, 128), 0)
+    ky = jnp.where(ky >= NY // 2, ky - NY, ky)
     plane = ky * ky + kx * kx
     weight = jnp.where(ky == 0, 1.0, 2.0)
+    extra_row = (iota((8, 128), 0) == 0) & (first_ref[1] == 3 * NY // 4)
+    extra_plane = kx[0:8] * kx[0:8]
     energy, square = [], []
     for kz in range(2):
         total = jnp.zeros((64, 128), F32)
+        extra = jnp.zeros((8, 128), F32)
         for part in range(2):
             for c in range(3):
                 here = slice(256 * part + 128 * kz, 256 * part + 128 * kz + 128)
-                out_ref[part, c, kz] = res[64 * c : 64 * c + 64, here]
-                block = res[192 + 64 * c : 256 + 64 * c, here]
+                block = res[64 * c : 64 * c + 64, here]
+                out_ref[part, c, kz] = block
                 total += block * block
+                block = res[192 + 8 * c : 200 + 8 * c, here]
+                extra += block * block
         wave = first_ref[0] + kz
         wave = jnp.where(wave >= NZ // 2, wave - NZ, wave)
-        energy.append(total * weight)
-        square.append(plane + wave * wave)
+        energy += [total * weight, jnp.where(extra_row, extra, 0.0)]
+        square += [plane + wave * wave, extra_plane + wave * wave]
     energy = jnp.concatenate(energy, axis=0)
     square = jnp.concatenate(square, axis=0)
     for s in range(NSHELL):
@@ -692,7 +700,7 @@
     )
     new_velocity = collide(EARLY, STEPS, grid_shift, velocity, place, views, updated)
     pencil, new_velocity = lax.optimization_barrier((pencil, new_velocity))
-    rows = pl.pallas_call(y_body, name="y_lines", out_shape=struct(4, 384, 128), compiler_params=params(12))(
+    rows = pl.pallas_call(y_body, name="y_lines", out_shape=struct(4, 224, 128), compiler_params=params(12))(
         pencil.reshape(768, 128), *y_tables()
     )
     columns = lax.all_to_all(rows, "gx", split_axis=0, concat_axis=0, tiled=True)
@@ -705,6 +713,9 @@
         compiler_params=params(12),
     )(first, columns, *x_tables())
     total = gathered_sum(shells, GY_GZ)
+    passed = lax.ppermute(total, "gx", [(0, 1), (3, 2)])
+    x_part = lax.axis_index("gx")
+    total = jnp.where((x_part == 1) | (x_part == 2), passed, total)
     spectrum = total[0, :NSHELL] / shell_counts()
     return new_velocity, modes, spectrum
 

time: 115 us -> 115 us (level)
  blocking collectives: 33 us -> 29.4 us
  starting transfers between devices: 24.3 us -> 26.5 us
    all_to_all x1, blocking collectives: 15.8 us -> 12.5 us  [per_device(): lax.all_to_all(rows, 'gx', split_axis=0, concat_axis=0, tiled=True)]
    ppermute x0 -> x1, starting transfers between devices: none -> 2.18 us  [per_device(): passed = lax.ppermute(total, 'gx', [(0, 1), (3, 2)])]
  transfers between devices with their start and end apart: 8 -> 9, of which waited for: 5 -> 6; matrix products, arithmetic and copies ran while one was open for 0% -> 0% of each run, Pallas kernels for 13% -> 13%
where the time goes in v3:
time: 115 us; the launch traced here: 114 us
  Pallas kernels  33.9 us (29%)
  blocking collectives  29.4 us (26%)
  starting transfers between devices  26.5 us (23%)
  waiting for transfers between devices  16 us (14%)
  local copies, waits for them, and re-layouts  6.57 us (6%)
    all_to_all x1, blocking collectives, gathered_sum(): lax.all_to_all(copies, axes, split_axis=0, concat_axis=0, tiled=True)  17 us
    pallas_call x2, Pallas kernels, collide(): pl.pallas_call(lambda *refs: collide_body(start, *refs), name='collide',...  13 us
    all_to_all x1, blocking collectives, per_device(): lax.all_to_all(rows, 'gx', split_axis=0, concat_axis=0, tiled=True)  12.5 us
    pallas_call x1, Pallas kernels, per_device(): pl.pallas_call(scatter_body, name='scatter', grid=(BLOCKS,), in_specs=[SM...  10.6 us
    ppermute x3, starting transfers between devices, ring(): lax.ppermute(high, axis, forward)  8.32 us
    all_to_all x1, waiting for transfers between devices, per_device(): lax.all_to_all(lines.reshape(16, 48, 128), ('gy_0', 'gy_1', 'gz_0'), spli...  7.59 us
    all_to_all x1, starting transfers between devices, per_device(): lax.all_to_all(lines.reshape(16, 48, 128), ('gy_0', 'gy_1', 'gz_0'), spli...  6.38 us
    unnamed x29, local copies, waits for them, and re-layouts  6.36 us
  transfers between devices with their start and end apart: 9, of which 6 were waited for; matrix products, arithmetic and copies ran while one was open for 0% of the time, Pallas kernels for 13%

profile of v3, /device:TPU:1, one launch (start us, length us, event | category | flops | bytes accessed | tf_op | source)
XLA Modules:
  0.0 113.8 jit_solution(17773874241199626177)
XLA Ops:
  0.7 1.3 %copy.18 = s32[32,32,16]{2,1,0:T(8,128)S(1)} copy(s32[32,32,16]{1,2,0:T(8,128)} %param.14) | data formatting | bytes 131072 | tf_op args[3]
  1.9 0.2 reshape.23.axis_ref
  2.1 1.0 copy-done.4
  3.1 10.6 %scatter.1 = (f32[32,128,128]{2,1,0:T(8,128)S(1)}, f32[3,128,128]{2,1,0:T(8,128)S(1)}, f32[40,128]{1,0:T(8,128)S(1)}, f32[40,128]{1,0:T(8,128)S(1)}) custom-call(s32[3]{0:T(128)S(1)} %copy-done.12, f32[3,81920]{1,0:T(4,128)S(1)} %copy-done, s32[640,128]{1,0:T(8,128)S(1)} %bitcast.13, s32[128,128]{1,0:T(8,128)S(1)} %reshape.23.axis_ref), custom_call_target="tpu_custom_call" | custom-call | tf_op jit(solution)/shard_map/scatter/pallas_call | solution.py:645
  13.7 2.1 %collective-permute-start = (f32[40,128]{1,0:T(8,128)S(1)}, f32[40,128]{1,0:T(8,128)S(1)}, u32[]{:S(2)}, u32[]{:S(2)}) collective-permute-start(f32[40,128]{1,0:T(8,128)S(1)} %get-tuple-element.32.xhi_ref), channel_id=1, source_target_pairs={{0,64},{64,128},{128,192},{192,0},{1,65},{65,129},{129,193},{193,1... | collective-permute-start | bytes 61448 | tf_op jit(solution)/shard_map/ppermute | solution.py:599
  15.8 1.3 %collective-permute-start.1 = (f32[40,128]{1,0:T(8,128)S(1)}, f32[40,128]{1,0:T(8,128)S(1)}, u32[]{:S(2)}, u32[]{:S(2)}) collective-permute-start(f32[40,128]{1,0:T(8,128)S(1)} %get-tuple-element.31.xlo_ref), channel_id=1, source_target_pairs={{64,0},{128,64},{192,128},{0,192},{65,1},{129,65},{193,129},{1,193... | collective-permute-start | bytes 61448 | tf_op jit(solution)/shard_map/ppermute | solution.py:599
  17.2 1.4 %planes.1 = (f32[4,160,128]{2,1,0:T(8,128)S(1)}, f32[40,128]{1,0:T(8,128)S(1)}, f32[40,128]{1,0:T(8,128)S(1)}, f32[160,128]{1,0:T(8,128)S(1)}, f32[160,128]{1,0:T(8,128)S(1)}) custom-call(f32[32,128,128]{2,1,0:T(8,128)S(1)} %get-tuple-element.28.s_ref, f32[3,128,128]{2,1,0:T(8,128)S(1)} %get-tuple-element.29.n_ref), custom_call_target="tpu_custom_call" | custom-call | flops 1000000000 | bytes 3000000 | tf_op jit(solution)/shard_map/planes/pallas_call | solution.py:655
  18.7 4.8 %collective-permute-start.2 = (f32[40,128]{1,0:T(8,128)S(1)}, f32[40,128]{1,0:T(8,128)S(1)}, u32[]{:S(2)}, u32[]{:S(2)}) collective-permute-start(f32[40,128]{1,0:T(8,128)S(1)} %get-tuple-element.38.yhi_ref), channel_id=1, source_target_pairs={{0,8},{8,16},{16,24},{24,32},{32,40},{40,48},{48,56},{56,0},{1,9},... | collective-permute-start | bytes 61448 | tf_op jit(solution)/shard_map/ppermute | solution.py:599
  23.5 0.9 collective-permute-done.2.from_low
  24.4 3.3 %collective-permute-done.3.from_high = f32[40,128]{1,0:T(8,128)S(1)} collective-permute-done((f32[40,128]{1,0:T(8,128)S(1)}, f32[40,128]{1,0:T(8,128)S(1)}, u32[]{:S(2)}, u32[]{:S(2)}) %collective-permute-start.3) | collective-permute-done | bytes 20512 | tf_op jit(solution)/shard_map/ppermute | solution.py:599
  27.7 0.2 fold_y.1
  27.9 1.4 %collective-permute-start.4 = (f32[160,128]{1,0:T(8,128)S(1)}, f32[160,128]{1,0:T(8,128)S(1)}, u32[]{:S(2)}, u32[]{:S(2)}) collective-permute-start(f32[160,128]{1,0:T(8,128)S(1)} %get-tuple-element.44.zhi_ref), channel_id=1, source_target_pairs={{0,1},{1,2},{2,3},{3,4},{4,5},{5,6},{6,7},{7,0},{8,9},{9,10},{10,1... | collective-permute-start | bytes 245768 | tf_op jit(solution)/shard_map/ppermute | solution.py:599
  29.2 2.8 %collective-permute-start.5 = (f32[160,128]{1,0:T(8,128)S(1)}, f32[160,128]{1,0:T(8,128)S(1)}, u32[]{:S(2)}, u32[]{:S(2)}) collective-permute-start(f32[160,128]{1,0:T(8,128)S(1)} %get-tuple-element.43.zlo_ref), channel_id=1, source_target_pairs={{1,0},{2,1},{3,2},{4,3},{5,4},{6,5},{7,6},{0,7},{9,8},{10,9},{11,1... | collective-permute-start | bytes 245768 | tf_op jit(solution)/shard_map/ppermute | solution.py:599
  32.1 2.4 %collective-permute-done.4.from_low = f32[160,128]{1,0:T(8,128)S(1)} collective-permute-done((f32[160,128]{1,0:T(8,128)S(1)}, f32[160,128]{1,0:T(8,128)S(1)}, u32[]{:S(2)}, u32[]{:S(2)}) %collective-permute-start.4) | collective-permute-done | bytes 81952 | tf_op jit(solution)/shard_map/ppermute | solution.py:599
  34.4 4.3 %cells.1 = (f32[24,136,128]{2,1,0:T(8,128)S(1)}, f32[8,192,128]{2,1,0:T(8,128)}) custom-call(f32[32,128,128]{2,1,0:T(8,128)S(1)} %get-tuple-element.28.s_ref, f32[4,160,128]{2,1,0:T(8,128)S(1)} %get-tuple-element.30.m_ref, f32[3,128,128]{2,1,0:T(8,128)S(1)} %get-tuple-element.29.n_ref, f32[40,128]{1,0:T(8,128)S(1)} %get-tuple-element.35.xlo_ref, ...), custom_call_target="tpu_custom_call" | custom-call | tf_op jit(solution)/shard_map/cells/pallas_call | solution.py:673
  38.7 1.2 %copy-done.1 = f32[24,136,128]{2,1,0:T(8,128)} copy-done((f32[24,136,128]{2,1,0:T(8,128)}, f32[24,136,128]{2,1,0:T(8,128)S(1)}, u32[]{:S(2)}) %copy-start.1) | copy-done | bytes 1671192
  39.9 5.5 %all-to-all-start = ((f32[8,192,128]{2,1,0:T(8,128)}), f32[8,192,128]{2,1,0:T(8,128)S(1)}, u32[]{:S(2)}, u32[]{:S(2)}) async-start(f32[8,192,128]{2,1,0:T(8,128)} %get-tuple-element.45), calls=%async_computation | async-start | bytes 1572864 | tf_op jit(solution)/shard_map/all_to_all | solution.py:687
  45.5 1.4 %copy-done.2 = f32[24,136,128]{2,1,0:T(8,128)S(1)} copy-done((f32[24,136,128]{2,1,0:T(8,128)S(1)}, f32[24,136,128]{2,1,0:T(8,128)}, u32[]{:S(2)}) %copy-start.2) | copy-done | bytes 1671192
  46.9 9.2 %collide.2.refs_4_ = f32[3,81920]{1,0:T(4,128)} custom-call(s32[3]{0:T(128)S(1)} %copy-done.12, f32[3,81920]{1,0:T(4,128)S(1)} %copy-done, s32[640,128]{1,0:T(8,128)S(1)} %bitcast.14, f32[24,136,128]{2,1,0:T(8,128)S(1)} %copy-done.2), custom_call_target="tpu_custom_call" | custom-call | flops 4800000000 | bytes 4000000 | tf_op jit(solution)/shard_map/collide/pallas_call | solution.py:621
  56.1 1.1 %all-to-all-done.in_ref = f32[8,192,128]{2,1,0:T(8,128)S(1)} async-done(((f32[8,192,128]{2,1,0:T(8,128)}), f32[8,192,128]{2,1,0:T(8,128)S(1)}, u32[]{:S(2)}, u32[]{:S(2)}) %all-to-all-start) | async-done | bytes 786464 | tf_op jit(solution)/shard_map/all_to_all | solution.py:687
  57.2 1.8 %z_lines.1 = f32[768,128]{1,0:T(8,128)} custom-call(s32[3]{0:T(128)S(1)} %pad_add_fusion.first_ref, f32[8,192,128]{2,1,0:T(8,128)S(1)} %all-to-all-done.in_ref, bf16[4,64,128]{2,1,0:T(8,128)(2,1)S(1)} %copy-done.10, bf16[4,64,128]{2,1,0:T(8,128)(2,1)S(1)} %copy-done.11), custom_call_target="tpu_custom_call" | custom-call | tf_op jit(solution)/shard_map/z_lines/pallas_call | solution.py:691
  59.0 6.4 %all-to-all-start.1 = ((f32[16,48,128]{2,1,0:T(8,128)}), f32[16,48,128]{2,1,0:T(8,128)S(1)}, u32[]{:S(2)}, u32[]{:S(2)}) async-start(f32[16,48,128]{2,1,0:T(8,128)} %bitcast.4), calls=%async_computation.1 | async-start | bytes 786432 | tf_op jit(solution)/shard_map/all_to_all | solution.py:698
  65.4 1.4 %copy-done.3 = f32[24,136,128]{2,1,0:T(8,128)S(1)} copy-done((f32[24,136,128]{2,1,0:T(8,128)S(1)}, f32[24,136,128]{2,1,0:T(8,128)}, u32[]{:S(2)}) %copy-start.3) | copy-done | bytes 1671192
  66.8 3.9 %collide.3 = f32[3,81920]{1,0:T(4,128)} custom-call(s32[3]{0:T(128)S(1)} %copy-done.12, f32[3,81920]{1,0:T(4,128)S(1)} %copy-done, s32[640,128]{1,0:T(8,128)S(1)} %bitcast.15, f32[24,136,128]{2,1,0:T(8,128)S(1)} %copy-done.3, f32[3,81920]{1,0:T(4,128)} %collide.2.refs_4_), custom_call_target="tpu_custom_call", output_to_operand_aliasing={{}: (4, {})} | custom-call | flops 1600000000 | bytes 4000000 | tf_op jit(solution)/shard_map/collide/pallas_call | solution.py:621
  70.7 7.6 %all-to-all-done.1 = f32[16,48,128]{2,1,0:T(8,128)S(1)} async-done(((f32[16,48,128]{2,1,0:T(8,128)}), f32[16,48,128]{2,1,0:T(8,128)S(1)}, u32[]{:S(2)}, u32[]{:S(2)}) %all-to-all-start.1) | async-done | bytes 393248 | tf_op jit(solution)/shard_map/all_to_all | solution.py:698
  78.3 0.8 y_lines.1
  79.1 12.5 %all_to_all.20.in_ref = f32[4,224,128]{2,1,0:T(8,128)S(1)} all-to-all(f32[4,224,128]{2,1,0:T(8,128)S(1)} %y_lines.1), channel_id=1, replica_groups=mesh['gx'=4,'gy_0'=4,'gy_1'=2,'gz_0'=2,'gz_1'=4] {'gx'}, dimensions={0} | all-to-all | bytes 917504 | tf_op jit(solution)/shard_map/all_to_all | solution.py:706
  91.6 1.8 %x_lines.1 = (f32[2,3,2,64,128]{4,3,2,1,0:T(8,128)}, f32[1,128]{1,0:T(1,128)S(1)}) custom-call(s32[3]{0:T(128)S(1)} %pad_add_fusion.first_ref, f32[4,224,128]{2,1,0:T(8,128)S(1)} %all_to_all.20.in_ref, bf16[512,512]{1,0:T(8,128)(2,1)S(1)} %copy-done.6, bf16[512,512]{1,0:T(8,128)(2,1)S(1)} %copy-done.7), custom_call_target="tpu_custom_call" | custom-call | tf_op jit(solution)/shard_map/x_lines/pallas_call | solution.py:707
  93.4 17.0 %all_to_all.21 = f32[64,1,128]{2,1,0:T(1,128)S(1)} all-to-all(f32[64,1,128]{2,1,0:T(1,128)S(1)} %broadcast_in_dim.9), channel_id=1, replica_groups=mesh['gx'=4,'gy_0'=4,'gy_1'=2,'gz_0'=2,'gz_1'=4] {'gy_0','gy_1','gz_0','..., dimensions={0} | all-to-all | bytes 65536 | tf_op jit(solution)/shard_map/all_to_all | solution.py:605
  110.4 2.2 %collective-permute-start.6 = (f32[1,128]{1,0:T(1,128)S(1)}, f32[1,128]{1,0:T(1,128)S(1)}, u32[]{:S(2)}, u32[]{:S(2)}) collective-permute-start(f32[1,128]{1,0:T(1,128)S(1)} %bitcast.18), channel_id=1, source_target_pairs={{0,64},{192,128},{1,65},{193,129},{2,66},{194,130},{3,67},{195,131... | collective-permute-start | bytes 1544 | tf_op jit(solution)/shard_map/ppermute | solution.py:716
  112.6 0.7 collective-permute-done.6
  113.3 0.5 multiply_bitcast_fusion
  (33 shorter events, 0.3 us)
Async XLA Ops:
  0.6 1.5 %copy-start = (f32[3,81920]{1,0:T(4,128)S(1)}, f32[3,81920]{1,0:T(4,128)}, u32[]{:S(2)}) copy-start(f32[3,81920]{1,0:T(4,128)} %refs_1_.3) | copy-start | bytes 2949124
  0.6 1.5 %copy-start.12 = (s32[3]{0:T(128)S(1)}, s32[3]{0:T(128)}, u32[]{:S(2)}) copy-start(s32[3]{0:T(128)} %refs_0_.3) | copy-start | bytes 40
  2.1 1.0 copy-start.4
  13.7 4.9 %collective-permute-start = (f32[40,128]{1,0:T(8,128)S(1)}, f32[40,128]{1,0:T(8,128)S(1)}, u32[]{:S(2)}, u32[]{:S(2)}) collective-permute-start(f32[40,128]{1,0:T(8,128)S(1)} %get-tuple-element.32.xhi_ref), channel_id=1, source_target_pairs={{0,64},{64,128},{128,192},{192,0},{1,65},{65,129},{129,193},{193,1... | collective-permute-start | bytes 61448 | tf_op jit(solution)/shard_map/ppermute | solution.py:599
  15.8 2.8 %collective-permute-start.1 = (f32[40,128]{1,0:T(8,128)S(1)}, f32[40,128]{1,0:T(8,128)S(1)}, u32[]{:S(2)}, u32[]{:S(2)}) collective-permute-start(f32[40,128]{1,0:T(8,128)S(1)} %get-tuple-element.31.xlo_ref), channel_id=1, source_target_pairs={{64,0},{128,64},{192,128},{0,192},{65,1},{129,65},{193,129},{1,193... | collective-permute-start | bytes 61448 | tf_op jit(solution)/shard_map/ppermute | solution.py:599
  18.7 5.7 %collective-permute-start.2 = (f32[40,128]{1,0:T(8,128)S(1)}, f32[40,128]{1,0:T(8,128)S(1)}, u32[]{:S(2)}, u32[]{:S(2)}) collective-permute-start(f32[40,128]{1,0:T(8,128)S(1)} %get-tuple-element.38.yhi_ref), channel_id=1, source_target_pairs={{0,8},{8,16},{16,24},{24,32},{32,40},{40,48},{48,56},{56,0},{1,9},... | collective-permute-start | bytes 61448 | tf_op jit(solution)/shard_map/ppermute | solution.py:599
  23.5 4.2 %collective-permute-start.3 = (f32[40,128]{1,0:T(8,128)S(1)}, f32[40,128]{1,0:T(8,128)S(1)}, u32[]{:S(2)}, u32[]{:S(2)}) collective-permute-start(f32[40,128]{1,0:T(8,128)S(1)} %get-tuple-element.37.ylo_ref), channel_id=1, source_target_pairs={{8,0},{16,8},{24,16},{32,24},{40,32},{48,40},{56,48},{0,56},{9,1},... | collective-permute-start | bytes 61448 | tf_op jit(solution)/shard_map/ppermute | solution.py:599
  27.9 6.5 %collective-permute-start.4 = (f32[160,128]{1,0:T(8,128)S(1)}, f32[160,128]{1,0:T(8,128)S(1)}, u32[]{:S(2)}, u32[]{:S(2)}) collective-permute-start(f32[160,128]{1,0:T(8,128)S(1)} %get-tuple-element.44.zhi_ref), channel_id=1, source_target_pairs={{0,1},{1,2},{2,3},{3,4},{4,5},{5,6},{6,7},{7,0},{8,9},{9,10},{10,1... | collective-permute-start | bytes 245768 | tf_op jit(solution)/shard_map/ppermute | solution.py:599
  29.2 5.2 %collective-permute-start.5 = (f32[160,128]{1,0:T(8,128)S(1)}, f32[160,128]{1,0:T(8,128)S(1)}, u32[]{:S(2)}, u32[]{:S(2)}) collective-permute-start(f32[160,128]{1,0:T(8,128)S(1)} %get-tuple-element.43.zlo_ref), channel_id=1, source_target_pairs={{1,0},{2,1},{3,2},{4,3},{5,4},{6,5},{7,6},{0,7},{9,8},{10,9},{11,1... | collective-permute-start | bytes 245768 | tf_op jit(solution)/shard_map/ppermute | solution.py:599
  38.7 1.2 %copy-start.1 = (f32[24,136,128]{2,1,0:T(8,128)}, f32[24,136,128]{2,1,0:T(8,128)S(1)}, u32[]{:S(2)}) copy-start(f32[24,136,128]{2,1,0:T(8,128)S(1)} %get-tuple-element.46.refs_3_) | copy-start | bytes 5013508
  39.9 5.5 %copy-start.5 = (s32[81920]{0:T(1024)S(1)}, s32[81920]{0:T(1024)}, u32[]{:S(2)}) copy-start(s32[81920]{0:T(1024)} %param.12) | copy-start | bytes 983044
  39.9 17.3 %all-to-all-start = ((f32[8,192,128]{2,1,0:T(8,128)}), f32[8,192,128]{2,1,0:T(8,128)S(1)}, u32[]{:S(2)}, u32[]{:S(2)}) async-start(f32[8,192,128]{2,1,0:T(8,128)} %get-tuple-element.45), calls=%async_computation | async-start | bytes 1572864 | tf_op jit(solution)/shard_map/all_to_all | solution.py:687
  45.5 1.4 %copy-start.2 = (f32[24,136,128]{2,1,0:T(8,128)S(1)}, f32[24,136,128]{2,1,0:T(8,128)}, u32[]{:S(2)}) copy-start(f32[24,136,128]{2,1,0:T(8,128)} %copy-done.1) | copy-start | bytes 5013508
  46.9 10.3 %copy-start.10 = (bf16[4,64,128]{2,1,0:T(8,128)(2,1)S(1)}, bf16[4,64,128]{2,1,0:T(8,128)(2,1)}, u32[]{:S(2)}) copy-start(bf16[4,64,128]{2,1,0:T(8,128)(2,1)} %constant.48.clone.fh_ref) | copy-start | bytes 196612
  46.9 10.3 %copy-start.11 = (bf16[4,64,128]{2,1,0:T(8,128)(2,1)S(1)}, bf16[4,64,128]{2,1,0:T(8,128)(2,1)}, u32[]{:S(2)}) copy-start(bf16[4,64,128]{2,1,0:T(8,128)(2,1)} %constant.49.clone.fl_ref) | copy-start | bytes 196612
  59.0 19.3 %all-to-all-start.1 = ((f32[16,48,128]{2,1,0:T(8,128)}), f32[16,48,128]{2,1,0:T(8,128)S(1)}, u32[]{:S(2)}, u32[]{:S(2)}) async-start(f32[16,48,128]{2,1,0:T(8,128)} %bitcast.4), calls=%async_computation.1 | async-start | bytes 786432 | tf_op jit(solution)/shard_map/all_to_all | solution.py:698
  65.4 1.4 %copy-start.3 = (f32[24,136,128]{2,1,0:T(8,128)S(1)}, f32[24,136,128]{2,1,0:T(8,128)}, u32[]{:S(2)}) copy-start(f32[24,136,128]{2,1,0:T(8,128)} %copy-done.1) | copy-start | bytes 5013508
  66.8 11.5 %copy-start.8 = (bf16[512,256]{1,0:T(8,128)(2,1)S(1)}, bf16[512,256]{1,0:T(8,128)(2,1)}, u32[]{:S(2)}) copy-start(bf16[512,256]{1,0:T(8,128)(2,1)} %constant.50.clone.fh_ref) | copy-start | bytes 786436
  66.8 11.5 %copy-start.9 = (bf16[512,256]{1,0:T(8,128)(2,1)S(1)}, bf16[512,256]{1,0:T(8,128)(2,1)}, u32[]{:S(2)}) copy-start(bf16[512,256]{1,0:T(8,128)(2,1)} %constant.51.clone.fl_ref) | copy-start | bytes 786436
  70.7 20.9 %copy-start.6 = (bf16[512,512]{1,0:T(8,128)(2,1)S(1)}, bf16[512,512]{1,0:T(8,128)(2,1)}, u32[]{:S(2)}) copy-start(bf16[512,512]{1,0:T(8,128)(2,1)} %constant.52.clone.fh_ref) | copy-start | bytes 1572868
  70.7 20.9 %copy-start.7 = (bf16[512,512]{1,0:T(8,128)(2,1)S(1)}, bf16[512,512]{1,0:T(8,128)(2,1)}, u32[]{:S(2)}) copy-start(bf16[512,512]{1,0:T(8,128)(2,1)} %constant.53.clone.fl_ref) | copy-start | bytes 1572868
  79.1 34.2 %copy-start.13 = (f32[1,64]{1,0:T(1,128)S(1)}, f32[1,64]{1,0:T(1,128)}, u32[]{:S(2)}) copy-start(f32[1,64]{1,0:T(1,128)} %constant.56) | copy-start | bytes 772
  110.4 2.9 %collective-permute-start.6 = (f32[1,128]{1,0:T(1,128)S(1)}, f32[1,128]{1,0:T(1,128)S(1)}, u32[]{:S(2)}, u32[]{:S(2)}) collective-permute-start(f32[1,128]{1,0:T(1,128)S(1)} %bitcast.18), channel_id=1, source_target_pairs={{0,64},{192,128},{1,65},{193,129},{2,66},{194,130},{3,67},{195,131... | collective-permute-start | bytes 1544 | tf_op jit(solution)/shard_map/ppermute | solution.py:716

commit v4 on v2

--- a/solution.py
+++ b/solution.py
@@ -65,11 +65,11 @@
     return jnp.dot(a, b, preferred_element_type=F32)
 
 
-def octants(place, shift_ref):
-    bit_x = (((place >> 4) & 3) + shift_ref[0] >= SUB).astype(jnp.int32)
-    bit_y = (((place >> 2) & 3) + shift_ref[1] >= SUB).astype(jnp.int32)
-    bit_z = ((place & 3) + shift_ref[2] >= SUB).astype(jnp.int32)
-    return bit_x * 4 + bit_y * 2 + bit_z
+def particle_codes(place, grid_shift):
+    bit_x = (((place >> 4) & 3) + grid_shift[0] >= SUB).astype(jnp.int32)
+    bit_y = (((place >> 2) & 3) + grid_shift[1] >= SUB).astype(jnp.int32)
+    bit_z = ((place & 3) + grid_shift[2] >= SUB).astype(jnp.int32)
+    return (place >> 6) * 8 + bit_x * 4 + bit_y * 2 + bit_z
 
 
 def tile_row(rows, t):
@@ -93,15 +93,15 @@
     )
 
 
-def scatter_body(shift_ref, v_ref, p_ref, axis_ref, s_ref, n_ref, xlo_ref, xhi_ref, turn_ref):
+def scatter_body(v_ref, p_ref, axis_ref, s_ref, n_ref, xlo_ref, xhi_ref, turn_ref):
     step = pl.program_id(0)
     cells = iota((TILE, TILE), 0).astype(F32).astype(BF16)
     upper = iota((8, TILE), 0) < 4
 
     def group(g, carry):
-        place = p_ref[pl.ds(pl.multiple_of(g * 40, 8), 40), :]
-        member = (place >> 6).astype(F32)
-        octant = octants(place, shift_ref)
+        codes = p_ref[pl.ds(pl.multiple_of(g * 40, 8), 40), :]
+        member = (codes >> 3).astype(F32)
+        octant = codes & 7
         speed = v_ref[:, pl.ds(pl.multiple_of(g * 5120, 128), 5120)]
         high = speed.astype(BF16).astype(F32)
         low = speed - high
@@ -396,7 +396,7 @@
             send_ref[part, 64 * c : 64 * c + 64, :] = plane[64 * (part // 4) : 64 * (part // 4) + 64]
 
 
-def collide_body(start, shift_ref, v_ref, p_ref, view_ref, *refs):
+def collide_body(start, v_ref, p_ref, view_ref, *refs):
     out_ref, turn_ref = refs[-2:]
     step = pl.program_id(0) + start
     cells = iota((TILE, TILE), 0).astype(F32).astype(BF16)
@@ -406,9 +406,9 @@
         turn_ref[...] = jnp.zeros(turn_ref.shape, F32)
 
     def group(g, carry):
-        place = p_ref[pl.ds(pl.multiple_of(g * 40, 8), 40), :]
-        member = (place >> 6).astype(F32)
-        octant = octants(place, shift_ref)
+        codes = p_ref[pl.ds(pl.multiple_of(g * 40, 8), 40), :]
+        member = (codes >> 3).astype(F32)
+        octant = codes & 7
         first = pl.multiple_of((step * PARTS + g) * 8, 8)
         for bx in range(2):
             for bz in range(2):
@@ -542,7 +542,7 @@
             out_ref[d, 192 + 64 * c : 256 + 64 * c, :] = out[0:64]
 
 
-def x_body(first_ref, in_ref, fh_ref, fl_ref, out_ref, shell_ref, sums_ref):
+def x_body(first_ref, in_ref, fh_ref, fl_ref, modes_ref, shell_ref, sums_ref, out_ref, sem):
     data = jnp.concatenate([in_ref[s] for s in range(4)], axis=1)
     high, low = split(data)
     fh, fl = fh_ref[...], fl_ref[...]
@@ -565,6 +565,8 @@
         wave = jnp.where(wave >= NZ // 2, wave - NZ, wave)
         energy.append(total * weight)
         square.append(plane + wave * wave)
+    modes_copy = pltpu.make_async_copy(out_ref, modes_ref, sem)
+    modes_copy.start()
     energy = jnp.concatenate(energy, axis=0)
     square = jnp.concatenate(square, axis=0)
     for s in range(NSHELL):
@@ -574,6 +576,7 @@
     before = jnp.where(iota((NSHELL, 128), 0) == 0, 0.0, sroll(cumulative, 1))
     own = jnp.concatenate([cumulative - before, jnp.zeros((64, 128), F32)], axis=0)
     shell_ref[...] = jnp.sum(own.T, axis=0, keepdims=True)
+    modes_copy.wait()
 
 
 def struct(*shape):
@@ -605,7 +608,7 @@
     return pl.BlockSpec(shape, lambda i: (0,) * len(shape))
 
 
-def collide(start, stop, grid_shift, velocity, place, views, earlier):
+def collide(start, stop, velocity, codes, views, earlier):
     span = TILES * TILE * PPC // STEPS
     speed_spec = pl.BlockSpec((3, span), lambda i: (0, i + start))
     place_spec = pl.BlockSpec((640 // STEPS, 128), lambda i: (i + start, 0))
@@ -614,21 +617,21 @@
         lambda *refs: collide_body(start, *refs),
         name="collide",
         grid=(stop - start,),
-        in_specs=[SMEM, speed_spec, place_spec, whole(24, VROWS, 128)]
+        in_specs=[speed_spec, place_spec, whole(24, VROWS, 128)]
         + [pl.BlockSpec(memory_space=pl.ANY)] * len(more),
         out_specs=speed_spec,
         out_shape=struct(*velocity.shape),
         scratch_shapes=[pltpu.VMEM((8 * LROW, 128), F32)],
-        input_output_aliases={4: 0} if more else {},
+        input_output_aliases={3: 0} if more else {},
         compiler_params=params(12),
         cost_estimate=pl.CostEstimate(
             flops=800_000_000 * (stop - start), bytes_accessed=4_000_000, transcendentals=0
         ),
-    )(grid_shift, velocity, place, views, *more)
+    )(velocity, codes, views, *more)
 
 
 def per_device(velocity, particle_place, grid_shift, rotation_axis):
-    place = particle_place.reshape(640, 128)
+    codes = particle_codes(particle_place, grid_shift).reshape(640, 128)
     axis_index = rotation_axis.reshape(TILES, 128)
     span = TILES * TILE * PPC // BLOCKS
     speed_spec = pl.BlockSpec((3, span), lambda i: (0, i))
@@ -638,12 +641,12 @@
         scatter_body,
         name="scatter",
         grid=(BLOCKS,),
-        in_specs=[SMEM, speed_spec, place_spec, whole(TILES, 128)],
+        in_specs=[speed_spec, place_spec, whole(TILES, 128)],
         out_specs=[whole(*s) for s in out_shapes],
         out_shape=[struct(*s) for s in out_shapes],
         scratch_shapes=[pltpu.VMEM((8 * SROW, 128), F32)],
         compiler_params=params(12),
-    )(grid_shift, velocity, place, axis_index)
+    )(velocity, codes, axis_index)
     main, y_lo, y_hi, z_lo, z_hi = pl.pallas_call(
         plane_body,
         name="planes",
@@ -677,7 +680,7 @@
         [lax.axis_index(GY_GZ) * 2, lax.axis_index("gx") * 64, lax.axis_index("gz_1")]
     ).astype(jnp.int32)
     arrived = lax.all_to_all(sent, GZ, split_axis=0, concat_axis=0, tiled=True)
-    updated = collide(0, EARLY, grid_shift, velocity, place, views, None)
+    updated = collide(0, EARLY, velocity, codes, views, None)
     arrived, updated = lax.optimization_barrier((arrived, updated))
     vmem = pl.BlockSpec(memory_space=pltpu.VMEM)
     lines = pl.pallas_call(
@@ -690,7 +693,7 @@
     pencil = lax.all_to_all(
         lines.reshape(16, 48, 128), ("gy_0", "gy_1", "gz_0"), split_axis=0, concat_axis=0, tiled=True
     )
-    new_velocity = collide(EARLY, STEPS, grid_shift, velocity, place, views, updated)
+    new_velocity = collide(EARLY, STEPS, velocity, codes, views, updated)
     pencil, new_velocity = lax.optimization_barrier((pencil, new_velocity))
     rows = pl.pallas_call(y_body, name="y_lines", out_shape=struct(4, 384, 128), compiler_params=params(12))(
         pencil.reshape(768, 128), *y_tables()
@@ -701,7 +704,12 @@
         name="x_lines",
         in_specs=[SMEM, vmem, vmem, vmem],
         out_shape=[struct(2, 3, 2, 64, 128), struct(1, 128)],
-        scratch_shapes=[pltpu.VMEM((NSHELL, 128), F32)],
+        out_specs=[pl.BlockSpec(memory_space=pl.ANY), vmem],
+        scratch_shapes=[
+            pltpu.VMEM((NSHELL, 128), F32),
+            pltpu.VMEM((2, 3, 2, 64, 128), F32),
+            pltpu.SemaphoreType.DMA,
+        ],
         compiler_params=params(12),
     )(first, columns, *x_tables())
     total = gathered_sum(shells, GY_GZ)

time: 115 us -> 116 us (level)
  other arithmetic: 0.61 us -> 2.76 us
  Pallas kernels: 34.2 us -> 32.5 us
    reshape x0 -> x1, other arithmetic: none -> 2.15 us  [per_device(): codes = particle_codes(particle_place, grid_shift).reshape(640, 128)]
    slice x0 -> x1, local copies, waits for them, and re-layouts: none -> 1.39 us  [particle_codes(): bit_x = ((place >> 4 & 3) + grid_shift[0] >= SUB).astype(jnp.int32)]
    unnamed x29 -> x25, local copies, waits for them, and re-layouts: 6.37 us -> 5.3 us
  transfers between devices with their start and end apart: 8 -> 8, of which waited for: 5 -> 5; matrix products, arithmetic and copies ran while one was open for 0% -> 0% of each run, Pallas kernels for 13% -> 11%
where the time goes in v4:
time: 116 us
  Pallas kernels  32.5 us (28%)
  blocking collectives  32.4 us (28%)
  starting transfers between devices  24.2 us (21%)
  waiting for transfers between devices  16.4 us (14%)
  local copies, waits for them, and re-layouts  6.9 us (6%)
  other arithmetic  2.76 us (2%)
    all_to_all x1, blocking collectives, gathered_sum(): lax.all_to_all(copies, axes, split_axis=0, concat_axis=0, tiled=True)  16.6 us
    all_to_all x1, blocking collectives, per_device(): lax.all_to_all(rows, 'gx', split_axis=0, concat_axis=0, tiled=True)  15.8 us
    pallas_call x2, Pallas kernels, collide(): pl.pallas_call(lambda *refs: collide_body(start, *refs), name='collide',...  11.9 us
    pallas_call x1, Pallas kernels, per_device(): pl.pallas_call(scatter_body, name='scatter', grid=(BLOCKS,), in_specs=[sp...  10 us
    ppermute x3, starting transfers between devices, ring(): lax.ppermute(high, axis, forward)  8.33 us
    all_to_all x1, waiting for transfers between devices, per_device(): lax.all_to_all(lines.reshape(16, 48, 128), ('gy_0', 'gy_1', 'gz_0'), spli...  8.15 us
    all_to_all x1, starting transfers between devices, per_device(): lax.all_to_all(lines.reshape(16, 48, 128), ('gy_0', 'gy_1', 'gz_0'), spli...  6.39 us
    all_to_all x1, starting transfers between devices, per_device(): arrived = lax.all_to_all(sent, GZ, split_axis=0, concat_axis=0, tiled=True)  5.33 us
  transfers between devices with their start and end apart: 8, of which 5 were waited for; matrix products, arithmetic and copies ran while one was open for 0% of the time, Pallas kernels for 11%

profile of v4, /device:TPU:1, one launch (start us, length us, event | category | flops | bytes accessed | tf_op | source)
XLA Modules:
  0.0 115.9 jit_solution(18197331614966416554)
XLA Ops:
  0.7 1.4 %fusion = (s32[1]{0:T(128)}, s32[1]{0:T(128)}, s32[1]{0:T(128)}) fusion(s32[3]{0:T(128)} %param.13), kind=kLoop, calls=%fused_computation.6 | loop fusion | bytes 24 | tf_op jit(solution)/shard_map/slice | solution.py:69
  2.0 1.2 %copy.18 = s32[32,32,16]{2,1,0:T(8,128)S(1)} copy(s32[32,32,16]{1,2,0:T(8,128)} %param.14) | data formatting | bytes 131072 | tf_op args[3]
  3.2 0.2 reshape.23.axis_ref
  3.4 2.1 %add_bitcast_fusion.p_ref.refs_1_ = s32[640,128]{1,0:T(8,128)S(1)} fusion(s32[81920]{0:T(1024)S(1)} %copy-done.10, s32[]{:T(128)} %bitcast.5, s32[]{:T(128)} %bitcast.4, s32[]{:T(128)} %bitcast.3), kind=kLoop, calls=%fused_computation | loop fusion | flops 1556480 | bytes 655372 | tf_op jit(solution)/shard_map/reshape | solution.py:634
  5.6 10.0 %scatter.1 = (f32[32,128,128]{2,1,0:T(8,128)S(1)}, f32[3,128,128]{2,1,0:T(8,128)S(1)}, f32[40,128]{1,0:T(8,128)S(1)}, f32[40,128]{1,0:T(8,128)S(1)}) custom-call(f32[3,81920]{1,0:T(4,128)S(1)} %copy-done, s32[640,128]{1,0:T(8,128)S(1)} %add_bitcast_fusion.p_ref.refs_1_, s32[128,128]{1,0:T(8,128)S(1)} %reshape.23.axis_ref), custom_call_target="tpu_custom_call" | custom-call | tf_op jit(solution)/shard_map/scatter/pallas_call | solution.py:640
  15.6 2.1 %collective-permute-start = (f32[40,128]{1,0:T(8,128)S(1)}, f32[40,128]{1,0:T(8,128)S(1)}, u32[]{:S(2)}, u32[]{:S(2)}) collective-permute-start(f32[40,128]{1,0:T(8,128)S(1)} %get-tuple-element.32.xhi_ref), channel_id=1, source_target_pairs={{0,64},{64,128},{128,192},{192,0},{1,65},{65,129},{129,193},{193,1... | collective-permute-start | bytes 61448 | tf_op jit(solution)/shard_map/ppermute | solution.py:594
  17.7 1.4 %collective-permute-start.1 = (f32[40,128]{1,0:T(8,128)S(1)}, f32[40,128]{1,0:T(8,128)S(1)}, u32[]{:S(2)}, u32[]{:S(2)}) collective-permute-start(f32[40,128]{1,0:T(8,128)S(1)} %get-tuple-element.31.xlo_ref), channel_id=1, source_target_pairs={{64,0},{128,64},{192,128},{0,192},{65,1},{129,65},{193,129},{1,193... | collective-permute-start | bytes 61448 | tf_op jit(solution)/shard_map/ppermute | solution.py:594
  19.1 1.4 %planes.1 = (f32[4,160,128]{2,1,0:T(8,128)S(1)}, f32[40,128]{1,0:T(8,128)S(1)}, f32[40,128]{1,0:T(8,128)S(1)}, f32[160,128]{1,0:T(8,128)S(1)}, f32[160,128]{1,0:T(8,128)S(1)}) custom-call(f32[32,128,128]{2,1,0:T(8,128)S(1)} %get-tuple-element.28.s_ref, f32[3,128,128]{2,1,0:T(8,128)S(1)} %get-tuple-element.29.n_ref), custom_call_target="tpu_custom_call" | custom-call | flops 1000000000 | bytes 3000000 | tf_op jit(solution)/shard_map/planes/pallas_call | solution.py:650
  20.5 0.1 fold_x.1
  20.6 4.8 %collective-permute-start.2 = (f32[40,128]{1,0:T(8,128)S(1)}, f32[40,128]{1,0:T(8,128)S(1)}, u32[]{:S(2)}, u32[]{:S(2)}) collective-permute-start(f32[40,128]{1,0:T(8,128)S(1)} %get-tuple-element.38.yhi_ref), channel_id=1, source_target_pairs={{0,8},{8,16},{16,24},{24,32},{32,40},{40,48},{48,56},{56,0},{1,9},... | collective-permute-start | bytes 61448 | tf_op jit(solution)/shard_map/ppermute | solution.py:594
  25.5 0.9 collective-permute-done.2.from_low
  26.4 3.3 %collective-permute-done.3.from_high = f32[40,128]{1,0:T(8,128)S(1)} collective-permute-done((f32[40,128]{1,0:T(8,128)S(1)}, f32[40,128]{1,0:T(8,128)S(1)}, u32[]{:S(2)}, u32[]{:S(2)}) %collective-permute-start.3) | collective-permute-done | bytes 20512 | tf_op jit(solution)/shard_map/ppermute | solution.py:594
  29.6 0.2 fold_y.1
  29.8 1.4 %collective-permute-start.4 = (f32[160,128]{1,0:T(8,128)S(1)}, f32[160,128]{1,0:T(8,128)S(1)}, u32[]{:S(2)}, u32[]{:S(2)}) collective-permute-start(f32[160,128]{1,0:T(8,128)S(1)} %get-tuple-element.44.zhi_ref), channel_id=1, source_target_pairs={{0,1},{1,2},{2,3},{3,4},{4,5},{5,6},{6,7},{7,0},{8,9},{9,10},{10,1... | collective-permute-start | bytes 245768 | tf_op jit(solution)/shard_map/ppermute | solution.py:594
  31.2 2.8 %collective-permute-start.5 = (f32[160,128]{1,0:T(8,128)S(1)}, f32[160,128]{1,0:T(8,128)S(1)}, u32[]{:S(2)}, u32[]{:S(2)}) collective-permute-start(f32[160,128]{1,0:T(8,128)S(1)} %get-tuple-element.43.zlo_ref), channel_id=1, source_target_pairs={{1,0},{2,1},{3,2},{4,3},{5,4},{6,5},{7,6},{0,7},{9,8},{10,9},{11,1... | collective-permute-start | bytes 245768 | tf_op jit(solution)/shard_map/ppermute | solution.py:594
  34.0 2.4 %collective-permute-done.4.from_low = f32[160,128]{1,0:T(8,128)S(1)} collective-permute-done((f32[160,128]{1,0:T(8,128)S(1)}, f32[160,128]{1,0:T(8,128)S(1)}, u32[]{:S(2)}, u32[]{:S(2)}) %collective-permute-start.4) | collective-permute-done | bytes 81952 | tf_op jit(solution)/shard_map/ppermute | solution.py:594
  36.3 4.3 %cells.1 = (f32[24,136,128]{2,1,0:T(8,128)S(1)}, f32[8,192,128]{2,1,0:T(8,128)}) custom-call(f32[32,128,128]{2,1,0:T(8,128)S(1)} %get-tuple-element.28.s_ref, f32[4,160,128]{2,1,0:T(8,128)S(1)} %get-tuple-element.30.m_ref, f32[3,128,128]{2,1,0:T(8,128)S(1)} %get-tuple-element.29.n_ref, f32[40,128]{1,0:T(8,128)S(1)} %get-tuple-element.35.xlo_ref, ...), custom_call_target="tpu_custom_call" | custom-call | tf_op jit(solution)/shard_map/cells/pallas_call | solution.py:668
  40.7 1.2 %copy-done.1 = f32[24,136,128]{2,1,0:T(8,128)} copy-done((f32[24,136,128]{2,1,0:T(8,128)}, f32[24,136,128]{2,1,0:T(8,128)S(1)}, u32[]{:S(2)}) %copy-start.1) | copy-done | bytes 1671192
  41.9 5.3 %all-to-all-start = ((f32[8,192,128]{2,1,0:T(8,128)}), f32[8,192,128]{2,1,0:T(8,128)S(1)}, u32[]{:S(2)}, u32[]{:S(2)}) async-start(f32[8,192,128]{2,1,0:T(8,128)} %get-tuple-element.45), calls=%async_computation | async-start | bytes 1572864 | tf_op jit(solution)/shard_map/all_to_all | solution.py:682
  47.3 1.4 %copy-done.2 = f32[24,136,128]{2,1,0:T(8,128)S(1)} copy-done((f32[24,136,128]{2,1,0:T(8,128)S(1)}, f32[24,136,128]{2,1,0:T(8,128)}, u32[]{:S(2)}) %copy-start.2) | copy-done | bytes 1671192
  48.7 8.6 %collide.2.refs_3_ = f32[3,81920]{1,0:T(4,128)} custom-call(f32[3,81920]{1,0:T(4,128)S(1)} %copy-done, s32[640,128]{1,0:T(8,128)S(1)} %add_bitcast_fusion.p_ref.refs_1_, f32[24,136,128]{2,1,0:T(8,128)S(1)} %copy-done.2), custom_call_target="tpu_custom_call" | custom-call | flops 4800000000 | bytes 4000000 | tf_op jit(solution)/shard_map/collide/pallas_call | solution.py:616
  57.3 1.8 %all-to-all-done.in_ref = f32[8,192,128]{2,1,0:T(8,128)S(1)} async-done(((f32[8,192,128]{2,1,0:T(8,128)}), f32[8,192,128]{2,1,0:T(8,128)S(1)}, u32[]{:S(2)}, u32[]{:S(2)}) %all-to-all-start) | async-done | bytes 786464 | tf_op jit(solution)/shard_map/all_to_all | solution.py:682
  59.0 1.8 %z_lines.1 = f32[768,128]{1,0:T(8,128)} custom-call(s32[3]{0:T(128)S(1)} %pad_add_fusion.first_ref, f32[8,192,128]{2,1,0:T(8,128)S(1)} %all-to-all-done.in_ref, bf16[4,64,128]{2,1,0:T(8,128)(2,1)S(1)} %copy-done.8, bf16[4,64,128]{2,1,0:T(8,128)(2,1)S(1)} %copy-done.9), custom_call_target="tpu_custom_call" | custom-call | tf_op jit(solution)/shard_map/z_lines/pallas_call | solution.py:686
  60.8 6.4 %all-to-all-start.1 = ((f32[16,48,128]{2,1,0:T(8,128)}), f32[16,48,128]{2,1,0:T(8,128)S(1)}, u32[]{:S(2)}, u32[]{:S(2)}) async-start(f32[16,48,128]{2,1,0:T(8,128)} %bitcast.7), calls=%async_computation.1 | async-start | bytes 786432 | tf_op jit(solution)/shard_map/all_to_all | solution.py:693
  67.2 1.4 %copy-done.3 = f32[24,136,128]{2,1,0:T(8,128)S(1)} copy-done((f32[24,136,128]{2,1,0:T(8,128)S(1)}, f32[24,136,128]{2,1,0:T(8,128)}, u32[]{:S(2)}) %copy-start.3) | copy-done | bytes 1671192
  68.7 3.3 %collide.3 = f32[3,81920]{1,0:T(4,128)} custom-call(f32[3,81920]{1,0:T(4,128)S(1)} %copy-done, s32[640,128]{1,0:T(8,128)S(1)} %add_bitcast_fusion.p_ref.refs_1_, f32[24,136,128]{2,1,0:T(8,128)S(1)} %copy-done.3, f32[3,81920]{1,0:T(4,128)} %collide.2.refs_3_), custom_call_target="tpu_custom_call", output_to_operand_aliasing={{}: (3, {})} | custom-call | flops 1600000000 | bytes 4000000 | tf_op jit(solution)/shard_map/collide/pallas_call | solution.py:616
  72.0 8.1 %all-to-all-done.1 = f32[16,48,128]{2,1,0:T(8,128)S(1)} async-done(((f32[16,48,128]{2,1,0:T(8,128)}), f32[16,48,128]{2,1,0:T(8,128)S(1)}, u32[]{:S(2)}, u32[]{:S(2)}) %all-to-all-start.1) | async-done | bytes 393248 | tf_op jit(solution)/shard_map/all_to_all | solution.py:693
  80.1 0.8 y_lines.1
  80.9 15.8 %all_to_all.20.in_ref = f32[4,384,128]{2,1,0:T(8,128)S(1)} all-to-all(f32[4,384,128]{2,1,0:T(8,128)S(1)} %y_lines.1), channel_id=1, replica_groups=mesh['gx'=4,'gy_0'=4,'gy_1'=2,'gz_0'=2,'gz_1'=4] {'gx'}, dimensions={0} | all-to-all | bytes 1572864 | tf_op jit(solution)/shard_map/all_to_all | solution.py:701
  96.7 2.0 %x_lines.1 = (f32[2,3,2,64,128]{4,3,2,1,0:T(8,128)}, f32[1,128]{1,0:T(1,128)S(1)}) custom-call(s32[3]{0:T(128)S(1)} %pad_add_fusion.first_ref, f32[4,384,128]{2,1,0:T(8,128)S(1)} %all_to_all.20.in_ref, bf16[512,512]{1,0:T(8,128)(2,1)S(1)} %copy-done.4, bf16[512,512]{1,0:T(8,128)(2,1)S(1)} %copy-done.5), custom_call_target="tpu_custom_call" | custom-call | tf_op jit(solution)/shard_map/x_lines/pallas_call | solution.py:702
  98.8 16.6 %all_to_all.21 = f32[64,1,128]{2,1,0:T(1,128)S(1)} all-to-all(f32[64,1,128]{2,1,0:T(1,128)S(1)} %broadcast_in_dim.9), channel_id=1, replica_groups=mesh['gx'=4,'gy_0'=4,'gy_1'=2,'gz_0'=2,'gz_1'=4] {'gy_0','gy_1','gz_0','..., dimensions={0} | all-to-all | bytes 65536 | tf_op jit(solution)/shard_map/all_to_all | solution.py:600
  115.4 0.5 multiply_bitcast_fusion
  (28 shorter events, 0.2 us)
Async XLA Ops:
  0.6 2.8 %copy-start.10 = (s32[81920]{0:T(1024)S(1)}, s32[81920]{0:T(1024)}, u32[]{:S(2)}) copy-start(s32[81920]{0:T(1024)} %param.12) | copy-start | bytes 983044
  0.6 4.9 %copy-start = (f32[3,81920]{1,0:T(4,128)S(1)}, f32[3,81920]{1,0:T(4,128)}, u32[]{:S(2)}) copy-start(f32[3,81920]{1,0:T(4,128)} %refs_0_.3) | copy-start | bytes 2949124
  15.6 4.9 %collective-permute-start = (f32[40,128]{1,0:T(8,128)S(1)}, f32[40,128]{1,0:T(8,128)S(1)}, u32[]{:S(2)}, u32[]{:S(2)}) collective-permute-start(f32[40,128]{1,0:T(8,128)S(1)} %get-tuple-element.32.xhi_ref), channel_id=1, source_target_pairs={{0,64},{64,128},{128,192},{192,0},{1,65},{65,129},{129,193},{193,1... | collective-permute-start | bytes 61448 | tf_op jit(solution)/shard_map/ppermute | solution.py:594
  17.7 2.8 %collective-permute-start.1 = (f32[40,128]{1,0:T(8,128)S(1)}, f32[40,128]{1,0:T(8,128)S(1)}, u32[]{:S(2)}, u32[]{:S(2)}) collective-permute-start(f32[40,128]{1,0:T(8,128)S(1)} %get-tuple-element.31.xlo_ref), channel_id=1, source_target_pairs={{64,0},{128,64},{192,128},{0,192},{65,1},{129,65},{193,129},{1,193... | collective-permute-start | bytes 61448 | tf_op jit(solution)/shard_map/ppermute | solution.py:594
  20.6 5.7 %collective-permute-start.2 = (f32[40,128]{1,0:T(8,128)S(1)}, f32[40,128]{1,0:T(8,128)S(1)}, u32[]{:S(2)}, u32[]{:S(2)}) collective-permute-start(f32[40,128]{1,0:T(8,128)S(1)} %get-tuple-element.38.yhi_ref), channel_id=1, source_target_pairs={{0,8},{8,16},{16,24},{24,32},{32,40},{40,48},{48,56},{56,0},{1,9},... | collective-permute-start | bytes 61448 | tf_op jit(solution)/shard_map/ppermute | solution.py:594
  25.5 4.2 %collective-permute-start.3 = (f32[40,128]{1,0:T(8,128)S(1)}, f32[40,128]{1,0:T(8,128)S(1)}, u32[]{:S(2)}, u32[]{:S(2)}) collective-permute-start(f32[40,128]{1,0:T(8,128)S(1)} %get-tuple-element.37.ylo_ref), channel_id=1, source_target_pairs={{8,0},{16,8},{24,16},{32,24},{40,32},{48,40},{56,48},{0,56},{9,1},... | collective-permute-start | bytes 61448 | tf_op jit(solution)/shard_map/ppermute | solution.py:594
  29.8 6.5 %collective-permute-start.4 = (f32[160,128]{1,0:T(8,128)S(1)}, f32[160,128]{1,0:T(8,128)S(1)}, u32[]{:S(2)}, u32[]{:S(2)}) collective-permute-start(f32[160,128]{1,0:T(8,128)S(1)} %get-tuple-element.44.zhi_ref), channel_id=1, source_target_pairs={{0,1},{1,2},{2,3},{3,4},{4,5},{5,6},{6,7},{7,0},{8,9},{9,10},{10,1... | collective-permute-start | bytes 245768 | tf_op jit(solution)/shard_map/ppermute | solution.py:594
  31.2 5.2 %collective-permute-start.5 = (f32[160,128]{1,0:T(8,128)S(1)}, f32[160,128]{1,0:T(8,128)S(1)}, u32[]{:S(2)}, u32[]{:S(2)}) collective-permute-start(f32[160,128]{1,0:T(8,128)S(1)} %get-tuple-element.43.zlo_ref), channel_id=1, source_target_pairs={{1,0},{2,1},{3,2},{4,3},{5,4},{6,5},{7,6},{0,7},{9,8},{10,9},{11,1... | collective-permute-start | bytes 245768 | tf_op jit(solution)/shard_map/ppermute | solution.py:594
  40.7 1.2 %copy-start.1 = (f32[24,136,128]{2,1,0:T(8,128)}, f32[24,136,128]{2,1,0:T(8,128)S(1)}, u32[]{:S(2)}) copy-start(f32[24,136,128]{2,1,0:T(8,128)S(1)} %get-tuple-element.46.refs_2_) | copy-start | bytes 5013508
  41.9 17.2 %all-to-all-start = ((f32[8,192,128]{2,1,0:T(8,128)}), f32[8,192,128]{2,1,0:T(8,128)S(1)}, u32[]{:S(2)}, u32[]{:S(2)}) async-start(f32[8,192,128]{2,1,0:T(8,128)} %get-tuple-element.45), calls=%async_computation | async-start | bytes 1572864 | tf_op jit(solution)/shard_map/all_to_all | solution.py:682
  47.3 1.4 %copy-start.2 = (f32[24,136,128]{2,1,0:T(8,128)S(1)}, f32[24,136,128]{2,1,0:T(8,128)}, u32[]{:S(2)}) copy-start(f32[24,136,128]{2,1,0:T(8,128)} %copy-done.1) | copy-start | bytes 5013508
  48.7 10.3 %copy-start.8 = (bf16[4,64,128]{2,1,0:T(8,128)(2,1)S(1)}, bf16[4,64,128]{2,1,0:T(8,128)(2,1)}, u32[]{:S(2)}) copy-start(bf16[4,64,128]{2,1,0:T(8,128)(2,1)} %constant.56.clone.fh_ref) | copy-start | bytes 196612
  48.7 10.3 %copy-start.9 = (bf16[4,64,128]{2,1,0:T(8,128)(2,1)S(1)}, bf16[4,64,128]{2,1,0:T(8,128)(2,1)}, u32[]{:S(2)}) copy-start(bf16[4,64,128]{2,1,0:T(8,128)(2,1)} %constant.57.clone.fl_ref) | copy-start | bytes 196612
  60.8 19.3 %all-to-all-start.1 = ((f32[16,48,128]{2,1,0:T(8,128)}), f32[16,48,128]{2,1,0:T(8,128)S(1)}, u32[]{:S(2)}, u32[]{:S(2)}) async-start(f32[16,48,128]{2,1,0:T(8,128)} %bitcast.7), calls=%async_computation.1 | async-start | bytes 786432 | tf_op jit(solution)/shard_map/all_to_all | solution.py:693
  67.2 1.4 %copy-start.3 = (f32[24,136,128]{2,1,0:T(8,128)S(1)}, f32[24,136,128]{2,1,0:T(8,128)}, u32[]{:S(2)}) copy-start(f32[24,136,128]{2,1,0:T(8,128)} %copy-done.1) | copy-start | bytes 5013508
  68.7 11.5 %copy-start.6 = (bf16[512,256]{1,0:T(8,128)(2,1)S(1)}, bf16[512,256]{1,0:T(8,128)(2,1)}, u32[]{:S(2)}) copy-start(bf16[512,256]{1,0:T(8,128)(2,1)} %constant.58.clone.fh_ref) | copy-start | bytes 786436
  68.7 11.5 %copy-start.7 = (bf16[512,256]{1,0:T(8,128)(2,1)S(1)}, bf16[512,256]{1,0:T(8,128)(2,1)}, u32[]{:S(2)}) copy-start(bf16[512,256]{1,0:T(8,128)(2,1)} %constant.59.clone.fl_ref) | copy-start | bytes 786436
  80.1 16.6 %copy-start.4 = (bf16[512,512]{1,0:T(8,128)(2,1)S(1)}, bf16[512,512]{1,0:T(8,128)(2,1)}, u32[]{:S(2)}) copy-start(bf16[512,512]{1,0:T(8,128)(2,1)} %constant.60.clone.fh_ref) | copy-start | bytes 1572868
  80.1 16.6 %copy-start.5 = (bf16[512,512]{1,0:T(8,128)(2,1)S(1)}, bf16[512,512]{1,0:T(8,128)(2,1)}, u32[]{:S(2)}) copy-start(bf16[512,512]{1,0:T(8,128)(2,1)} %constant.61.clone.fl_ref) | copy-start | bytes 1572868
  96.7 18.6 %copy-start.11 = (f32[1,64]{1,0:T(1,128)S(1)}, f32[1,64]{1,0:T(1,128)}, u32[]{:S(2)}) copy-start(f32[1,64]{1,0:T(1,128)} %constant.64) | copy-start | bytes 772

commit v5 on v2

--- a/solution.py
+++ b/solution.py
@@ -30,7 +30,7 @@
 BLOCKS = 1
 GROUPS = TILES // 8 // BLOCKS
 STEPS = 8
-EARLY = 6
+EARLY = 5
 PARTS = TILES // 8 // STEPS
 
 
@@ -124,6 +124,8 @@
                 both = jnp.where(upper, even + sroll(even, 4), odd + sroll(odd, 4))
                 turn_ref[SROW * t + 8 * pair : SROW * t + 8 * pair + 8, :] = both
         first = pl.multiple_of((step * GROUPS + g) * 8, 8)
+        for c, axis in enumerate(axis_vectors(axis_ref[pl.ds(first, 8), :])):
+            n_ref[c, pl.ds(first, 8), :] = axis
         for r in range(32):
             s_ref[r, pl.ds(first, 8), :] = turn_ref[pl.ds(r, 8, stride=SROW), :]
         return carry
@@ -132,8 +134,6 @@
 
     @pl.when(step == BLOCKS - 1)
     def _():
-        for c, part in enumerate(axis_vectors(axis_ref[...])):
-            n_ref[c] = part
         z = iota((32, 128), 1) & 15
         lane = iota((40, 128), 1)
         pad = jnp.zeros((8, 128), F32)
@@ -298,8 +298,8 @@
 VROWS = 136
 
 
-def cell_body(s_ref, m_ref, n_ref, xlo_ref, xhi_ref, ylo_ref, yhi_ref, zlo_ref, zhi_ref,
-              from_low, from_high, view_ref, send_ref, ext_ref, end_ref, vel_ref):
+def view_body(m_ref, n_ref, xlo_ref, xhi_ref, ylo_ref, yhi_ref, zlo_ref, zhi_ref,
+              from_low, from_high, view_ref, ext_ref, end_ref):
     z_low = zlo_ref[0:VROWS, :] + from_low[0:VROWS, :]
     z_high = zhi_ref[0:VROWS, :] + from_high[0:VROWS, :]
     x_low = xlo_ref[...]
@@ -356,6 +356,12 @@
             ahead = jnp.where(x_in < 7, rolled, jnp.where(x_out == 3, end, sroll(rolled, -1)))
             view_ref[bz * 6 + slot] = main
             view_ref[(2 + bz) * 6 + slot] = ahead
+
+
+def cell_body(s_ref, *refs):
+    inputs = refs[:10]
+    send_ref, view_ref, ext_ref, end_ref, vel_ref = refs[10:]
+    view_body(*inputs, view_ref, ext_ref, end_ref)
 
     def group(g, carry):
         first = pl.multiple_of(g * 8, 8)
@@ -542,11 +548,24 @@
             out_ref[d, 192 + 64 * c : 256 + 64 * c, :] = out[0:64]
 
 
-def x_body(first_ref, in_ref, fh_ref, fl_ref, out_ref, shell_ref, sums_ref):
-    data = jnp.concatenate([in_ref[s] for s in range(4)], axis=1)
+def x_lines(in_ref, fh_ref, fl_ref, first):
+    data = jnp.concatenate([in_ref[s, first : first + 192, :] for s in range(4)], axis=1)
     high, low = split(data)
     fh, fl = fh_ref[...], fl_ref[...]
-    res = dot(high, fh) + dot(low, fh) + dot(high, fl)
+    return dot(high, fh) + dot(low, fh) + dot(high, fl)
+
+
+def mode_body(in_ref, fh_ref, fl_ref, out_ref):
+    res = x_lines(in_ref, fh_ref, fl_ref, 0)
+    for part in range(2):
+        for c in range(3):
+            for kz in range(2):
+                here = slice(256 * part + 128 * kz, 256 * part + 128 * kz + 128)
+                out_ref[part, c, kz] = res[64 * c : 64 * c + 64, here]
+
+
+def shell_body(first_ref, in_ref, fh_ref, fl_ref, shell_ref, sums_ref):
+    res = x_lines(in_ref, fh_ref, fl_ref, 192)
     ky = iota((64, 128), 0)
     kx = iota((64, 128), 1)
     kx = jnp.where(kx >= NX // 2, kx - NX, kx)
@@ -558,8 +577,7 @@
         for part in range(2):
             for c in range(3):
                 here = slice(256 * part + 128 * kz, 256 * part + 128 * kz + 128)
-                out_ref[part, c, kz] = res[64 * c : 64 * c + 64, here]
-                block = res[192 + 64 * c : 256 + 64 * c, here]
+                block = res[64 * c : 64 * c + 64, here]
                 total += block * block
         wave = first_ref[0] + kz
         wave = jnp.where(wave >= NZ // 2, wave - NZ, wave)
@@ -662,17 +680,29 @@
         compiler_params=params(3),
     )(y_lo, y_hi, below, above, x_lo, x_hi, z_lo, z_hi)
     below, above = ring((z_lo, z_hi), GZ)
-    views, sent = pl.pallas_call(
+    pieces = (main, normal, x_lo, x_hi, y_lo, y_hi, z_lo, z_hi, below, above)
+    plane = pltpu.VMEM((7, ROWS, 128), F32)
+    sent = pl.pallas_call(
         cell_body,
         name="cells",
-        out_shape=[struct(24, VROWS, 128), struct(8, 192, 128)],
+        out_shape=struct(8, 192, 128),
         scratch_shapes=[
-            pltpu.VMEM((7, ROWS, 128), F32),
-            pltpu.VMEM((7, ROWS, 128), F32),
+            pltpu.VMEM((24, VROWS, 128), F32),
+            plane,
+            plane,
             pltpu.VMEM((3, TILES, 128), F32),
         ],
         compiler_params=params(12),
-    )(sums, main, normal, x_lo, x_hi, y_lo, y_hi, z_lo, z_hi, below, above)
+    )(sums, *pieces)
+    pieces, sent = lax.optimization_barrier((pieces, sent))
+    views = pl.pallas_call(
+        view_body,
+        name="views",
+        out_shape=struct(24, VROWS, 128),
+        scratch_shapes=[plane, plane],
+        compiler_params=params(12),
+        cost_estimate=pl.CostEstimate(flops=1_000_000_000, bytes_accessed=3_000_000, transcendentals=0),
+    )(*pieces)
     first = jnp.stack(
         [lax.axis_index(GY_GZ) * 2, lax.axis_index("gx") * 64, lax.axis_index("gz_1")]
     ).astype(jnp.int32)
@@ -696,14 +726,23 @@
         pencil.reshape(768, 128), *y_tables()
     )
     columns = lax.all_to_all(rows, "gx", split_axis=0, concat_axis=0, tiled=True)
-    modes, shells = pl.pallas_call(
-        x_body,
-        name="x_lines",
+    tables = x_tables()
+    shells = pl.pallas_call(
+        shell_body,
+        name="x_shells",
         in_specs=[SMEM, vmem, vmem, vmem],
-        out_shape=[struct(2, 3, 2, 64, 128), struct(1, 128)],
+        out_shape=struct(1, 128),
         scratch_shapes=[pltpu.VMEM((NSHELL, 128), F32)],
         compiler_params=params(12),
-    )(first, columns, *x_tables())
+    )(first, columns, *tables)
+    columns, shells = lax.optimization_barrier((columns, shells))
+    modes = pl.pallas_call(
+        mode_body,
+        name="x_modes",
+        out_shape=struct(2, 3, 2, 64, 128),
+        compiler_params=params(12),
+        cost_estimate=pl.CostEstimate(flops=2_000_000_000, bytes_accessed=3_000_000, transcendentals=0),
+    )(columns, *tables)
     total = gathered_sum(shells, GY_GZ)
     spectrum = total[0, :NSHELL] / shell_counts()
     return new_velocity, modes, spectrum

time: 115 us -> 114 us (level)
  blocking collectives: 33 us -> 15.8 us
  starting transfers between devices: 24.3 us -> 31.9 us
  waiting for transfers between devices: 15.3 us -> 22.3 us
  Pallas kernels: 34.2 us -> 36.2 us
    all_to_all x1 -> x0, blocking collectives: 17.2 us -> none  [gathered_sum(): lax.all_to_all(copies, axes, split_axis=0, concat_axis=0, tiled=True)]
    all_to_all x0 -> x1, waiting for transfers between devices: none -> 8 us  [gathered_sum(): lax.all_to_all(copies, axes, split_axis=0, concat_axis=0, tiled=True)]
    all_to_all x0 -> x1, starting transfers between devices: none -> 7.7 us  [gathered_sum(): lax.all_to_all(copies, axes, split_axis=0, concat_axis=0, tiled=True)]
    pallas_call x2 -> x4, Pallas kernels: 6.34 us -> 8.38 us  [the longest x1 4.39 us: per_device(): pl.pallas_call(cell_body, name='cells', out_shape=struct(8, 192, 128), sc...]
    unnamed x29 -> x27, local copies, waits for them, and re-layouts: 6.37 us -> 4.94 us
    all_to_all x1, waiting for transfers between devices: 7.59 us -> 6.27 us  [per_device(): lax.all_to_all(lines.reshape(16, 48, 128), ('gy_0', 'gy_1', 'gz_0'), spli...]
  transfers between devices with their start and end apart: 8 -> 9, of which waited for: 5 -> 6; matrix products, arithmetic and copies ran while one was open for 0% -> 0% of each run, Pallas kernels for 13% -> 15%
where the time goes in v5:
time: 114 us; the launch traced here: 113 us
  Pallas kernels  36.2 us (32%)
  starting transfers between devices  31.9 us (28%)
  waiting for transfers between devices  22.3 us (20%)
  blocking collectives  15.8 us (14%)
  local copies, waits for them, and re-layouts  5.77 us (5%)
    all_to_all x1, blocking collectives, per_device(): lax.all_to_all(rows, 'gx', split_axis=0, concat_axis=0, tiled=True)  15.8 us
    pallas_call x2, Pallas kernels, collide(): pl.pallas_call(lambda *refs: collide_body(start, *refs), name='collide',...  13 us
    pallas_call x1, Pallas kernels, per_device(): pl.pallas_call(scatter_body, name='scatter', grid=(BLOCKS,), in_specs=[SM...  10.5 us
    ppermute x3, starting transfers between devices, ring(): lax.ppermute(high, axis, forward)  8.3 us
    all_to_all x1, waiting for transfers between devices, gathered_sum(): lax.all_to_all(copies, axes, split_axis=0, concat_axis=0, tiled=True)  8 us
    all_to_all x1, starting transfers between devices, gathered_sum(): lax.all_to_all(copies, axes, split_axis=0, concat_axis=0, tiled=True)  7.7 us
    all_to_all x1, starting transfers between devices, per_device(): lax.all_to_all(lines.reshape(16, 48, 128), ('gy_0', 'gy_1', 'gz_0'), spli...  6.4 us
    all_to_all x1, waiting for transfers between devices, per_device(): lax.all_to_all(lines.reshape(16, 48, 128), ('gy_0', 'gy_1', 'gz_0'), spli...  6.27 us
  transfers between devices with their start and end apart: 9, of which 6 were waited for; matrix products, arithmetic and copies ran while one was open for 0% of the time, Pallas kernels for 15%

profile of v5, /device:TPU:1, one launch (start us, length us, event | category | flops | bytes accessed | tf_op | source)
XLA Modules:
  0.0 113.4 jit_solution(12933006652923710295)
XLA Ops:
  0.7 1.3 %copy.18 = s32[32,32,16]{2,1,0:T(8,128)S(1)} copy(s32[32,32,16]{1,2,0:T(8,128)} %param.14) | data formatting | bytes 131072 | tf_op args[3]
  1.9 0.2 reshape.23.axis_ref
  2.2 1.0 copy-done.3
  3.1 10.5 %scatter.1 = (f32[32,128,128]{2,1,0:T(8,128)S(1)}, f32[3,128,128]{2,1,0:T(8,128)S(1)}, f32[40,128]{1,0:T(8,128)S(1)}, f32[40,128]{1,0:T(8,128)S(1)}) custom-call(s32[3]{0:T(128)S(1)} %copy-done.9, f32[3,81920]{1,0:T(4,128)S(1)} %copy-done, s32[640,128]{1,0:T(8,128)S(1)} %bitcast.12, s32[128,128]{1,0:T(8,128)S(1)} %reshape.23.axis_ref), custom_call_target="tpu_custom_call" | custom-call | tf_op jit(solution)/shard_map/scatter/pallas_call | solution.py:655
  13.6 2.1 %collective-permute-start = (f32[40,128]{1,0:T(8,128)S(1)}, f32[40,128]{1,0:T(8,128)S(1)}, u32[]{:S(2)}, u32[]{:S(2)}) collective-permute-start(f32[40,128]{1,0:T(8,128)S(1)} %get-tuple-element.41.xhi_ref), channel_id=1, source_target_pairs={{0,64},{64,128},{128,192},{192,0},{1,65},{65,129},{129,193},{193,1... | collective-permute-start | bytes 61448 | tf_op jit(solution)/shard_map/ppermute | solution.py:609
  15.7 1.4 %collective-permute-start.1 = (f32[40,128]{1,0:T(8,128)S(1)}, f32[40,128]{1,0:T(8,128)S(1)}, u32[]{:S(2)}, u32[]{:S(2)}) collective-permute-start(f32[40,128]{1,0:T(8,128)S(1)} %get-tuple-element.40.xlo_ref), channel_id=1, source_target_pairs={{64,0},{128,64},{192,128},{0,192},{65,1},{129,65},{193,129},{1,193... | collective-permute-start | bytes 61448 | tf_op jit(solution)/shard_map/ppermute | solution.py:609
  17.1 1.4 %planes.1 = (f32[4,160,128]{2,1,0:T(8,128)S(1)}, f32[40,128]{1,0:T(8,128)S(1)}, f32[40,128]{1,0:T(8,128)S(1)}, f32[160,128]{1,0:T(8,128)S(1)}, f32[160,128]{1,0:T(8,128)S(1)}) custom-call(f32[32,128,128]{2,1,0:T(8,128)S(1)} %get-tuple-element.37.s_ref, f32[3,128,128]{2,1,0:T(8,128)S(1)} %get-tuple-element.56.n_ref.refs_1_), custom_call_target="tpu_custom_call" | custom-call | flops 1000000000 | bytes 3000000 | tf_op jit(solution)/shard_map/planes/pallas_call | solution.py:665
  18.6 4.8 %collective-permute-start.2 = (f32[40,128]{1,0:T(8,128)S(1)}, f32[40,128]{1,0:T(8,128)S(1)}, u32[]{:S(2)}, u32[]{:S(2)}) collective-permute-start(f32[40,128]{1,0:T(8,128)S(1)} %get-tuple-element.47.yhi_ref), channel_id=1, source_target_pairs={{0,8},{8,16},{16,24},{24,32},{32,40},{40,48},{48,56},{56,0},{1,9},... | collective-permute-start | bytes 61448 | tf_op jit(solution)/shard_map/ppermute | solution.py:609
  23.5 0.9 collective-permute-done.2.from_low
  24.4 3.3 %collective-permute-done.3.from_high = f32[40,128]{1,0:T(8,128)S(1)} collective-permute-done((f32[40,128]{1,0:T(8,128)S(1)}, f32[40,128]{1,0:T(8,128)S(1)}, u32[]{:S(2)}, u32[]{:S(2)}) %collective-permute-start.3) | collective-permute-done | bytes 20512 | tf_op jit(solution)/shard_map/ppermute | solution.py:609
  27.8 1.4 %collective-permute-start.4 = (f32[160,128]{1,0:T(8,128)S(1)}, f32[160,128]{1,0:T(8,128)S(1)}, u32[]{:S(2)}, u32[]{:S(2)}) collective-permute-start(f32[160,128]{1,0:T(8,128)S(1)} %get-tuple-element.62.refs_7_.zhi_ref), channel_id=1, source_target_pairs={{0,1},{1,2},{2,3},{3,4},{4,5},{5,6},{6,7},{7,0},{8,9},{9,10},{10,1... | collective-permute-start | bytes 245768 | tf_op jit(solution)/shard_map/ppermute | solution.py:609
  29.2 2.8 %collective-permute-start.5 = (f32[160,128]{1,0:T(8,128)S(1)}, f32[160,128]{1,0:T(8,128)S(1)}, u32[]{:S(2)}, u32[]{:S(2)}) collective-permute-start(f32[160,128]{1,0:T(8,128)S(1)} %get-tuple-element.61.refs_6_.zlo_ref), channel_id=1, source_target_pairs={{1,0},{2,1},{3,2},{4,3},{5,4},{6,5},{7,6},{0,7},{9,8},{10,9},{11,1... | collective-permute-start | bytes 245768 | tf_op jit(solution)/shard_map/ppermute | solution.py:609
  32.0 2.3 %collective-permute-done.4.refs_8_.from_low = f32[160,128]{1,0:T(8,128)S(1)} collective-permute-done((f32[160,128]{1,0:T(8,128)S(1)}, f32[160,128]{1,0:T(8,128)S(1)}, u32[]{:S(2)}, u32[]{:S(2)}) %collective-permute-start.4) | collective-permute-done | bytes 81952 | tf_op jit(solution)/shard_map/ppermute | solution.py:609
  34.3 4.4 %cells.1 = f32[8,192,128]{2,1,0:T(8,128)} custom-call(f32[32,128,128]{2,1,0:T(8,128)S(1)} %get-tuple-element.37.s_ref, f32[4,160,128]{2,1,0:T(8,128)S(1)} %get-tuple-element.55.refs_0_.m_ref, f32[3,128,128]{2,1,0:T(8,128)S(1)} %get-tuple-element.56.n_ref.refs_1_, f32[40,128]{1,0:T(8,128)S(1)} %get-tuple-element.57.xlo_ref.refs_2_, ...), custom_call_target="tpu_custom_call" | custom-call | tf_op jit(solution)/shard_map/cells/pallas_call | solution.py:685
  38.7 5.3 %all-to-all-start = ((f32[8,192,128]{2,1,0:T(8,128)}), f32[8,192,128]{2,1,0:T(8,128)S(1)}, u32[]{:S(2)}, u32[]{:S(2)}) async-start(f32[8,192,128]{2,1,0:T(8,128)} %cells.1), calls=%async_computation | async-start | bytes 1572864 | tf_op jit(solution)/shard_map/all_to_all | solution.py:709
  44.1 1.1 views.1.refs_3_
  45.3 7.9 %collide.2.refs_4_ = f32[3,81920]{1,0:T(4,128)} custom-call(s32[3]{0:T(128)S(1)} %copy-done.9, f32[3,81920]{1,0:T(4,128)S(1)} %copy-done, s32[640,128]{1,0:T(8,128)S(1)} %bitcast.13, f32[24,136,128]{2,1,0:T(8,128)S(1)} %views.1.refs_3_), custom_call_target="tpu_custom_call" | custom-call | flops 4000000000 | bytes 4000000 | tf_op jit(solution)/shard_map/collide/pallas_call | solution.py:631
  53.1 1.2 %copy-done.10 = f32[24,136,128]{2,1,0:T(8,128)} copy-done((f32[24,136,128]{2,1,0:T(8,128)}, f32[24,136,128]{2,1,0:T(8,128)S(1)}, u32[]{:S(2)}) %copy-start.10) | copy-done | bytes 1671192
  54.3 1.5 %all-to-all-done.in_ref = f32[8,192,128]{2,1,0:T(8,128)S(1)} async-done(((f32[8,192,128]{2,1,0:T(8,128)}), f32[8,192,128]{2,1,0:T(8,128)S(1)}, u32[]{:S(2)}, u32[]{:S(2)}) %all-to-all-start) | async-done | bytes 786464 | tf_op jit(solution)/shard_map/all_to_all | solution.py:709
  55.9 1.8 %z_lines.1 = f32[768,128]{1,0:T(8,128)} custom-call(s32[3]{0:T(128)S(1)} %pad_add_fusion.first_ref, f32[8,192,128]{2,1,0:T(8,128)S(1)} %all-to-all-done.in_ref, bf16[4,64,128]{2,1,0:T(8,128)(2,1)S(1)} %copy-done.7, bf16[4,64,128]{2,1,0:T(8,128)(2,1)S(1)} %copy-done.8), custom_call_target="tpu_custom_call" | custom-call | tf_op jit(solution)/shard_map/z_lines/pallas_call | solution.py:713
  57.7 6.4 %all-to-all-start.1 = ((f32[16,48,128]{2,1,0:T(8,128)}), f32[16,48,128]{2,1,0:T(8,128)S(1)}, u32[]{:S(2)}, u32[]{:S(2)}) async-start(f32[16,48,128]{2,1,0:T(8,128)} %bitcast.4), calls=%async_computation.1 | async-start | bytes 786432 | tf_op jit(solution)/shard_map/all_to_all | solution.py:720
  64.1 1.4 %copy-done.11 = f32[24,136,128]{2,1,0:T(8,128)S(1)} copy-done((f32[24,136,128]{2,1,0:T(8,128)S(1)}, f32[24,136,128]{2,1,0:T(8,128)}, u32[]{:S(2)}) %copy-start.11) | copy-done | bytes 1671192
  65.5 5.2 %collide.3 = f32[3,81920]{1,0:T(4,128)} custom-call(s32[3]{0:T(128)S(1)} %copy-done.9, f32[3,81920]{1,0:T(4,128)S(1)} %copy-done, s32[640,128]{1,0:T(8,128)S(1)} %bitcast.14, f32[24,136,128]{2,1,0:T(8,128)S(1)} %copy-done.11, f32[3,81920]{1,0:T(4,128)} %collide.2.refs_4_), custom_call_target="tpu_custom_call", output_to_operand_aliasing={{}: (4, {})} | custom-call | flops 2400000000 | bytes 4000000 | tf_op jit(solution)/shard_map/collide/pallas_call | solution.py:631
  70.7 6.3 %all-to-all-done.1 = f32[16,48,128]{2,1,0:T(8,128)S(1)} async-done(((f32[16,48,128]{2,1,0:T(8,128)}), f32[16,48,128]{2,1,0:T(8,128)S(1)}, u32[]{:S(2)}, u32[]{:S(2)}) %all-to-all-start.1) | async-done | bytes 393248 | tf_op jit(solution)/shard_map/all_to_all | solution.py:720
  77.0 0.8 y_lines.1
  77.8 15.8 %all_to_all.20.in_ref = f32[4,384,128]{2,1,0:T(8,128)S(1)} all-to-all(f32[4,384,128]{2,1,0:T(8,128)S(1)} %y_lines.1), channel_id=1, replica_groups=mesh['gx'=4,'gy_0'=4,'gy_1'=2,'gz_0'=2,'gz_1'=4] {'gx'}, dimensions={0} | all-to-all | bytes 1572864 | tf_op jit(solution)/shard_map/all_to_all | solution.py:728
  93.6 1.7 %x_shells.1 = f32[1,128]{1,0:T(1,128)S(1)} custom-call(s32[3]{0:T(128)S(1)} %pad_add_fusion.first_ref, f32[4,384,128]{2,1,0:T(8,128)S(1)} %all_to_all.20.in_ref, bf16[512,512]{1,0:T(8,128)(2,1)S(1)} %copy-done.1, bf16[512,512]{1,0:T(8,128)(2,1)S(1)} %copy-done.2), custom_call_target="tpu_custom_call" | custom-call | tf_op jit(solution)/shard_map/x_shells/pallas_call | solution.py:730
  95.3 0.6 broadcast_in_dim.9
  95.9 7.7 %all-to-all-start.3 = ((f32[64,1,128]{2,1,0:T(1,128)}), f32[64,1,128]{2,1,0:T(1,128)S(1)}, u32[]{:S(2)}, u32[]{:S(2)}) async-start(f32[64,1,128]{2,1,0:T(1,128)} %broadcast_in_dim.9), calls=%async_computation.3 | async-start | bytes 65536 | tf_op jit(solution)/shard_map/all_to_all | solution.py:615
  103.6 1.2 %x_modes.1 = f32[2,3,2,64,128]{4,3,2,1,0:T(8,128)} custom-call(f32[4,384,128]{2,1,0:T(8,128)S(1)} %all_to_all.20.in_ref, bf16[512,512]{1,0:T(8,128)(2,1)S(1)} %copy-done.1, bf16[512,512]{1,0:T(8,128)(2,1)S(1)} %copy-done.2), custom_call_target="tpu_custom_call" | custom-call | flops 2000000000 | bytes 3000000 | tf_op jit(solution)/shard_map/x_modes/pallas_call | solution.py:739
  104.8 8.0 %all-to-all-done.3 = f32[64,1,128]{2,1,0:T(1,128)S(1)} async-done(((f32[64,1,128]{2,1,0:T(1,128)}), f32[64,1,128]{2,1,0:T(1,128)S(1)}, u32[]{:S(2)}, u32[]{:S(2)}) %all-to-all-start.3) | async-done | bytes 32800 | tf_op jit(solution)/shard_map/all_to_all | solution.py:615
  112.9 0.5 multiply_bitcast_fusion
  (31 shorter events, 0.4 us)
Async XLA Ops:
  0.6 1.5 %copy-start.9 = (s32[3]{0:T(128)S(1)}, s32[3]{0:T(128)}, u32[]{:S(2)}) copy-start(s32[3]{0:T(128)} %refs_0_.3) | copy-start | bytes 40
  0.6 1.5 %copy-start = (f32[3,81920]{1,0:T(4,128)S(1)}, f32[3,81920]{1,0:T(4,128)}, u32[]{:S(2)}) copy-start(f32[3,81920]{1,0:T(4,128)} %refs_1_.3) | copy-start | bytes 2949124
  2.1 1.0 copy-start.3
  13.6 4.9 %collective-permute-start = (f32[40,128]{1,0:T(8,128)S(1)}, f32[40,128]{1,0:T(8,128)S(1)}, u32[]{:S(2)}, u32[]{:S(2)}) collective-permute-start(f32[40,128]{1,0:T(8,128)S(1)} %get-tuple-element.41.xhi_ref), channel_id=1, source_target_pairs={{0,64},{64,128},{128,192},{192,0},{1,65},{65,129},{129,193},{193,1... | collective-permute-start | bytes 61448 | tf_op jit(solution)/shard_map/ppermute | solution.py:609
  15.7 2.8 %collective-permute-start.1 = (f32[40,128]{1,0:T(8,128)S(1)}, f32[40,128]{1,0:T(8,128)S(1)}, u32[]{:S(2)}, u32[]{:S(2)}) collective-permute-start(f32[40,128]{1,0:T(8,128)S(1)} %get-tuple-element.40.xlo_ref), channel_id=1, source_target_pairs={{64,0},{128,64},{192,128},{0,192},{65,1},{129,65},{193,129},{1,193... | collective-permute-start | bytes 61448 | tf_op jit(solution)/shard_map/ppermute | solution.py:609
  18.6 5.7 %collective-permute-start.2 = (f32[40,128]{1,0:T(8,128)S(1)}, f32[40,128]{1,0:T(8,128)S(1)}, u32[]{:S(2)}, u32[]{:S(2)}) collective-permute-start(f32[40,128]{1,0:T(8,128)S(1)} %get-tuple-element.47.yhi_ref), channel_id=1, source_target_pairs={{0,8},{8,16},{16,24},{24,32},{32,40},{40,48},{48,56},{56,0},{1,9},... | collective-permute-start | bytes 61448 | tf_op jit(solution)/shard_map/ppermute | solution.py:609
  23.5 4.2 %collective-permute-start.3 = (f32[40,128]{1,0:T(8,128)S(1)}, f32[40,128]{1,0:T(8,128)S(1)}, u32[]{:S(2)}, u32[]{:S(2)}) collective-permute-start(f32[40,128]{1,0:T(8,128)S(1)} %get-tuple-element.46.ylo_ref), channel_id=1, source_target_pairs={{8,0},{16,8},{24,16},{32,24},{40,32},{48,40},{56,48},{0,56},{9,1},... | collective-permute-start | bytes 61448 | tf_op jit(solution)/shard_map/ppermute | solution.py:609
  27.8 6.5 %collective-permute-start.4 = (f32[160,128]{1,0:T(8,128)S(1)}, f32[160,128]{1,0:T(8,128)S(1)}, u32[]{:S(2)}, u32[]{:S(2)}) collective-permute-start(f32[160,128]{1,0:T(8,128)S(1)} %get-tuple-element.62.refs_7_.zhi_ref), channel_id=1, source_target_pairs={{0,1},{1,2},{2,3},{3,4},{4,5},{5,6},{6,7},{7,0},{8,9},{9,10},{10,1... | collective-permute-start | bytes 245768 | tf_op jit(solution)/shard_map/ppermute | solution.py:609
  29.2 5.2 %collective-permute-start.5 = (f32[160,128]{1,0:T(8,128)S(1)}, f32[160,128]{1,0:T(8,128)S(1)}, u32[]{:S(2)}, u32[]{:S(2)}) collective-permute-start(f32[160,128]{1,0:T(8,128)S(1)} %get-tuple-element.61.refs_6_.zlo_ref), channel_id=1, source_target_pairs={{1,0},{2,1},{3,2},{4,3},{5,4},{6,5},{7,6},{0,7},{9,8},{10,9},{11,1... | collective-permute-start | bytes 245768 | tf_op jit(solution)/shard_map/ppermute | solution.py:609
  38.7 17.1 %all-to-all-start = ((f32[8,192,128]{2,1,0:T(8,128)}), f32[8,192,128]{2,1,0:T(8,128)S(1)}, u32[]{:S(2)}, u32[]{:S(2)}) async-start(f32[8,192,128]{2,1,0:T(8,128)} %cells.1), calls=%async_computation | async-start | bytes 1572864 | tf_op jit(solution)/shard_map/all_to_all | solution.py:709
  44.1 1.1 copy-start.4
  45.2 10.6 %copy-start.7 = (bf16[4,64,128]{2,1,0:T(8,128)(2,1)S(1)}, bf16[4,64,128]{2,1,0:T(8,128)(2,1)}, u32[]{:S(2)}) copy-start(bf16[4,64,128]{2,1,0:T(8,128)(2,1)} %constant.46.clone.fh_ref) | copy-start | bytes 196612
  45.2 10.6 %copy-start.8 = (bf16[4,64,128]{2,1,0:T(8,128)(2,1)S(1)}, bf16[4,64,128]{2,1,0:T(8,128)(2,1)}, u32[]{:S(2)}) copy-start(bf16[4,64,128]{2,1,0:T(8,128)(2,1)} %constant.47.clone.fl_ref) | copy-start | bytes 196612
  53.1 1.2 %copy-start.10 = (f32[24,136,128]{2,1,0:T(8,128)}, f32[24,136,128]{2,1,0:T(8,128)S(1)}, u32[]{:S(2)}) copy-start(f32[24,136,128]{2,1,0:T(8,128)S(1)} %views.1.refs_3_) | copy-start | bytes 5013508
  57.7 19.3 %all-to-all-start.1 = ((f32[16,48,128]{2,1,0:T(8,128)}), f32[16,48,128]{2,1,0:T(8,128)S(1)}, u32[]{:S(2)}, u32[]{:S(2)}) async-start(f32[16,48,128]{2,1,0:T(8,128)} %bitcast.4), calls=%async_computation.1 | async-start | bytes 786432 | tf_op jit(solution)/shard_map/all_to_all | solution.py:720
  64.1 1.4 %copy-start.11 = (f32[24,136,128]{2,1,0:T(8,128)S(1)}, f32[24,136,128]{2,1,0:T(8,128)}, u32[]{:S(2)}) copy-start(f32[24,136,128]{2,1,0:T(8,128)} %copy-done.10) | copy-start | bytes 5013508
  65.5 11.5 %copy-start.5 = (bf16[512,256]{1,0:T(8,128)(2,1)S(1)}, bf16[512,256]{1,0:T(8,128)(2,1)}, u32[]{:S(2)}) copy-start(bf16[512,256]{1,0:T(8,128)(2,1)} %constant.48.clone.fh_ref) | copy-start | bytes 786436
  65.5 11.5 %copy-start.6 = (bf16[512,256]{1,0:T(8,128)(2,1)S(1)}, bf16[512,256]{1,0:T(8,128)(2,1)}, u32[]{:S(2)}) copy-start(bf16[512,256]{1,0:T(8,128)(2,1)} %constant.49.clone.fl_ref) | copy-start | bytes 786436
  77.0 16.6 %copy-start.1 = (bf16[512,512]{1,0:T(8,128)(2,1)S(1)}, bf16[512,512]{1,0:T(8,128)(2,1)}, u32[]{:S(2)}) copy-start(bf16[512,512]{1,0:T(8,128)(2,1)} %constant.50.clone.fh_ref) | copy-start | bytes 1572868
  77.0 16.6 %copy-start.2 = (bf16[512,512]{1,0:T(8,128)(2,1)S(1)}, bf16[512,512]{1,0:T(8,128)(2,1)}, u32[]{:S(2)}) copy-start(bf16[512,512]{1,0:T(8,128)(2,1)} %constant.51.clone.fl_ref) | copy-start | bytes 1572868
  95.9 16.9 %all-to-all-start.3 = ((f32[64,1,128]{2,1,0:T(1,128)}), f32[64,1,128]{2,1,0:T(1,128)S(1)}, u32[]{:S(2)}, u32[]{:S(2)}) async-start(f32[64,1,128]{2,1,0:T(1,128)} %broadcast_in_dim.9), calls=%async_computation.3 | async-start | bytes 65536 | tf_op jit(solution)/shard_map/all_to_all | solution.py:615
  103.6 9.3 %copy-start.12 = (f32[1,64]{1,0:T(1,128)S(1)}, f32[1,64]{1,0:T(1,128)}, u32[]{:S(2)}) copy-start(f32[1,64]{1,0:T(1,128)} %constant.54) | copy-start | bytes 772

commit v6 on v5

--- a/solution.py
+++ b/solution.py
@@ -530,7 +530,8 @@
                 out_ref[pl.ds(16 * c + 4 * r + k, 16, stride=48), :] = g[k]
 
 
-def y_body(in_ref, fh_ref, fl_ref, out_ref):
+def y_body(first_ref, in_ref, fh_ref, fl_ref, extra_ref, *refs):
+    own_ref = refs[-1]
     both = in_ref[...].reshape(16, 48, 128)
     data = jnp.concatenate(
         [both[:, 16 * c : 16 * c + 16].reshape(256, 128) for c in range(3)], axis=1
@@ -544,19 +545,23 @@
         odd = res[256:512, 128 * c : 128 * c + 128]
         out = even + jnp.where(is_real, lroll(odd, -4), -lroll(odd, 4))
         for d in range(4):
-            out_ref[d, 64 * c : 64 * c + 64, :] = out[64 * d : 64 * d + 64]
-            out_ref[d, 192 + 64 * c : 256 + 64 * c, :] = out[0:64]
-
-
-def x_lines(in_ref, fh_ref, fl_ref, first):
-    data = jnp.concatenate([in_ref[s, first : first + 192, :] for s in range(4)], axis=1)
+            own_ref[d, 64 * c : 64 * c + 64, :] = out[64 * d : 64 * d + 64]
+            extra_ref[d, 64 * c : 64 * c + 64, :] = out[0:64]
+    for k in range(4):
+        refs[k][...] = own_ref[(first_ref[3] + k) & 3]
+
+
+def x_lines(in_ref, fh_ref, fl_ref):
+    data = jnp.concatenate([in_ref[s] for s in range(4)], axis=1)
     high, low = split(data)
     fh, fl = fh_ref[...], fl_ref[...]
     return dot(high, fh) + dot(low, fh) + dot(high, fl)
 
 
-def mode_body(in_ref, fh_ref, fl_ref, out_ref):
-    res = x_lines(in_ref, fh_ref, fl_ref, 0)
+def mode_body(first_ref, a_ref, b_ref, c_ref, d_ref, fh_ref, fl_ref, out_ref, all_ref):
+    for k, part in enumerate((a_ref, b_ref, c_ref, d_ref)):
+        all_ref[(first_ref[3] - k) & 3] = part[...]
+    res = x_lines(all_ref, fh_ref, fl_ref)
     for part in range(2):
         for c in range(3):
             for kz in range(2):
@@ -565,7 +570,7 @@
 
 
 def shell_body(first_ref, in_ref, fh_ref, fl_ref, shell_ref, sums_ref):
-    res = x_lines(in_ref, fh_ref, fl_ref, 192)
+    res = x_lines(in_ref, fh_ref, fl_ref)
     ky = iota((64, 128), 0)
     kx = iota((64, 128), 1)
     kx = jnp.where(kx >= NX // 2, kx - NX, kx)
@@ -591,7 +596,7 @@
     cumulative = sums_ref[...]
     before = jnp.where(iota((NSHELL, 128), 0) == 0, 0.0, sroll(cumulative, 1))
     own = jnp.concatenate([cumulative - before, jnp.zeros((64, 128), F32)], axis=0)
-    shell_ref[...] = jnp.sum(own.T, axis=0, keepdims=True)
+    shell_ref[...] = jnp.broadcast_to(jnp.sum(own.T, axis=0, keepdims=True), (64, 128))
 
 
 def struct(*shape):
@@ -607,12 +612,6 @@
     backward = [(target, source) for source, target in forward]
     low, high = x
     return lax.ppermute(high, axis, forward), lax.ppermute(low, axis, backward)
-
-
-def gathered_sum(x, axes):
-    count = lax.axis_size(axes)
-    copies = jnp.broadcast_to(x[None], (count, *x.shape))
-    return jnp.sum(lax.all_to_all(copies, axes, split_axis=0, concat_axis=0, tiled=True), axis=0)
 
 
 def params(mib):
@@ -704,7 +703,8 @@
         cost_estimate=pl.CostEstimate(flops=1_000_000_000, bytes_accessed=3_000_000, transcendentals=0),
     )(*pieces)
     first = jnp.stack(
-        [lax.axis_index(GY_GZ) * 2, lax.axis_index("gx") * 64, lax.axis_index("gz_1")]
+        [lax.axis_index(GY_GZ) * 2, lax.axis_index("gx") * 64, lax.axis_index("gz_1"),
+         lax.axis_index("gx")]
     ).astype(jnp.int32)
     arrived = lax.all_to_all(sent, GZ, split_axis=0, concat_axis=0, tiled=True)
     updated = collide(0, EARLY, grid_shift, velocity, place, views, None)
@@ -722,28 +722,39 @@
     )
     new_velocity = collide(EARLY, STEPS, grid_shift, velocity, place, views, updated)
     pencil, new_velocity = lax.optimization_barrier((pencil, new_velocity))
-    rows = pl.pallas_call(y_body, name="y_lines", out_shape=struct(4, 384, 128), compiler_params=params(12))(
-        pencil.reshape(768, 128), *y_tables()
-    )
-    columns = lax.all_to_all(rows, "gx", split_axis=0, concat_axis=0, tiled=True)
+    extra, *own = pl.pallas_call(
+        y_body,
+        name="y_lines",
+        in_specs=[SMEM, vmem, vmem, vmem],
+        out_shape=[struct(4, 192, 128)] + [struct(192, 128)] * 4,
+        scratch_shapes=[pltpu.VMEM((4, 192, 128), F32)],
+        compiler_params=params(12),
+    )(first, pencil.reshape(768, 128), *y_tables())
+    columns = lax.all_to_all(extra, "gx", split_axis=0, concat_axis=0, tiled=True)
     tables = x_tables()
     shells = pl.pallas_call(
         shell_body,
         name="x_shells",
         in_specs=[SMEM, vmem, vmem, vmem],
-        out_shape=struct(1, 128),
+        out_shape=struct(64, 128),
         scratch_shapes=[pltpu.VMEM((NSHELL, 128), F32)],
         compiler_params=params(12),
     )(first, columns, *tables)
-    columns, shells = lax.optimization_barrier((columns, shells))
+    own, shells = lax.optimization_barrier((own, shells))
+    gathered = lax.all_to_all(shells.reshape(64, 1, 128), GY_GZ, split_axis=0, concat_axis=0, tiled=True)
+    received = [own[0]] + [
+        lax.ppermute(own[k], "gx", [(i, (i + k) % 4) for i in range(4)]) for k in range(1, 4)
+    ]
     modes = pl.pallas_call(
         mode_body,
         name="x_modes",
+        in_specs=[SMEM] + [vmem] * 6,
         out_shape=struct(2, 3, 2, 64, 128),
+        scratch_shapes=[pltpu.VMEM((4, 192, 128), F32)],
         compiler_params=params(12),
         cost_estimate=pl.CostEstimate(flops=2_000_000_000, bytes_accessed=3_000_000, transcendentals=0),
-    )(columns, *tables)
-    total = gathered_sum(shells, GY_GZ)
+    )(first, *received, *tables)
+    total = jnp.sum(gathered, axis=0)
     spectrum = total[0, :NSHELL] / shell_counts()
     return new_velocity, modes, spectrum
 

time: 114 us -> 112 us (0.982)
  blocking collectives: 15.8 us -> 11.6 us
  starting transfers between devices: 31.9 us -> 34.7 us
  Pallas kernels: 36.2 us -> 37.9 us
  waiting for transfers between devices: 22.3 us -> 20.7 us
    all_to_all x1, blocking collectives: 15.8 us -> 11.6 us  [per_device(): lax.all_to_all(extra, 'gx', split_axis=0, concat_axis=0, tiled=True)]
    ppermute x0 -> x3, starting transfers between devices: none -> 2.85 us  [per_device(): lax.ppermute(own[k], 'gx', [(i, (i + k) % 4) for i in range(4)])]
    all_to_all x1, waiting for transfers between devices: 8 us -> 6.32 us  [per_device(): lax.all_to_all(shells.reshape(64, 1, 128), GY_GZ, split_axis=0, concat_ax...]
    pallas_call x2, Pallas kernels: 2.02 us -> 3.17 us  [the longest x1 1.81 us: per_device(): pl.pallas_call(mode_body, name='x_modes', in_specs=[SMEM] + [vmem] * 6, o...]
  transfers between devices with their start and end apart: 9 -> 12, of which waited for: 6 -> 6; matrix products, arithmetic and copies ran while one was open for 0% -> 1% of each run, Pallas kernels for 15% -> 14%
where the time goes in v6:
time: 112 us
  Pallas kernels  37.9 us (34%)
  starting transfers between devices  34.7 us (31%)
  waiting for transfers between devices  20.7 us (18%)
  blocking collectives  11.6 us (10%)
  local copies, waits for them, and re-layouts  5.11 us (5%)
    pallas_call x2, Pallas kernels, collide(): pl.pallas_call(lambda *refs: collide_body(start, *refs), name='collide',...  13 us
    all_to_all x1, blocking collectives, per_device(): lax.all_to_all(extra, 'gx', split_axis=0, concat_axis=0, tiled=True)  11.6 us
    pallas_call x1, Pallas kernels, per_device(): pl.pallas_call(scatter_body, name='scatter', grid=(BLOCKS,), in_specs=[SM...  10.5 us
    ppermute x3, starting transfers between devices, ring(): lax.ppermute(high, axis, forward)  8.3 us
    all_to_all x1, starting transfers between devices, per_device(): lax.all_to_all(shells.reshape(64, 1, 128), GY_GZ, split_axis=0, concat_ax...  7.68 us
    all_to_all x1, starting transfers between devices, per_device(): lax.all_to_all(lines.reshape(16, 48, 128), ('gy_0', 'gy_1', 'gz_0'), spli...  6.4 us
    all_to_all x1, waiting for transfers between devices, per_device(): lax.all_to_all(shells.reshape(64, 1, 128), GY_GZ, split_axis=0, concat_ax...  6.32 us
    all_to_all x1, waiting for transfers between devices, per_device(): lax.all_to_all(lines.reshape(16, 48, 128), ('gy_0', 'gy_1', 'gz_0'), spli...  6.26 us
  transfers between devices with their start and end apart: 12, of which 6 were waited for; matrix products, arithmetic and copies ran while one was open for 1% of the time, Pallas kernels for 14%

profile of v6, /device:TPU:1, one launch (start us, length us, event | category | flops | bytes accessed | tf_op | source)
XLA Modules:
  0.0 111.5 jit_solution(12498481334999372395)
XLA Ops:
  0.7 1.3 %copy.17 = s32[32,32,16]{2,1,0:T(8,128)S(1)} copy(s32[32,32,16]{1,2,0:T(8,128)} %param.14) | data formatting | bytes 131072 | tf_op args[3]
  2.2 1.0 copy-done.3
  3.1 10.5 %scatter.1 = (f32[32,128,128]{2,1,0:T(8,128)S(1)}, f32[3,128,128]{2,1,0:T(8,128)S(1)}, f32[40,128]{1,0:T(8,128)S(1)}, f32[40,128]{1,0:T(8,128)S(1)}) custom-call(s32[3]{0:T(128)S(1)} %copy-done.9, f32[3,81920]{1,0:T(4,128)S(1)} %copy-done, s32[640,128]{1,0:T(8,128)S(1)} %bitcast.14, s32[128,128]{1,0:T(8,128)S(1)} %reshape.23.axis_ref), custom_call_target="tpu_custom_call" | custom-call | tf_op jit(solution)/shard_map/scatter/pallas_call | solution.py:654
  13.6 2.1 %collective-permute-start = (f32[40,128]{1,0:T(8,128)S(1)}, f32[40,128]{1,0:T(8,128)S(1)}, u32[]{:S(2)}, u32[]{:S(2)}) collective-permute-start(f32[40,128]{1,0:T(8,128)S(1)} %get-tuple-element.49.xhi_ref), channel_id=1, source_target_pairs={{0,64},{64,128},{128,192},{192,0},{1,65},{65,129},{129,193},{193,1... | collective-permute-start | bytes 61448 | tf_op jit(solution)/shard_map/ppermute | solution.py:614
  15.7 1.4 %collective-permute-start.1 = (f32[40,128]{1,0:T(8,128)S(1)}, f32[40,128]{1,0:T(8,128)S(1)}, u32[]{:S(2)}, u32[]{:S(2)}) collective-permute-start(f32[40,128]{1,0:T(8,128)S(1)} %get-tuple-element.48.xlo_ref), channel_id=1, source_target_pairs={{64,0},{128,64},{192,128},{0,192},{65,1},{129,65},{193,129},{1,193... | collective-permute-start | bytes 61448 | tf_op jit(solution)/shard_map/ppermute | solution.py:614
  17.1 1.4 %planes.1 = (f32[4,160,128]{2,1,0:T(8,128)S(1)}, f32[40,128]{1,0:T(8,128)S(1)}, f32[40,128]{1,0:T(8,128)S(1)}, f32[160,128]{1,0:T(8,128)S(1)}, f32[160,128]{1,0:T(8,128)S(1)}) custom-call(f32[32,128,128]{2,1,0:T(8,128)S(1)} %get-tuple-element.45.s_ref, f32[3,128,128]{2,1,0:T(8,128)S(1)} %get-tuple-element.64.n_ref.refs_1_), custom_call_target="tpu_custom_call" | custom-call | flops 1000000000 | bytes 3000000 | tf_op jit(solution)/shard_map/planes/pallas_call | solution.py:664
  18.6 4.8 %collective-permute-start.2 = (f32[40,128]{1,0:T(8,128)S(1)}, f32[40,128]{1,0:T(8,128)S(1)}, u32[]{:S(2)}, u32[]{:S(2)}) collective-permute-start(f32[40,128]{1,0:T(8,128)S(1)} %get-tuple-element.55.yhi_ref), channel_id=1, source_target_pairs={{0,8},{8,16},{16,24},{24,32},{32,40},{40,48},{48,56},{56,0},{1,9},... | collective-permute-start | bytes 61448 | tf_op jit(solution)/shard_map/ppermute | solution.py:614
  23.5 0.9 collective-permute-done.2.from_low
  24.4 3.3 %collective-permute-done.3.from_high = f32[40,128]{1,0:T(8,128)S(1)} collective-permute-done((f32[40,128]{1,0:T(8,128)S(1)}, f32[40,128]{1,0:T(8,128)S(1)}, u32[]{:S(2)}, u32[]{:S(2)}) %collective-permute-start.3) | collective-permute-done | bytes 20512 | tf_op jit(solution)/shard_map/ppermute | solution.py:614
  27.8 1.4 %collective-permute-start.4 = (f32[160,128]{1,0:T(8,128)S(1)}, f32[160,128]{1,0:T(8,128)S(1)}, u32[]{:S(2)}, u32[]{:S(2)}) collective-permute-start(f32[160,128]{1,0:T(8,128)S(1)} %get-tuple-element.70.refs_7_.zhi_ref), channel_id=1, source_target_pairs={{0,1},{1,2},{2,3},{3,4},{4,5},{5,6},{6,7},{7,0},{8,9},{9,10},{10,1... | collective-permute-start | bytes 245768 | tf_op jit(solution)/shard_map/ppermute | solution.py:614
  29.2 2.8 %collective-permute-start.5 = (f32[160,128]{1,0:T(8,128)S(1)}, f32[160,128]{1,0:T(8,128)S(1)}, u32[]{:S(2)}, u32[]{:S(2)}) collective-permute-start(f32[160,128]{1,0:T(8,128)S(1)} %get-tuple-element.69.refs_6_.zlo_ref), channel_id=1, source_target_pairs={{1,0},{2,1},{3,2},{4,3},{5,4},{6,5},{7,6},{0,7},{9,8},{10,9},{11,1... | collective-permute-start | bytes 245768 | tf_op jit(solution)/shard_map/ppermute | solution.py:614
  32.0 2.3 %collective-permute-done.4.refs_8_.from_low = f32[160,128]{1,0:T(8,128)S(1)} collective-permute-done((f32[160,128]{1,0:T(8,128)S(1)}, f32[160,128]{1,0:T(8,128)S(1)}, u32[]{:S(2)}, u32[]{:S(2)}) %collective-permute-start.4) | collective-permute-done | bytes 81952 | tf_op jit(solution)/shard_map/ppermute | solution.py:614
  34.3 4.4 %cells.1 = f32[8,192,128]{2,1,0:T(8,128)} custom-call(f32[32,128,128]{2,1,0:T(8,128)S(1)} %get-tuple-element.45.s_ref, f32[4,160,128]{2,1,0:T(8,128)S(1)} %get-tuple-element.63.refs_0_.m_ref, f32[3,128,128]{2,1,0:T(8,128)S(1)} %get-tuple-element.64.n_ref.refs_1_, f32[40,128]{1,0:T(8,128)S(1)} %get-tuple-element.65.xlo_ref.refs_2_, ...), custom_call_target="tpu_custom_call" | custom-call | tf_op jit(solution)/shard_map/cells/pallas_call | solution.py:684
  38.7 5.3 %all-to-all-start = ((f32[8,192,128]{2,1,0:T(8,128)}), f32[8,192,128]{2,1,0:T(8,128)S(1)}, u32[]{:S(2)}, u32[]{:S(2)}) async-start(f32[8,192,128]{2,1,0:T(8,128)} %cells.1), calls=%async_computation | async-start | bytes 1572864 | tf_op jit(solution)/shard_map/all_to_all | solution.py:709
  44.1 1.1 views.1.refs_3_
  45.2 7.9 %collide.2.refs_4_ = f32[3,81920]{1,0:T(4,128)} custom-call(s32[3]{0:T(128)S(1)} %copy-done.9, f32[3,81920]{1,0:T(4,128)S(1)} %copy-done, s32[640,128]{1,0:T(8,128)S(1)} %bitcast.15, f32[24,136,128]{2,1,0:T(8,128)S(1)} %views.1.refs_3_), custom_call_target="tpu_custom_call" | custom-call | flops 4000000000 | bytes 4000000 | tf_op jit(solution)/shard_map/collide/pallas_call | solution.py:630
  53.1 1.2 %copy-done.10 = f32[24,136,128]{2,1,0:T(8,128)} copy-done((f32[24,136,128]{2,1,0:T(8,128)}, f32[24,136,128]{2,1,0:T(8,128)S(1)}, u32[]{:S(2)}) %copy-start.10) | copy-done | bytes 1671192
  54.3 1.6 %all-to-all-done.in_ref = f32[8,192,128]{2,1,0:T(8,128)S(1)} async-done(((f32[8,192,128]{2,1,0:T(8,128)}), f32[8,192,128]{2,1,0:T(8,128)S(1)}, u32[]{:S(2)}, u32[]{:S(2)}) %all-to-all-start) | async-done | bytes 786464 | tf_op jit(solution)/shard_map/all_to_all | solution.py:709
  55.8 1.8 %z_lines.1 = f32[768,128]{1,0:T(8,128)} custom-call(s32[4]{0:T(128)S(1)} %pad_add_fusion.first_ref, f32[8,192,128]{2,1,0:T(8,128)S(1)} %all-to-all-done.in_ref, bf16[4,64,128]{2,1,0:T(8,128)(2,1)S(1)} %copy-done.7, bf16[4,64,128]{2,1,0:T(8,128)(2,1)S(1)} %copy-done.8), custom_call_target="tpu_custom_call" | custom-call | tf_op jit(solution)/shard_map/z_lines/pallas_call | solution.py:713
  57.6 6.4 %all-to-all-start.1 = ((f32[16,48,128]{2,1,0:T(8,128)}), f32[16,48,128]{2,1,0:T(8,128)S(1)}, u32[]{:S(2)}, u32[]{:S(2)}) async-start(f32[16,48,128]{2,1,0:T(8,128)} %bitcast.5), calls=%async_computation.1 | async-start | bytes 786432 | tf_op jit(solution)/shard_map/all_to_all | solution.py:720
  64.0 1.4 %copy-done.11 = f32[24,136,128]{2,1,0:T(8,128)S(1)} copy-done((f32[24,136,128]{2,1,0:T(8,128)S(1)}, f32[24,136,128]{2,1,0:T(8,128)}, u32[]{:S(2)}) %copy-start.11) | copy-done | bytes 1671192
  65.5 5.2 %collide.3 = f32[3,81920]{1,0:T(4,128)} custom-call(s32[3]{0:T(128)S(1)} %copy-done.9, f32[3,81920]{1,0:T(4,128)S(1)} %copy-done, s32[640,128]{1,0:T(8,128)S(1)} %bitcast.16, f32[24,136,128]{2,1,0:T(8,128)S(1)} %copy-done.11, f32[3,81920]{1,0:T(4,128)} %collide.2.refs_4_), custom_call_target="tpu_custom_call", output_to_operand_aliasing={{}: (4, {})} | custom-call | flops 2400000000 | bytes 4000000 | tf_op jit(solution)/shard_map/collide/pallas_call | solution.py:630
  70.7 6.3 %all-to-all-done.1 = f32[16,48,128]{2,1,0:T(8,128)S(1)} async-done(((f32[16,48,128]{2,1,0:T(8,128)}), f32[16,48,128]{2,1,0:T(8,128)S(1)}, u32[]{:S(2)}, u32[]{:S(2)}) %all-to-all-start.1) | async-done | bytes 393248 | tf_op jit(solution)/shard_map/all_to_all | solution.py:720
  76.9 1.4 %y_lines.1 = (f32[4,192,128]{2,1,0:T(8,128)S(1)}, f32[192,128]{1,0:T(8,128)S(1)}, f32[192,128]{1,0:T(8,128)S(1)}, f32[192,128]{1,0:T(8,128)S(1)}, f32[192,128]{1,0:T(8,128)S(1)}) custom-call(s32[4]{0:T(128)S(1)} %pad_add_fusion.first_ref, f32[768,128]{1,0:T(8,128)S(1)} %bitcast.13, bf16[512,256]{1,0:T(8,128)(2,1)S(1)} %copy-done.5, ...), custom_call_target="tpu_custom_call" | custom-call | tf_op jit(solution)/shard_map/y_lines/pallas_call | solution.py:725
  78.3 11.6 %all_to_all.20.in_ref = f32[4,192,128]{2,1,0:T(8,128)S(1)} all-to-all(f32[4,192,128]{2,1,0:T(8,128)S(1)} %get-tuple-element.81), channel_id=1, replica_groups=mesh['gx'=4,'gy_0'=4,'gy_1'=2,'gz_0'=2,'gz_1'=4] {'gx'}, dimensions={0} | all-to-all | bytes 786432 | tf_op jit(solution)/shard_map/all_to_all | solution.py:733
  89.9 2.3 %x_shells.1 = f32[64,128]{1,0:T(8,128)} custom-call(s32[4]{0:T(128)S(1)} %pad_add_fusion.first_ref, f32[4,192,128]{2,1,0:T(8,128)S(1)} %all_to_all.20.in_ref, bf16[512,512]{1,0:T(8,128)(2,1)S(1)} %copy-done.1, bf16[512,512]{1,0:T(8,128)(2,1)S(1)} %copy-done.2), custom_call_target="tpu_custom_call" | custom-call | tf_op jit(solution)/shard_map/x_shells/pallas_call | solution.py:735
  92.2 7.7 %all-to-all-start.3 = ((f32[64,1,128]{2,1,0:T(1,128)}), f32[64,1,128]{2,1,0:T(1,128)S(1)}, u32[]{:S(2)}, u32[]{:S(2)}) async-start(f32[64,1,128]{2,1,0:T(1,128)} %bitcast.8), calls=%async_computation.3 | async-start | bytes 65536 | tf_op jit(solution)/shard_map/all_to_all | solution.py:744
  100.3 1.8 %collective-permute-start.7 = (f32[192,128]{1,0:T(8,128)S(1)}, f32[192,128]{1,0:T(8,128)S(1)}, u32[]{:S(2)}, u32[]{:S(2)}) collective-permute-start(f32[192,128]{1,0:T(8,128)S(1)} %get-tuple-element.84), channel_id=1, source_target_pairs={{0,128},{64,192},{128,0},{192,64},{1,129},{65,193},{129,1},{193,65... | collective-permute-start | bytes 294920 | tf_op jit(solution)/shard_map/ppermute | solution.py:746
  102.1 0.7 collective-permute-start.8
  102.8 6.3 %all-to-all-done.3 = f32[64,1,128]{2,1,0:T(1,128)S(1)} async-done(((f32[64,1,128]{2,1,0:T(1,128)}), f32[64,1,128]{2,1,0:T(1,128)S(1)}, u32[]{:S(2)}, u32[]{:S(2)}) %all-to-all-start.3) | async-done | bytes 32800 | tf_op jit(solution)/shard_map/all_to_all | solution.py:744
  109.2 0.5 multiply_bitcast_fusion
  109.7 1.8 %x_modes.1 = f32[2,3,2,64,128]{4,3,2,1,0:T(8,128)} custom-call(s32[4]{0:T(128)S(1)} %pad_add_fusion.first_ref, f32[192,128]{1,0:T(8,128)S(1)} %get-tuple-element.82.a_ref, f32[192,128]{1,0:T(8,128)S(1)} %collective-permute-done.6.b_ref, f32[192,128]{1,0:T(8,128)S(1)} %collective-permute-done.7.c_ref, f32[192,128]{1,0:T(8,128)S(1)} %collective-permute-done.8.d_ref, ...), custom_call_target="tpu_custom_call" | custom-call | flops 2000000000 | bytes 3000000 | tf_op jit(solution)/shard_map/x_modes/pallas_call | solution.py:748
  (36 shorter events, 1.0 us)
Async XLA Ops:
  0.6 1.5 %copy-start.9 = (s32[3]{0:T(128)S(1)}, s32[3]{0:T(128)}, u32[]{:S(2)}) copy-start(s32[3]{0:T(128)} %refs_0_.3) | copy-start | bytes 40
  0.6 1.5 %copy-start = (f32[3,81920]{1,0:T(4,128)S(1)}, f32[3,81920]{1,0:T(4,128)}, u32[]{:S(2)}) copy-start(f32[3,81920]{1,0:T(4,128)} %refs_1_.3) | copy-start | bytes 2949124
  2.1 1.0 copy-start.3
  13.6 4.9 %collective-permute-start = (f32[40,128]{1,0:T(8,128)S(1)}, f32[40,128]{1,0:T(8,128)S(1)}, u32[]{:S(2)}, u32[]{:S(2)}) collective-permute-start(f32[40,128]{1,0:T(8,128)S(1)} %get-tuple-element.49.xhi_ref), channel_id=1, source_target_pairs={{0,64},{64,128},{128,192},{192,0},{1,65},{65,129},{129,193},{193,1... | collective-permute-start | bytes 61448 | tf_op jit(solution)/shard_map/ppermute | solution.py:614
  15.7 2.8 %collective-permute-start.1 = (f32[40,128]{1,0:T(8,128)S(1)}, f32[40,128]{1,0:T(8,128)S(1)}, u32[]{:S(2)}, u32[]{:S(2)}) collective-permute-start(f32[40,128]{1,0:T(8,128)S(1)} %get-tuple-element.48.xlo_ref), channel_id=1, source_target_pairs={{64,0},{128,64},{192,128},{0,192},{65,1},{129,65},{193,129},{1,193... | collective-permute-start | bytes 61448 | tf_op jit(solution)/shard_map/ppermute | solution.py:614
  18.6 5.7 %collective-permute-start.2 = (f32[40,128]{1,0:T(8,128)S(1)}, f32[40,128]{1,0:T(8,128)S(1)}, u32[]{:S(2)}, u32[]{:S(2)}) collective-permute-start(f32[40,128]{1,0:T(8,128)S(1)} %get-tuple-element.55.yhi_ref), channel_id=1, source_target_pairs={{0,8},{8,16},{16,24},{24,32},{32,40},{40,48},{48,56},{56,0},{1,9},... | collective-permute-start | bytes 61448 | tf_op jit(solution)/shard_map/ppermute | solution.py:614
  23.5 4.2 %collective-permute-start.3 = (f32[40,128]{1,0:T(8,128)S(1)}, f32[40,128]{1,0:T(8,128)S(1)}, u32[]{:S(2)}, u32[]{:S(2)}) collective-permute-start(f32[40,128]{1,0:T(8,128)S(1)} %get-tuple-element.54.ylo_ref), channel_id=1, source_target_pairs={{8,0},{16,8},{24,16},{32,24},{40,32},{48,40},{56,48},{0,56},{9,1},... | collective-permute-start | bytes 61448 | tf_op jit(solution)/shard_map/ppermute | solution.py:614
  27.8 6.5 %collective-permute-start.4 = (f32[160,128]{1,0:T(8,128)S(1)}, f32[160,128]{1,0:T(8,128)S(1)}, u32[]{:S(2)}, u32[]{:S(2)}) collective-permute-start(f32[160,128]{1,0:T(8,128)S(1)} %get-tuple-element.70.refs_7_.zhi_ref), channel_id=1, source_target_pairs={{0,1},{1,2},{2,3},{3,4},{4,5},{5,6},{6,7},{7,0},{8,9},{9,10},{10,1... | collective-permute-start | bytes 245768 | tf_op jit(solution)/shard_map/ppermute | solution.py:614
  29.2 5.2 %collective-permute-start.5 = (f32[160,128]{1,0:T(8,128)S(1)}, f32[160,128]{1,0:T(8,128)S(1)}, u32[]{:S(2)}, u32[]{:S(2)}) collective-permute-start(f32[160,128]{1,0:T(8,128)S(1)} %get-tuple-element.69.refs_6_.zlo_ref), channel_id=1, source_target_pairs={{1,0},{2,1},{3,2},{4,3},{5,4},{6,5},{7,6},{0,7},{9,8},{10,9},{11,1... | collective-permute-start | bytes 245768 | tf_op jit(solution)/shard_map/ppermute | solution.py:614
  38.7 17.1 %all-to-all-start = ((f32[8,192,128]{2,1,0:T(8,128)}), f32[8,192,128]{2,1,0:T(8,128)S(1)}, u32[]{:S(2)}, u32[]{:S(2)}) async-start(f32[8,192,128]{2,1,0:T(8,128)} %cells.1), calls=%async_computation | async-start | bytes 1572864 | tf_op jit(solution)/shard_map/all_to_all | solution.py:709
  44.1 1.1 copy-start.4
  45.2 10.6 %copy-start.7 = (bf16[4,64,128]{2,1,0:T(8,128)(2,1)S(1)}, bf16[4,64,128]{2,1,0:T(8,128)(2,1)}, u32[]{:S(2)}) copy-start(bf16[4,64,128]{2,1,0:T(8,128)(2,1)} %constant.46.clone.fh_ref) | copy-start | bytes 196612
  45.2 10.6 %copy-start.8 = (bf16[4,64,128]{2,1,0:T(8,128)(2,1)S(1)}, bf16[4,64,128]{2,1,0:T(8,128)(2,1)}, u32[]{:S(2)}) copy-start(bf16[4,64,128]{2,1,0:T(8,128)(2,1)} %constant.47.clone.fl_ref) | copy-start | bytes 196612
  53.1 1.2 %copy-start.10 = (f32[24,136,128]{2,1,0:T(8,128)}, f32[24,136,128]{2,1,0:T(8,128)S(1)}, u32[]{:S(2)}) copy-start(f32[24,136,128]{2,1,0:T(8,128)S(1)} %views.1.refs_3_) | copy-start | bytes 5013508
  57.6 19.3 %all-to-all-start.1 = ((f32[16,48,128]{2,1,0:T(8,128)}), f32[16,48,128]{2,1,0:T(8,128)S(1)}, u32[]{:S(2)}, u32[]{:S(2)}) async-start(f32[16,48,128]{2,1,0:T(8,128)} %bitcast.5), calls=%async_computation.1 | async-start | bytes 786432 | tf_op jit(solution)/shard_map/all_to_all | solution.py:720
  64.0 1.4 %copy-start.11 = (f32[24,136,128]{2,1,0:T(8,128)S(1)}, f32[24,136,128]{2,1,0:T(8,128)}, u32[]{:S(2)}) copy-start(f32[24,136,128]{2,1,0:T(8,128)} %copy-done.10) | copy-start | bytes 5013508
  65.5 11.5 %copy-start.5 = (bf16[512,256]{1,0:T(8,128)(2,1)S(1)}, bf16[512,256]{1,0:T(8,128)(2,1)}, u32[]{:S(2)}) copy-start(bf16[512,256]{1,0:T(8,128)(2,1)} %constant.48.clone.fh_ref) | copy-start | bytes 786436
  65.5 11.5 %copy-start.6 = (bf16[512,256]{1,0:T(8,128)(2,1)S(1)}, bf16[512,256]{1,0:T(8,128)(2,1)}, u32[]{:S(2)}) copy-start(bf16[512,256]{1,0:T(8,128)(2,1)} %constant.49.clone.fl_ref) | copy-start | bytes 786436
  70.7 19.3 %copy-start.1 = (bf16[512,512]{1,0:T(8,128)(2,1)S(1)}, bf16[512,512]{1,0:T(8,128)(2,1)}, u32[]{:S(2)}) copy-start(bf16[512,512]{1,0:T(8,128)(2,1)} %constant.50.clone.fh_ref) | copy-start | bytes 1572868
  70.7 19.3 %copy-start.2 = (bf16[512,512]{1,0:T(8,128)(2,1)S(1)}, bf16[512,512]{1,0:T(8,128)(2,1)}, u32[]{:S(2)}) copy-start(bf16[512,512]{1,0:T(8,128)(2,1)} %constant.51.clone.fl_ref) | copy-start | bytes 1572868
  78.3 30.9 %copy-start.12 = (f32[1,64]{1,0:T(1,128)S(1)}, f32[1,64]{1,0:T(1,128)}, u32[]{:S(2)}) copy-start(f32[1,64]{1,0:T(1,128)} %constant.54) | copy-start | bytes 772
  92.2 16.9 %all-to-all-start.3 = ((f32[64,1,128]{2,1,0:T(1,128)}), f32[64,1,128]{2,1,0:T(1,128)S(1)}, u32[]{:S(2)}, u32[]{:S(2)}) async-start(f32[64,1,128]{2,1,0:T(1,128)} %bitcast.8), calls=%async_computation.3 | async-start | bytes 65536 | tf_op jit(solution)/shard_map/all_to_all | solution.py:744
  99.9 9.8 %collective-permute-start.6 = (f32[192,128]{1,0:T(8,128)S(1)}, f32[192,128]{1,0:T(8,128)S(1)}, u32[]{:S(2)}, u32[]{:S(2)}) collective-permute-start(f32[192,128]{1,0:T(8,128)S(1)} %get-tuple-element.83), channel_id=1, source_target_pairs={{0,64},{64,128},{128,192},{192,0},{1,65},{65,129},{129,193},{193,1... | collective-permute-start | bytes 294920 | tf_op jit(solution)/shard_map/ppermute | solution.py:746
  100.3 9.4 %collective-permute-start.7 = (f32[192,128]{1,0:T(8,128)S(1)}, f32[192,128]{1,0:T(8,128)S(1)}, u32[]{:S(2)}, u32[]{:S(2)}) collective-permute-start(f32[192,128]{1,0:T(8,128)S(1)} %get-tuple-element.84), channel_id=1, source_target_pairs={{0,128},{64,192},{128,0},{192,64},{1,129},{65,193},{129,1},{193,65... | collective-permute-start | bytes 294920 | tf_op jit(solution)/shard_map/ppermute | solution.py:746
  102.1 7.6 %collective-permute-start.8 = (f32[192,128]{1,0:T(8,128)S(1)}, f32[192,128]{1,0:T(8,128)S(1)}, u32[]{:S(2)}, u32[]{:S(2)}) collective-permute-start(f32[192,128]{1,0:T(8,128)S(1)} %get-tuple-element.85), channel_id=1, source_target_pairs={{0,192},{64,0},{128,64},{192,128},{1,193},{65,1},{129,65},{193,129... | collective-permute-start | bytes 294920 | tf_op jit(solution)/shard_map/ppermute | solution.py:746
